TPU v7x, 32 devices: a whole 2x2x4 slice. The times are simulated.
32 devices in a mesh: tm: 4 (over y, x), users: 8 (over z, core).
Axes of the slice: x: 2, y: 2, z: 4, core: 2. Of those that a mesh axis runs over, the one named last changes fastest.
Arguments:
- features: float32 [131072, 128], P(('tm', 'users')), may hold values from -6 to 6
- home: int32 [131072, 1], P(('tm', 'users')), may hold values from 0 to 7; in each aligned block of 4096 rows (0 to 4095, 4096 to 8191, ...) at most 1024 rows name the same one
- account: int32 [131072], P(('tm', 'users')), may hold values from 0 to 127
- flags: int32 [131072], P(('tm', 'users')), may hold values 0 or 1
Outputs:
- session_mean: float32 [131072, 128], P(('tm', 'users'))
Inputs may be any that keep to these rules, and one draw needn't show every extreme that they name: `home`: the 4096 events of one device name one owner at most 1024 times, a bound that some block reaches.
All inputs are finite; a program needn't handle non-finite values. No bound on the sum of `flags` on one device may be relied on, other than what follows from the above.
Results may differ from a plain program's by a relative error of at most 0.00007.
Values sent between devices are 32-bit elements; how exact they have to be, the bound alone decides.
No kernel may reach another device: no remote copies, remote signals or barrier semaphores. Data moves between devices by JAX's collectives and lax.ppermute only.
A program may use at most 64 MiB of HBM per device.

v0:
```python
import math

import jax
import jax.numpy as jnp
from jax import lax
from jax.sharding import PartitionSpec as P

ACCOUNTS = 128


EXACT_MATMUL = lax.Precision.HIGHEST


def destination_rank(owner_of, owners):
    count_per_row = owner_of.shape[0]
    block_rows = math.gcd(count_per_row, 512)
    blocks = count_per_row // block_rows
    strict_lower = (
        lax.broadcasted_iota(jnp.int32, (block_rows, block_rows), 0)
        > lax.broadcasted_iota(jnp.int32, (block_rows, block_rows), 1)
    ).astype(jnp.float32)
    columns = jnp.arange(owners, dtype=jnp.int32)

    def destination_advance(before, block_data):
        choose_mask = (block_data[:, None] == columns[None, :]).astype(jnp.float32)
        earlier = jnp.dot(strict_lower, choose_mask, precision=EXACT_MATMUL) + before[None, :]
        return (before + jnp.sum(choose_mask, axis=0), jnp.sum(earlier * choose_mask, axis=1))

    ignored, rank_rows = lax.scan(
        destination_advance, jnp.zeros((owners,), jnp.float32), owner_of.reshape(blocks, block_rows)
    )
    return rank_rows.reshape(count_per_row).astype(jnp.int32)


def decode_rows(code_rows):
    code_ints = code_rows.astype(jnp.int32)
    is_valid = code_ints >= 0
    account_rows = jnp.where(is_valid, code_ints // 2, -1)
    flag_rows = jnp.where(is_valid, code_ints % 2, 0).astype(jnp.float32)
    return (account_rows, flag_rows)


def session_sweep(values, account_rows, flag_rows, accounts):
    count_per_row, feature_count = values.shape
    block_rows = math.gcd(count_per_row, 512)
    blocks = count_per_row // block_rows
    row_ids = lax.broadcasted_iota(jnp.int32, (block_rows, block_rows), 0)
    col_ids = lax.broadcasted_iota(jnp.int32, (block_rows, block_rows), 1)
    up_to = col_ids <= row_ids
    later_rows = col_ids > row_ids
    up_to_float = up_to.astype(jnp.float32)
    columns = jnp.arange(accounts, dtype=jnp.int32)

    def session_advance(carried, block_data):
        open_sum, open_count, already_seen = carried
        rows_values, rows_account, rows_flag = block_data
        is_live = rows_account >= 0
        indicator_matrix = (rows_account[:, None] == columns[None, :]).astype(jnp.float32)
        flag_counts = jnp.dot(
            up_to_float, indicator_matrix * rows_flag[:, None], precision=EXACT_MATMUL
        )
        own_flags = jnp.sum(flag_counts * indicator_matrix, axis=1)
        same_user = (
            (rows_account[:, None] == rows_account[None, :]) & is_live[None, :] & is_live[:, None]
        )
        same_session = (same_user & up_to & (own_flags[:, None] == own_flags[None, :])).astype(
            jnp.float32
        )
        inside_sum = jnp.dot(same_session, rows_values, precision=EXACT_MATMUL)
        inside_count = jnp.sum(same_session, axis=1)
        session_continues = jnp.where(is_live & (own_flags == 0.0), 1.0, 0.0)
        running_sum = inside_sum + session_continues[:, None] * jnp.dot(
            indicator_matrix, open_sum, precision=EXACT_MATMUL
        )
        running_count = inside_count + session_continues * jnp.dot(
            indicator_matrix, open_count, precision=EXACT_MATMUL
        )
        without_flag = session_continues * (
            1.0 - jnp.dot(indicator_matrix, already_seen, precision=EXACT_MATMUL)
        )
        followers = jnp.sum((same_user & later_rows).astype(jnp.float32), axis=1)
        last_weight = jnp.where(is_live & (followers == 0.0), 1.0, 0.0)
        present = jnp.minimum(jnp.sum(indicator_matrix, axis=0), 1.0)
        updated_sum = (
            jnp.einsum(
                "ra,rf->af",
                indicator_matrix,
                last_weight[:, None] * running_sum,
                precision=EXACT_MATMUL,
            )
            + (1.0 - present)[:, None] * open_sum
        )
        updated_count = (
            jnp.dot(last_weight * running_count, indicator_matrix, precision=EXACT_MATMUL)
            + (1.0 - present) * open_count
        )
        any_flag = jnp.minimum(jnp.sum(indicator_matrix * rows_flag[:, None], axis=0), 1.0)
        updated_seen = jnp.maximum(already_seen, any_flag)
        return (
            (updated_sum, updated_count, updated_seen),
            (running_sum, running_count, without_flag),
        )

    start_state = (
        jnp.zeros((accounts, feature_count), jnp.float32),
        jnp.zeros((accounts,), jnp.float32),
        jnp.zeros((accounts,), jnp.float32),
    )
    block_data = (
        values.reshape(blocks, block_rows, feature_count),
        account_rows.reshape(blocks, block_rows),
        flag_rows.reshape(blocks, block_rows),
    )
    closing_state, row_pieces = lax.scan(session_advance, start_state, block_data)
    running_sum = row_pieces[0].reshape(count_per_row, feature_count)
    running_count = row_pieces[1].reshape(count_per_row)
    without_flag = row_pieces[2].reshape(count_per_row)
    return (closing_state, running_sum, running_count, without_flag)


def combine_states(earlier, later):
    carry_on = 1.0 - later[2]
    return (
        later[0] + carry_on[:, None] * earlier[0],
        later[1] + carry_on * earlier[1],
        jnp.maximum(earlier[2], later[2]),
    )


def body(features, home, account, flags):
    owners = lax.axis_size("users")
    event_rows, feature_count = features.shape
    slot_cap = 2 * event_rows // owners
    accounts = ACCOUNTS
    owner_of = home[:, 0]
    rank_rows = destination_rank(owner_of, owners)
    slot_index = owner_of * slot_cap + rank_rows
    code_values = (account * 2 + flags).astype(jnp.float32)
    send_values = (
        jnp.zeros((owners * slot_cap, feature_count), jnp.float32).at[slot_index].set(features)
    )
    send_codes = jnp.full((owners * slot_cap,), -1.0, jnp.float32).at[slot_index].set(code_values)
    got_values, got_codes = (
        lax.all_to_all(
            send_values.reshape(owners, slot_cap, feature_count),
            "users",
            split_axis=0,
            concat_axis=0,
            tiled=True,
        ),
        lax.all_to_all(
            send_codes.reshape(owners, slot_cap), "users", split_axis=0, concat_axis=0, tiled=True
        ),
    )
    account_rows, flag_rows = decode_rows(got_codes.reshape(owners * slot_cap))
    closing_state, running_sum, running_count, without_flag = session_sweep(
        got_values.reshape(owners * slot_cap, feature_count), account_rows, flag_rows, accounts
    )
    identity = (
        jnp.zeros((accounts, feature_count), jnp.float32),
        jnp.zeros((accounts,), jnp.float32),
        jnp.zeros((accounts,), jnp.float32),
    )
    gathered = (
        lax.all_gather(closing_state[0], "tm", axis=0, tiled=True),
        lax.all_gather(closing_state[1], "tm", axis=0, tiled=True),
        lax.all_gather(closing_state[2], "tm", axis=0, tiled=True),
    )
    my_group = lax.axis_index("tm")
    incoming = identity
    for position in range(lax.axis_size("tm")):
        group_state = (
            gathered[0][position * accounts : (position + 1) * accounts],
            gathered[1][position * accounts : (position + 1) * accounts],
            gathered[2][position * accounts : (position + 1) * accounts],
        )
        merged = combine_states(incoming, group_state)
        incoming = (
            jnp.where(position < my_group, merged[0], incoming[0]),
            jnp.where(position < my_group, merged[1], incoming[1]),
            jnp.where(position < my_group, merged[2], incoming[2]),
        )
    columns = jnp.arange(accounts, dtype=jnp.int32)
    onehot_rows = (account_rows[:, None] == columns[None, :]).astype(jnp.float32)
    overall_sum = running_sum + without_flag[:, None] * jnp.dot(
        onehot_rows, incoming[0], precision=EXACT_MATMUL
    )
    overall_count = running_count + without_flag * jnp.dot(
        onehot_rows, incoming[1], precision=EXACT_MATMUL
    )
    session_means = overall_sum / jnp.where(overall_count > 0.0, overall_count, 1.0)[:, None]
    returned_means = lax.all_to_all(
        session_means.reshape(owners, slot_cap, feature_count),
        "users",
        split_axis=0,
        concat_axis=0,
        tiled=True,
    )
    result = returned_means.reshape(owners * slot_cap, feature_count)[slot_index]
    return result


def solution(mesh):
    return jax.shard_map(
        body,
        mesh=mesh,
        in_specs=(
            P(("tm", "users"), None),
            P(("tm", "users"), None),
            P(("tm", "users")),
            P(("tm", "users")),
        ),
        out_specs=P(("tm", "users"), None),
        check_vma=False,
    )
```

profile of v0, /device:TPU:0, one launch (start us, length us, event | category | flops | bytes accessed | tf_op | source)
XLA Modules:
  0.0 385.4 jit_solution(16359685620664613377)
XLA Ops:
  0.6 1.4 reduce.7
  2.1 5.3 %while.34 = (s32[]{:T(128)}, f32[8]{0:T(128)S(1)}, f32[8,512]{1,0:T(8,128)S(1)}, s32[8,512]{1,0:T(8,128)S(1)}, s32[]{:T(128)}, /*index=5*/s32[]{:T(128)}) while((s32[]{:T(128)}, f32[8]{0:T(128)S(1)}, f32[8,512]{1,0:T(8,128)S(1)}, s32[8,512]{1,0:T(8,128)S(1)}, s32[]{:T(128)}, /*index=5*/s32[]{:T(128)}) %tuple.69), condition=%wide.region_3.4_spmd.clone, body=%wide.region_0.3_spmd.clone.sunk | while | flops 25722380 | bytes 14623 | solution.py:29
  8.9 16.1 %scatter_custom_fusion = f32[8192]{0:T(1024)} fusion(s32[4096]{0:T(1024)S(1)} %bitcast.173, f32[4096]{0:T(1024)S(1)} %add_convert_fusion, f32[]{:T(128)} %constant.54.clone.1), kind=kCustom, calls=%fused_computation.134 | custom fusion | bytes 32772 | tf_op jit(solution)/shard_map/scatter | solution.py:142
  25.0 6.4 %all-to-all-start = ((f32[8,1,1024]{2,1,0:T(1,128)}), f32[8,1,1024]{2,1,0:T(1,128)S(1)}, u32[]{:S(2)}, u32[]{:S(2)}) async-start(f32[8,1,1024]{2,1,0:T(1,128)} %bitcast.1), calls=%async_computation | async-start | bytes 65536 | tf_op jit(solution)/shard_map/all_to_all | solution.py:151
  31.3 13.1 %scatter_custom_fusion.1 = f32[8192,128]{1,0:T(8,128)} fusion(s32[4096]{0:T(1024)S(1)} %bitcast.174, f32[4096,128]{1,0:T(8,128)} %param.8, f32[]{:T(128)} %constant.49.clone.1), kind=kCustom, calls=%fused_computation.88 | custom fusion | bytes 4194816 | tf_op jit(solution)/shard_map/scatter | solution.py:140
  44.4 5.1 %all-to-all-start.1 = ((f32[8,1024,128]{2,1,0:T(8,128)}), f32[8,1024,128]{2,1,0:T(8,128)}, u32[]{:S(2)}, u32[]{:S(2)}) async-start(f32[8,1024,128]{2,1,0:T(8,128)} %bitcast.151), calls=%async_computation.1 | async-start | bytes 8388608 | tf_op jit(solution)/shard_map/all_to_all | solution.py:144
  49.8 93.8 %all-to-all-done.1 = f32[8,1024,128]{2,1,0:T(8,128)} async-done(((f32[8,1024,128]{2,1,0:T(8,128)}), f32[8,1024,128]{2,1,0:T(8,128)}, u32[]{:S(2)}, u32[]{:S(2)}) %all-to-all-start.1) | async-done | bytes 4194336 | tf_op jit(solution)/shard_map/all_to_all | solution.py:144
  143.6 90.4 %while.35 = (s32[]{:T(128)}, f32[128,128]{1,0:T(8,128)S(1)}, f32[128]{0:T(128)S(1)}, f32[128]{0:T(128)S(1)}, f32[16,512,128]{2,1,0:T(8,128)}, /*index=5*/f32[16,...) while((s32[]{:T(128)}, f32[128,128]{1,0:T(8,128)S(1)}, ...), condition=%wide.region_12.13_spmd.clone, body=%wide.region_6.12_spmd.clone.sunk | while | flops 1016011008 | bytes 1867940 | solution.py:114
  143.8 0.9 fusion.148
  146.0 1.7 fusion.150
  147.7 1.1 bitcast_dynamic-update-slice_fusion.2
  149.4 0.9 fusion.148
  151.6 1.7 fusion.150
  153.3 1.1 bitcast_dynamic-update-slice_fusion.2
  155.1 0.9 fusion.148
  157.3 1.7 fusion.150
  159.0 1.1 bitcast_dynamic-update-slice_fusion.2
  160.7 0.9 fusion.148
  162.9 1.7 fusion.150
  164.6 1.1 bitcast_dynamic-update-slice_fusion.2
  166.4 0.9 fusion.148
  168.6 1.7 fusion.150
  170.3 1.1 bitcast_dynamic-update-slice_fusion.2
  172.0 0.9 fusion.148
  174.2 1.7 fusion.150
  176.0 1.1 bitcast_dynamic-update-slice_fusion.2
  177.7 0.9 fusion.148
  179.9 1.7 fusion.150
  181.6 1.1 bitcast_dynamic-update-slice_fusion.2
  183.3 0.9 fusion.148
  185.6 1.7 fusion.150
  187.3 1.1 bitcast_dynamic-update-slice_fusion.2
  189.0 0.9 fusion.148
  191.2 1.7 fusion.150
  192.9 1.1 bitcast_dynamic-update-slice_fusion.2
  194.6 0.9 fusion.148
  196.9 1.7 fusion.150
  198.6 1.1 bitcast_dynamic-update-slice_fusion.2
  200.3 0.9 fusion.148
  202.5 1.7 fusion.150
  204.2 1.1 bitcast_dynamic-update-slice_fusion.2
  205.9 0.9 fusion.148
  208.2 1.7 fusion.150
  209.9 1.1 bitcast_dynamic-update-slice_fusion.2
  211.6 0.9 fusion.148
  213.8 1.7 fusion.150
  215.5 1.1 bitcast_dynamic-update-slice_fusion.2
  217.2 0.9 fusion.148
  219.5 1.7 fusion.150
  221.2 1.1 bitcast_dynamic-update-slice_fusion.2
  222.9 0.9 fusion.148
  225.1 1.7 fusion.150
  226.8 1.1 bitcast_dynamic-update-slice_fusion.2
  228.5 0.9 fusion.148
  230.8 1.7 fusion.150
  232.5 1.1 bitcast_dynamic-update-slice_fusion.2
  234.0 8.0 %all-gather = f32[4,1,128]{2,1,0:T(1,128)S(1)} all-gather(f32[1,1,128]{2,1,0:T(1,128)S(1)} %bitcast.184), channel_id=1, replica_groups=mesh['tm'=4,'users'=8] {'tm'}, dimensions={0}, use_global_device_ids=true | all-gather | bytes 2560 | tf_op jit(solution)/shard_map/all_gather | solution.py:167
  242.0 7.9 %all-gather.1 = f32[4,1,128]{2,1,0:T(1,128)S(1)} all-gather(f32[1,1,128]{2,1,0:T(1,128)S(1)} %bitcast.185), channel_id=1, replica_groups=mesh['tm'=4,'users'=8] {'tm'}, dimensions={0}, use_global_device_ids=true | all-gather | bytes 2560 | tf_op jit(solution)/shard_map/all_gather | solution.py:166
  249.9 8.0 %all_gather.9 = f32[512,128]{1,0:T(8,128)S(1)} all-gather(f32[128,128]{1,0:T(8,128)S(1)} %get-tuple-element.117), channel_id=1, replica_groups=mesh['tm'=4,'users'=8] {'tm'}, dimensions={0}, use_global_device_ids=true | all-gather | bytes 327680 | tf_op jit(solution)/shard_map/all_gather | solution.py:165
  257.9 2.9 fusion.58
  260.9 9.6 %fusion.57 = f32[8192,128]{1,0:T(8,128)} fusion(f32[8192,128]{1,0:T(8,128)} %bitcast.186, f32[8192]{0:T(1024)S(1)} %compare_select_fusion.1, s32[8192]{0:T(1024)S(1)} %fusion.78, f32[8192]{0:T(1024)S(1)} %bitcast.171, f32[512,128]{1,0:T(8,128)S(1)} %all_gather.9, f32[128]{0:T(128)S(1)} %get-tuple-element.232, f32[128]{0:T(128)S(1)} %get-tuple-element.230, ...), kind=kOutput, calls=%fused_computation.83 | convolution fusion | flops 1614987264 | bytes 8751108 | tf_op jit(solution)/shard_map/dot_general | solution.py:185
  270.5 4.5 %all-to-all-start.2 = ((f32[8,1024,128]{2,1,0:T(8,128)}), f32[8,1024,128]{2,1,0:T(8,128)}, u32[]{:S(2)}, u32[]{:S(2)}) async-start(f32[8,1024,128]{2,1,0:T(8,128)} %bitcast.152), calls=%async_computation.2 | async-start | bytes 8388608 | tf_op jit(solution)/shard_map/all_to_all | solution.py:192
  275.1 94.0 %all-to-all-done.2 = f32[8,1024,128]{2,1,0:T(8,128)} async-done(((f32[8,1024,128]{2,1,0:T(8,128)}), f32[8,1024,128]{2,1,0:T(8,128)}, u32[]{:S(2)}, u32[]{:S(2)}) %all-to-all-start.2) | async-done | bytes 4194336 | tf_op jit(solution)/shard_map/all_to_all | solution.py:192
  369.0 16.4 %gather_fusion = f32[4096,128]{1,0:T(8,128)} fusion(f32[8192,128]{1,0:T(8,128)} %bitcast.19, s32[4096]{0:T(1024)S(1)} %broadcast_clamp_fusion), kind=kCustom, calls=%fused_computation | custom fusion | bytes 4210688 | tf_op jit(solution)/shard_map/gather | solution.py:199
  (273 shorter events, 37.3 us)
Async XLA Ops:
  25.0 19.5 %all-to-all-start = ((f32[8,1,1024]{2,1,0:T(1,128)}), f32[8,1,1024]{2,1,0:T(1,128)S(1)}, u32[]{:S(2)}, u32[]{:S(2)}) async-start(f32[8,1,1024]{2,1,0:T(1,128)} %bitcast.1), calls=%async_computation | async-start | bytes 65536 | tf_op jit(solution)/shard_map/all_to_all | solution.py:151
  44.4 99.2 %all-to-all-start.1 = ((f32[8,1024,128]{2,1,0:T(8,128)}), f32[8,1024,128]{2,1,0:T(8,128)}, u32[]{:S(2)}, u32[]{:S(2)}) async-start(f32[8,1024,128]{2,1,0:T(8,128)} %bitcast.151), calls=%async_computation.1 | async-start | bytes 8388608 | tf_op jit(solution)/shard_map/all_to_all | solution.py:144
  270.5 98.5 %all-to-all-start.2 = ((f32[8,1024,128]{2,1,0:T(8,128)}), f32[8,1024,128]{2,1,0:T(8,128)}, u32[]{:S(2)}, u32[]{:S(2)}) async-start(f32[8,1024,128]{2,1,0:T(8,128)} %bitcast.152), calls=%async_computation.2 | async-start | bytes 8388608 | tf_op jit(solution)/shard_map/all_to_all | solution.py:192
where the time goes:
time: 387 us; the launch traced here: 385 us
  waiting for transfers between devices  188 us (49%)
  matrix products  90.2 us (23%)
  local copies, waits for them, and re-layouts  49.7 us (13%)
  blocking collectives  23.9 us (6%)
  other arithmetic  16.1 us (4%)
  starting transfers between devices  16 us (4%)
    all_to_all x1, waiting for transfers between devices, body(): lax.all_to_all(session_means.reshape(owners, slot_cap, feature_count), 'u...  94 us
    all_to_all x1, waiting for transfers between devices, body(): lax.all_to_all(send_values.reshape(owners, slot_cap, feature_count), 'use...  93.8 us
    dot_general x16, matrix products, session_advance(): inside_sum = jnp.dot(same_session, rows_values, precision=EXACT_MATMUL)  27.3 us
    dot_general x16, matrix products, session_advance(): jnp.dot(indicator_matrix, open_sum, precision=EXACT_MATMUL)  17.8 us
    gather x1, local copies, waits for them, and re-layouts, body(): returned_means.reshape(owners * slot_cap, feature_count)[slot_index]  16.4 us
    scatter x1, local copies, waits for them, and re-layouts, body(): jnp.full((owners * slot_cap,), -1.0, jnp.float32).at[slot_index]  16.1 us
    dot_general x16, matrix products, session_advance(): jnp.dot(up_to_float, indicator_matrix * rows_flag[:, None], precision=EXA...  14.1 us
    scatter x1, local copies, waits for them, and re-layouts, body(): jnp.zeros((owners * slot_cap, feature_count), jnp.float32).at[slot_index]  13.1 us
  transfers between devices with their start and end apart: 3, of which 2 were waited for; matrix products, arithmetic and copies ran while one was open for 3% of the time, Pallas kernels for 0%

commit v1 on v0

v1 whole, which is shorter than its diff:
```python
import functools

import jax
import jax.numpy as jnp
from jax import lax
from jax.experimental import pallas as pl
from jax.experimental.pallas import tpu as pltpu
from jax.sharding import PartitionSpec as P

ACCOUNTS = 128
LANES = 128
EXTRA = 8
HALVINGS = 2
AXES = ("tm", "users")
F32, BF16, I32 = jnp.float32, jnp.bfloat16, jnp.int32


def split_two(x):
    high = x.astype(BF16)
    return high, (x - high.astype(F32)).astype(BF16)


def sublane_ids():
    return lax.broadcasted_iota(I32, (ACCOUNTS, LANES), 0).astype(F32)


def row_positions(tiles):
    shape = (tiles, LANES)
    return lax.broadcasted_iota(I32, shape, 0) * LANES + lax.broadcasted_iota(I32, shape, 1)


def one_hot_tile(key_row, ids):
    return key_row == ids


def last_flag_row(kept, ids):
    tiles = kept.shape[0]
    latest = jnp.full((ACCOUNTS, LANES), -1.0, F32)
    for tile in range(tiles):
        latest = jnp.where(kept[tile : tile + 1] == ids, float(tile), latest)
    lane = lax.broadcasted_iota(I32, (ACCOUNTS, LANES), 1).astype(F32)
    place = jnp.where(latest >= 0.0, latest * LANES + lane, -1.0)
    return jnp.max(place.T, axis=0, keepdims=True)


def closing_kernel(flip_ref, home_ref, account_ref, flag_ref, x_ref, out_ref, parts_ref, last_ref):
    tiles = home_ref.shape[0]
    owners, rows = out_ref.shape[0], out_ref.shape[1]
    features = x_ref.shape[1]
    events = x_ref.shape[0]
    chunk = min(512, events)
    per_chunk = chunk // LANES
    group = 2 if owners % 2 == 0 else 1
    flip = flip_ref[0]
    ids = sublane_ids()
    home = home_ref[...]
    account = account_ref[...]
    flag = flag_ref[...]
    account_f = account.astype(F32)

    high, low = split_two(x_ref[...])
    parts_ref[:, 0:features] = high
    parts_ref[:, features : 2 * features] = low

    def find_last(owner, carry):
        kept = jnp.where((home == owner) & (flag == 1), account_f, -1.0)
        last_ref[pl.ds(owner, 1), :] = last_flag_row(kept, ids)
        return carry

    lax.fori_loop(0, owners, find_last, 0, unroll=min(owners, 4))

    def look_up(owner, least):
        row = jnp.broadcast_to(last_ref[pl.ds(owner, 1), :], (tiles, LANES))
        found = jnp.take_along_axis(row, account, axis=1)
        return jnp.where(home == owner, found, least)

    least = lax.fori_loop(
        0, owners, look_up, jnp.full((tiles, LANES), -1.0, F32), unroll=min(owners, 8)
    )
    live = row_positions(tiles).astype(F32) >= least
    weight = jnp.where(flag == 1, 8193.0, 1.0)

    def one_group(number, carry):
        kept = [
            jnp.where(live & (home == number * group + i), account_f, -1.0) for i in range(group)
        ]
        total = jnp.zeros((group * ACCOUNTS, 2 * features), F32)
        counts = [jnp.zeros((ACCOUNTS, LANES), F32) for i in range(group)]
        for first in range(0, events, chunk):
            blocks = []
            for i in range(group):
                pieces = []
                for tile in range(first // LANES, first // LANES + per_chunk):
                    mask = kept[i][tile : tile + 1] == ids
                    counts[i] = counts[i] + jnp.where(mask, weight[tile : tile + 1], 0.0)
                    pieces.append(jnp.where(mask, 1.0, 0.0).astype(BF16))
                blocks.append(jnp.concatenate(pieces, axis=1))
            total = total + jnp.dot(
                jnp.concatenate(blocks, axis=0),
                parts_ref[first : first + chunk, :],
                preferred_element_type=F32,
            )
        sums = total[:, 0:features] + total[:, features : 2 * features]
        for i in range(group):
            place = jnp.bitwise_xor(number * group + i, flip)
            mine = sums[i * ACCOUNTS : (i + 1) * ACCOUNTS]
            out_ref[place, 0:features, :] = mine.T
            tally = jnp.sum(counts[i].T, axis=0, keepdims=True)
            marked = jnp.where(tally >= 8192.0, 1.0, 0.0)
            spot = lax.broadcasted_iota(I32, (rows - features, LANES), 0)
            out_ref[place, features:rows, :] = jnp.where(
                spot == 0, tally - 8192.0 * marked, jnp.where(spot == 1, marked, 0.0)
            )
        return carry

    lax.fori_loop(0, owners // group, one_group, 0)


def local_kernel(
    home_ref, account_ref, flag_ref, x_ref, out_ref, key_ref, parts_ref, column_ref, start_ref, sid_ref
):
    tiles = home_ref.shape[0]
    events, features = x_ref.shape
    rows = parts_ref.shape[0]
    chunk = min(512, events)
    per_chunk = chunk // LANES
    home = home_ref[...]
    account = account_ref[...]
    flag = flag_ref[...]
    user = home * ACCOUNTS + account
    user_f = user.astype(F32)
    sid_ref[...] = user_f
    flagged = jnp.where(flag == 1, user_f, -1.0)
    row_id = lax.broadcasted_iota(I32, (LANES, LANES), 0)
    column_id = lax.broadcasted_iota(I32, (LANES, LANES), 1)
    reaches = row_id <= column_id
    spot = row_id.astype(F32)

    for tile in range(tiles):
        span = slice(tile * LANES, (tile + 1) * LANES)
        turned = x_ref[span, :].T
        high, low = split_two(turned)
        parts_ref[0:features, span] = high
        parts_ref[features : 2 * features, span] = low
        column_ref[span, :] = jnp.broadcast_to(flagged[tile : tile + 1], (LANES, LANES)).T
    extra = lax.broadcasted_iota(I32, (rows - 2 * features, events), 0)
    parts_ref[2 * features : rows, :] = jnp.where(extra == 0, 1.0, 0.0).astype(BF16)

    def find_start(tile, carry):
        mine = sid_ref[pl.ds(tile, 1), :]

        def earlier(other, latest):
            column = column_ref[pl.ds(other * LANES, LANES), :]
            place = spot + (other * LANES).astype(F32)
            return jnp.where(column == mine, place, latest)

        latest = lax.fori_loop(0, tile, earlier, jnp.full((LANES, LANES), -1.0, F32))
        column = column_ref[pl.ds(tile * LANES, LANES), :]
        place = spot + (tile * LANES).astype(F32)
        latest = jnp.where((column == mine) & reaches, place, latest)
        start_ref[pl.ds(tile, 1), :] = jnp.max(latest, axis=0, keepdims=True)
        return carry

    lax.fori_loop(0, tiles, find_start, 0)
    start = start_ref[...]
    key_ref[...] = jnp.where(start < 0.0, user, -1)
    sid = jnp.where(start < 0.0, user_f + float(events), start)
    sid_ref[...] = sid
    for tile in range(tiles):
        span = slice(tile * LANES, (tile + 1) * LANES)
        column_ref[span, :] = jnp.broadcast_to(sid[tile : tile + 1], (LANES, LANES)).T

    def mask_block(first_c, first_r, diagonal):
        pieces = []
        for a in range(per_chunk):
            column = column_ref[pl.ds(first_c + a * LANES, LANES), :]
            line = []
            for b in range(per_chunk):
                if diagonal and a > b:
                    line.append(jnp.zeros((LANES, LANES), BF16))
                    continue
                mine = sid_ref[pl.ds(first_r // LANES + b, 1), :]
                mask = column == mine
                if diagonal and a == b:
                    mask = mask & reaches
                line.append(jnp.where(mask, 1.0, 0.0).astype(BF16))
            pieces.append(jnp.concatenate(line, axis=1))
        return jnp.concatenate(pieces, axis=0)

    for number in range(events // chunk):
        first_r = number * chunk

        def before(other, total):
            first_c = pl.multiple_of(other * chunk, chunk)
            return total + jnp.dot(
                parts_ref[:, pl.ds(first_c, chunk)],
                mask_block(first_c, first_r, False),
                preferred_element_type=F32,
            )

        total = jnp.dot(
            parts_ref[:, first_r : first_r + chunk],
            mask_block(first_r, first_r, True),
            preferred_element_type=F32,
        )
        total = lax.fori_loop(0, number, before, total)
        out_ref[0:features, first_r : first_r + chunk] = (
            total[0:features] + total[features : 2 * features]
        )
        out_ref[features:, first_r : first_r + chunk] = total[2 * features : 2 * features + EXTRA]


def final_kernel(flip_ref, key_ref, local_ref, state_ref, out_ref, table_ref):
    owners = state_ref.shape[0]
    events, features = out_ref.shape
    rows = table_ref.shape[0]
    flip = flip_ref[0]
    group = min(8, owners)
    ids = sublane_ids()
    per_chunk = events // LANES

    @pl.when(pl.program_id(0) == 0)
    def fill():
        def one(owner, carry):
            place = jnp.bitwise_xor(owner, flip)
            high, low = split_two(state_ref[place, 0:features, :])
            span = pl.ds(pl.multiple_of(owner * ACCOUNTS, ACCOUNTS), ACCOUNTS)
            table_ref[0:features, span] = high
            table_ref[features : 2 * features, span] = low
            count = state_ref[place, features : features + 1, :].astype(I32)
            digit = lax.broadcasted_iota(I32, (rows - 2 * features, LANES), 0)
            extra = jnp.where(
                digit == 0,
                count // 65536,
                jnp.where(digit == 1, (count // 256) % 256, jnp.where(digit == 2, count % 256, 0)),
            )
            table_ref[2 * features : rows, span] = extra.astype(F32).astype(BF16)
            return carry

        lax.fori_loop(0, owners, one, 0)

    first = pl.program_id(0) * per_chunk
    key = key_ref[pl.ds(pl.multiple_of(first, per_chunk), per_chunk), :]

    def part(number, total):
        lines = []
        for i in range(group):
            offset = (number * group + i) * ACCOUNTS
            mine = (key - offset).astype(F32)
            pieces = [
                jnp.where(mine[tile : tile + 1] == ids, 1.0, 0.0).astype(BF16)
                for tile in range(per_chunk)
            ]
            lines.append(jnp.concatenate(pieces, axis=1))
        block = jnp.concatenate(lines, axis=0)
        span = pl.ds(pl.multiple_of(number * group * ACCOUNTS, LANES), group * ACCOUNTS)
        return total + jnp.dot(table_ref[:, span], block, preferred_element_type=F32)

    zero = jnp.zeros((rows, events), F32)
    if owners == group:
        total = part(0, zero)
    else:
        total = lax.fori_loop(0, owners // group, part, zero)
    more = total[2 * features : 2 * features + 3]
    count = local_ref[features : features + 1, :] + (
        more[0:1] * 65536.0 + more[1:2] * 256.0 + more[2:3]
    )
    sums = local_ref[0:features, :] + (total[0:features] + total[features : 2 * features])
    out_ref[...] = (sums / count).T


VMEM = pl.BlockSpec(memory_space=pltpu.VMEM)
SMEM = pl.BlockSpec(memory_space=pltpu.SMEM)
PARAMS = pltpu.CompilerParams(vmem_limit_bytes=48 * 1024 * 1024)


def closing_states(flip, home, account, flags, features, owners):
    events, width = features.shape
    return pl.pallas_call(
        closing_kernel,
        out_shape=jax.ShapeDtypeStruct((owners, width + EXTRA, LANES), F32),
        in_specs=[SMEM, VMEM, VMEM, VMEM, VMEM],
        out_specs=VMEM,
        scratch_shapes=[
            pltpu.VMEM((events, 2 * width), BF16),
            pltpu.VMEM((max(8, owners), LANES), F32),
        ],
        compiler_params=PARAMS,
        name="closing",
    )(flip, home, account, flags, features)


def local_sums(home, account, flags, features):
    events, width = features.shape
    tiles = home.shape[0]
    return pl.pallas_call(
        local_kernel,
        out_shape=(
            jax.ShapeDtypeStruct((width + EXTRA, events), F32),
            jax.ShapeDtypeStruct((tiles, LANES), I32),
        ),
        in_specs=[VMEM, VMEM, VMEM, VMEM],
        out_specs=(VMEM, VMEM),
        scratch_shapes=[
            pltpu.VMEM((2 * width + 16, events), BF16),
            pltpu.VMEM((events, LANES), F32),
            pltpu.VMEM((tiles, LANES), F32),
            pltpu.VMEM((tiles, LANES), F32),
        ],
        compiler_params=PARAMS,
        name="local",
    )(home, account, flags, features)


def final_means(flip, key, local, state, events, width):
    chunk = min(1024, events)
    owners = state.shape[0]
    return pl.pallas_call(
        final_kernel,
        out_shape=jax.ShapeDtypeStruct((events, width), F32),
        grid=(events // chunk,),
        in_specs=[
            SMEM,
            VMEM,
            pl.BlockSpec((width + EXTRA, chunk), lambda i: (0, i)),
            VMEM,
        ],
        out_specs=pl.BlockSpec((chunk, width), lambda i: (i, 0)),
        scratch_shapes=[pltpu.VMEM((2 * width + 16, owners * ACCOUNTS), BF16)],
        compiler_params=PARAMS,
        name="final",
    )(flip, key, local, state)


def combine(earlier, later, mark):
    return later + (1.0 - later[:, mark : mark + 1, :]) * earlier


def scan_states(state, me, devices, width):
    mark = width + 1
    steps = devices.bit_length() - 1
    halvings = min(HALVINGS, steps, state.shape[0].bit_length() - 1)

    def swap(value, step):
        return lax.ppermute(value, AXES, [(i, i ^ (1 << step)) for i in range(devices)])

    kept = []
    for step in range(halvings):
        half = state.shape[0] // 2
        got = swap(state[half:], step)
        mine = state[:half]
        upper = ((me >> step) & 1) == 1
        low, high = jnp.where(upper, got, mine), jnp.where(upper, mine, got)
        kept.append((upper, low))
        state = combine(low, high, mark)
    before = jnp.zeros_like(state)
    for step in range(halvings, steps):
        got = swap(state, step)
        upper = ((me >> step) & 1) == 1
        before = jnp.where(upper, combine(got, before, mark), before)
        low, high = jnp.where(upper, got, state), jnp.where(upper, state, got)
        state = combine(low, high, mark)
    for step in range(halvings - 1, -1, -1):
        upper, low = kept[step]
        after = combine(before, low, mark)
        mine, theirs = jnp.where(upper, after, before), jnp.where(upper, before, after)
        before = jnp.concatenate([mine, swap(theirs, step)], axis=0)
    return before


def flip_of(me, devices, owners):
    bits = owners.bit_length() - 1
    flip = jnp.zeros((), I32)
    for step in range(min(HALVINGS, devices.bit_length() - 1, bits)):
        flip = flip | (((me >> step) & 1) << (bits - 1 - step))
    return flip.reshape(1)


def body(features, home, account, flags):
    owners = lax.axis_size("users")
    devices = lax.axis_size("tm") * owners
    events, width = features.shape
    tiles = events // LANES
    me = lax.axis_index("tm") * owners + lax.axis_index("users")
    flip = flip_of(me, devices, owners)
    home2 = home.reshape(tiles, LANES)
    account2 = account.reshape(tiles, LANES)
    flags2 = flags.reshape(tiles, LANES)
    state = closing_states(flip, home2, account2, flags2, features, owners)
    local, key = local_sums(home2, account2, flags2, features)
    before = scan_states(state, me, devices, width)
    return final_means(flip, key, local, before, events, width)


def solution(mesh):
    return jax.shard_map(
        body,
        mesh=mesh,
        in_specs=(P(AXES, None), P(AXES, None), P(AXES), P(AXES)),
        out_specs=P(AXES, None),
        check_vma=False,
    )
```

time: 387 us -> 68.6 us (0.18)
  waiting for transfers between devices: 188 us -> 22.8 us
  matrix products: 90.2 us -> 0 us
  local copies, waits for them, and re-layouts: 49.7 us -> 3.8 us
  Pallas kernels: 0 us -> 30.5 us
  blocking collectives: 23.9 us -> 0 us
  other arithmetic: 16.1 us -> 0.46 us
  starting transfers between devices: 16 us -> 10.4 us
    all_to_all x3 -> x0, waiting for transfers between devices: 188 us -> none  [the longest x1 94 us: body(): lax.all_to_all(session_means.reshape(owners, slot_cap, feature_count), 'u...]
    dot_general x122 -> x0, matrix products: 90.2 us -> none  [the longest x16 27.3 us: session_advance(): inside_sum = jnp.dot(same_session, rows_values, precision=EXACT_MATMUL)]
    pallas_call x0 -> x3, Pallas kernels: none -> 30.5 us  [the longest x1 19.9 us: local_sums(): pl.pallas_call(local_kernel, out_shape=(jax.ShapeDtypeStruct((width + EXT...]
    scatter x2 -> x0, local copies, waits for them, and re-layouts: 29.2 us -> none  [the longest x1 16.1 us: body(): jnp.full((owners * slot_cap,), -1.0, jnp.float32).at[slot_index]]
    all_gather x3 -> x0, blocking collectives: 23.9 us -> none  [the longest x1 8.02 us: body(): lax.all_gather(closing_state[0], 'tm', axis=0, tiled=True)]
    ppermute x0 -> x7, waiting for transfers between devices: none -> 22.8 us  [swap(): lax.ppermute(value, AXES, [(i, i ^ 1 << step) for i in range(devices)])]
    gather x1 -> x0, local copies, waits for them, and re-layouts: 16.4 us -> none  [body(): returned_means.reshape(owners * slot_cap, feature_count)[slot_index]]
    all_to_all x3 -> x0, starting transfers between devices: 16 us -> none  [the longest x1 6.35 us: body(): lax.all_to_all(send_codes.reshape(owners, slot_cap), 'users', split_axis=...]
  transfers between devices with their start and end apart: 3 -> 7, of which waited for: 2 -> 6; matrix products, arithmetic and copies ran while one was open for 3% -> 0% of each run, Pallas kernels for 0% -> 29%
where the time goes in v1:
time: 68.6 us; the launch traced here: 68.1 us
  Pallas kernels  30.5 us (44%)
  waiting for transfers between devices  22.8 us (33%)
  starting transfers between devices  10.4 us (15%)
  local copies, waits for them, and re-layouts  3.8 us (6%)
    ppermute x7, waiting for transfers between devices, swap(): lax.ppermute(value, AXES, [(i, i ^ 1 << step) for i in range(devices)])  22.8 us
    pallas_call x1, Pallas kernels, local_sums(): pl.pallas_call(local_kernel, out_shape=(jax.ShapeDtypeStruct((width + EXT...  19.9 us
    ppermute x7, starting transfers between devices, swap(): lax.ppermute(value, AXES, [(i, i ^ 1 << step) for i in range(devices)])  10.4 us
    pallas_call x1, Pallas kernels, final_means(): pl.pallas_call(final_kernel, out_shape=jax.ShapeDtypeStruct((events, widt...  5.28 us
    pallas_call x1, Pallas kernels, closing_states(): pl.pallas_call(closing_kernel, out_shape=jax.ShapeDtypeStruct((owners, wi...  5.26 us
    unnamed x16, local copies, waits for them, and re-layouts  3.77 us
  transfers between devices with their start and end apart: 7, of which 6 were waited for; matrix products, arithmetic and copies ran while one was open for 0% of the time, Pallas kernels for 29%

profile of v1, /device:TPU:0, one launch (start us, length us, event | category | flops | bytes accessed | tf_op | source)
XLA Modules:
  0.0 68.1 jit_solution(2964237272220708424)
XLA Ops:
  0.0 0.0 copy-start
  0.0 1.6 %copy-done = f32[4096,128]{1,0:T(8,128)S(1)} copy-done((f32[4096,128]{1,0:T(8,128)S(1)}, f32[4096,128]{1,0:T(8,128)}, u32[]{:S(2)}) %copy-start) | copy-done | bytes 2097176
  1.6 0.0 copy-start.2
  1.6 0.7 %copy-done.2 = s32[4096,1]{0,1:T(1,128)S(1)} copy-done((s32[4096,1]{0,1:T(1,128)S(1)}, s32[4096,1]{0,1:T(1,128)}, u32[]{:S(2)}) %copy-start.2) | copy-done | bytes 16408
  2.3 0.0 copy-start.4
  2.3 0.7 %copy-done.4 = s32[4096]{0:T(1024)S(1)} copy-done((s32[4096]{0:T(1024)S(1)}, s32[4096]{0:T(1024)}, u32[]{:S(2)}) %copy-start.4) | copy-done | bytes 16408
  3.0 0.0 copy-start.6
  3.0 0.7 %copy-done.6 = s32[4096]{0:T(1024)S(1)} copy-done((s32[4096]{0:T(1024)S(1)}, s32[4096]{0:T(1024)}, u32[]{:S(2)}) %copy-start.6) | copy-done | bytes 16408
  3.7 5.3 %closing.1 = f32[8,136,128]{2,1,0:T(8,128)S(1)} custom-call(s32[1]{0:T(128)} %bitcast.flip_ref, s32[32,128]{1,0:T(8,128)S(1)} %bitcast.12, s32[32,128]{1,0:T(8,128)S(1)} %bitcast.14, s32[32,128]{1,0:T(8,128)S(1)} %bitcast.16, f32[4096,128]{1,0:T(8,128)S(1)} %copy-done), custom_call_target="tpu_custom_call" | custom-call | tf_op jit(solution)/shard_map/closing/pallas_call | solution.py:279
  9.0 0.6 collective-permute-start
  9.6 1.2 %collective-permute-done = f32[4,136,128]{2,1,0:T(8,128)S(1)} collective-permute-done((f32[4,136,128]{2,1,0:T(8,128)S(1)}, f32[4,136,128]{2,1,0:T(8,128)S(1)}, u32[]{:S(2)}, u32[]{:S(2)}) %collective-permute-start) | collective-permute-done | bytes 278560 | tf_op jit(solution)/shard_map/ppermute | solution.py:345
  10.8 0.1 multiply_add_fusion.1
  10.9 3.0 %collective-permute-start.1 = (f32[2,136,128]{2,1,0:T(8,128)S(1)}, f32[2,136,128]{2,1,0:T(8,128)S(1)}, u32[]{:S(2)}, u32[]{:S(2)}) collective-permute-start(f32[2,136,128]{2,1,0:T(8,128)S(1)} %slice.52), channel_id=1, source_target_pairs={{0,2},{1,3},{2,0},{3,1},{4,6},{5,7},{6,4},{7,5},{8,10},{9,11},{10,... | collective-permute-start | bytes 417800 | tf_op jit(solution)/shard_map/ppermute | solution.py:345
  13.9 4.0 %collective-permute-done.1 = f32[2,136,128]{2,1,0:T(8,128)S(1)} collective-permute-done((f32[2,136,128]{2,1,0:T(8,128)S(1)}, f32[2,136,128]{2,1,0:T(8,128)S(1)}, u32[]{:S(2)}, u32[]{:S(2)}) %collective-permute-start.1) | collective-permute-done | bytes 139296 | tf_op jit(solution)/shard_map/ppermute | solution.py:345
  18.0 0.0 copy-start.1
  18.0 0.0 copy-start.3
  18.0 0.0 copy-start.5
  18.0 0.0 copy-start.7
  18.0 2.8 %collective-permute-start.2 = (f32[2,136,128]{2,1,0:T(8,128)S(1)}, f32[2,136,128]{2,1,0:T(8,128)S(1)}, u32[]{:S(2)}, u32[]{:S(2)}) collective-permute-start(f32[2,136,128]{2,1,0:T(8,128)S(1)} %get-tuple-element.9), channel_id=1, source_target_pairs={{0,4},{1,5},{2,6},{3,7},{4,0},{5,1},{6,2},{7,3},{8,12},{9,13},{10,... | collective-permute-start | bytes 417800 | tf_op jit(solution)/shard_map/ppermute | solution.py:345
  20.8 6.3 %collective-permute-done.2 = f32[2,136,128]{2,1,0:T(8,128)S(1)} collective-permute-done((f32[2,136,128]{2,1,0:T(8,128)S(1)}, f32[2,136,128]{2,1,0:T(8,128)S(1)}, u32[]{:S(2)}, u32[]{:S(2)}) %collective-permute-start.2) | collective-permute-done | bytes 139296 | tf_op jit(solution)/shard_map/ppermute | solution.py:345
  27.2 1.4 %collective-permute-start.3 = (f32[2,136,128]{2,1,0:T(8,128)S(1)}, f32[2,136,128]{2,1,0:T(8,128)S(1)}, u32[]{:S(2)}, u32[]{:S(2)}) collective-permute-start(f32[2,136,128]{2,1,0:T(8,128)S(1)} %get-tuple-element.19), channel_id=1, source_target_pairs={{0,8},{1,9},{2,10},{3,11},{4,12},{5,13},{6,14},{7,15},{8,0},{9,1},... | collective-permute-start | bytes 417800 | tf_op jit(solution)/shard_map/ppermute | solution.py:345
  28.6 3.7 %collective-permute-done.3 = f32[2,136,128]{2,1,0:T(8,128)S(1)} collective-permute-done((f32[2,136,128]{2,1,0:T(8,128)S(1)}, f32[2,136,128]{2,1,0:T(8,128)S(1)}, u32[]{:S(2)}, u32[]{:S(2)}) %collective-permute-start.3) | collective-permute-done | bytes 139296 | tf_op jit(solution)/shard_map/ppermute | solution.py:345
  32.3 0.1 multiply_add_fusion.3
  32.4 1.5 %collective-permute-start.4 = (f32[2,136,128]{2,1,0:T(8,128)S(1)}, f32[2,136,128]{2,1,0:T(8,128)S(1)}, u32[]{:S(2)}, u32[]{:S(2)}) collective-permute-start(f32[2,136,128]{2,1,0:T(8,128)S(1)} %get-tuple-element.17), channel_id=1, source_target_pairs={{0,16},{1,17},{2,18},{3,19},{4,20},{5,21},{6,22},{7,23},{8,24},{9,... | collective-permute-start | bytes 417800 | tf_op jit(solution)/shard_map/ppermute | solution.py:345
  33.9 3.6 %collective-permute-done.4 = f32[2,136,128]{2,1,0:T(8,128)S(1)} collective-permute-done((f32[2,136,128]{2,1,0:T(8,128)S(1)}, f32[2,136,128]{2,1,0:T(8,128)S(1)}, u32[]{:S(2)}, u32[]{:S(2)}) %collective-permute-start.4) | collective-permute-done | bytes 139296 | tf_op jit(solution)/shard_map/ppermute | solution.py:345
  37.6 1.1 %collective-permute-start.5 = (f32[2,136,128]{2,1,0:T(8,128)S(1)}, f32[2,136,128]{2,1,0:T(8,128)S(1)}, u32[]{:S(2)}, u32[]{:S(2)}) collective-permute-start(f32[2,136,128]{2,1,0:T(8,128)S(1)} %get-tuple-element.16), channel_id=1, source_target_pairs={{0,2},{1,3},{2,0},{3,1},{4,6},{5,7},{6,4},{7,5},{8,10},{9,11},{10,... | collective-permute-start | bytes 417800 | tf_op jit(solution)/shard_map/ppermute | solution.py:345
  38.6 4.1 %collective-permute-done.5 = f32[2,136,128]{2,1,0:T(8,128)S(1)} collective-permute-done((f32[2,136,128]{2,1,0:T(8,128)S(1)}, f32[2,136,128]{2,1,0:T(8,128)S(1)}, u32[]{:S(2)}, u32[]{:S(2)}) %collective-permute-start.5) | collective-permute-done | bytes 139296 | tf_op jit(solution)/shard_map/ppermute | solution.py:345
  42.7 0.1 fusion.1
  42.7 0.1 collective-permute-start.6
  42.8 0.0 copy-done.1
  42.8 0.0 copy-done.3
  42.8 0.0 copy-done.5
  42.8 0.0 copy-done.7
  42.9 19.9 %local.1 = (f32[136,4096]{1,0:T(8,128)S(1)}, s32[32,128]{1,0:T(8,128)S(1)}) custom-call(s32[32,128]{1,0:T(8,128)S(1)} %bitcast.13, s32[32,128]{1,0:T(8,128)S(1)} %bitcast.15, s32[32,128]{1,0:T(8,128)S(1)} %bitcast.17, f32[4096,128]{1,0:T(8,128)S(1)} %copy-done.1), custom_call_target="tpu_custom_call" | custom-call | tf_op jit(solution)/shard_map/local/pallas_call | solution.py:296
  62.8 0.0 collective-permute-done.6
  62.9 5.3 %final.1 = f32[4096,128]{1,0:T(8,128)} custom-call(s32[1]{0:T(128)} %bitcast.flip_ref, s32[32,128]{1,0:T(8,128)S(1)} %get-tuple-element.7.key_ref, f32[136,4096]{1,0:T(8,128)S(1)} %get-tuple-element.8.local_ref, f32[8,136,128]{2,1,0:T(8,128)S(1)} %pad_maximum_fusion.state_ref), custom_call_target="tpu_custom_call" | custom-call | tf_op jit(solution)/shard_map/final/pallas_call | solution.py:318
  (18 shorter events, 0.3 us)
Async XLA Ops:
  0.0 1.6 %copy-start = (f32[4096,128]{1,0:T(8,128)S(1)}, f32[4096,128]{1,0:T(8,128)}, u32[]{:S(2)}) copy-start(f32[4096,128]{1,0:T(8,128)} %x_ref.3) | copy-start | bytes 6291460
  1.6 0.7 %copy-start.2 = (s32[4096,1]{0,1:T(1,128)S(1)}, s32[4096,1]{0,1:T(1,128)}, u32[]{:S(2)}) copy-start(s32[4096,1]{0,1:T(1,128)} %param.5) | copy-start | bytes 49156
  2.3 0.7 %copy-start.4 = (s32[4096]{0:T(1024)S(1)}, s32[4096]{0:T(1024)}, u32[]{:S(2)}) copy-start(s32[4096]{0:T(1024)} %param.6) | copy-start | bytes 49156
  3.0 0.7 %copy-start.6 = (s32[4096]{0:T(1024)S(1)}, s32[4096]{0:T(1024)}, u32[]{:S(2)}) copy-start(s32[4096]{0:T(1024)} %param.7) | copy-start | bytes 49156
  9.0 1.7 %collective-permute-start = (f32[4,136,128]{2,1,0:T(8,128)S(1)}, f32[4,136,128]{2,1,0:T(8,128)S(1)}, u32[]{:S(2)}, u32[]{:S(2)}) collective-permute-start(f32[4,136,128]{2,1,0:T(8,128)S(1)} %slice.48), channel_id=1, source_target_pairs={{0,1},{1,0},{2,3},{3,2},{4,5},{5,4},{6,7},{7,6},{8,9},{9,8},{10,11... | collective-permute-start | bytes 835592 | tf_op jit(solution)/shard_map/ppermute | solution.py:345
  10.9 7.0 %collective-permute-start.1 = (f32[2,136,128]{2,1,0:T(8,128)S(1)}, f32[2,136,128]{2,1,0:T(8,128)S(1)}, u32[]{:S(2)}, u32[]{:S(2)}) collective-permute-start(f32[2,136,128]{2,1,0:T(8,128)S(1)} %slice.52), channel_id=1, source_target_pairs={{0,2},{1,3},{2,0},{3,1},{4,6},{5,7},{6,4},{7,5},{8,10},{9,11},{10,... | collective-permute-start | bytes 417800 | tf_op jit(solution)/shard_map/ppermute | solution.py:345
  18.0 24.8 %copy-start.1 = (f32[4096,128]{1,0:T(8,128)S(1)}, f32[4096,128]{1,0:T(8,128)}, u32[]{:S(2)}) copy-start(f32[4096,128]{1,0:T(8,128)} %x_ref.3) | copy-start | bytes 6291460
  18.0 24.8 %copy-start.3 = (s32[4096,1]{0,1:T(1,128)S(1)}, s32[4096,1]{0,1:T(1,128)}, u32[]{:S(2)}) copy-start(s32[4096,1]{0,1:T(1,128)} %param.5) | copy-start | bytes 49156
  18.0 24.8 %copy-start.5 = (s32[4096]{0:T(1024)S(1)}, s32[4096]{0:T(1024)}, u32[]{:S(2)}) copy-start(s32[4096]{0:T(1024)} %param.6) | copy-start | bytes 49156
  18.0 24.8 %copy-start.7 = (s32[4096]{0:T(1024)S(1)}, s32[4096]{0:T(1024)}, u32[]{:S(2)}) copy-start(s32[4096]{0:T(1024)} %param.7) | copy-start | bytes 49156
  18.0 9.1 %collective-permute-start.2 = (f32[2,136,128]{2,1,0:T(8,128)S(1)}, f32[2,136,128]{2,1,0:T(8,128)S(1)}, u32[]{:S(2)}, u32[]{:S(2)}) collective-permute-start(f32[2,136,128]{2,1,0:T(8,128)S(1)} %get-tuple-element.9), channel_id=1, source_target_pairs={{0,4},{1,5},{2,6},{3,7},{4,0},{5,1},{6,2},{7,3},{8,12},{9,13},{10,... | collective-permute-start | bytes 417800 | tf_op jit(solution)/shard_map/ppermute | solution.py:345
  27.2 5.1 %collective-permute-start.3 = (f32[2,136,128]{2,1,0:T(8,128)S(1)}, f32[2,136,128]{2,1,0:T(8,128)S(1)}, u32[]{:S(2)}, u32[]{:S(2)}) collective-permute-start(f32[2,136,128]{2,1,0:T(8,128)S(1)} %get-tuple-element.19), channel_id=1, source_target_pairs={{0,8},{1,9},{2,10},{3,11},{4,12},{5,13},{6,14},{7,15},{8,0},{9,1},... | collective-permute-start | bytes 417800 | tf_op jit(solution)/shard_map/ppermute | solution.py:345
  32.4 5.1 %collective-permute-start.4 = (f32[2,136,128]{2,1,0:T(8,128)S(1)}, f32[2,136,128]{2,1,0:T(8,128)S(1)}, u32[]{:S(2)}, u32[]{:S(2)}) collective-permute-start(f32[2,136,128]{2,1,0:T(8,128)S(1)} %get-tuple-element.17), channel_id=1, source_target_pairs={{0,16},{1,17},{2,18},{3,19},{4,20},{5,21},{6,22},{7,23},{8,24},{9,... | collective-permute-start | bytes 417800 | tf_op jit(solution)/shard_map/ppermute | solution.py:345
  37.6 5.1 %collective-permute-start.5 = (f32[2,136,128]{2,1,0:T(8,128)S(1)}, f32[2,136,128]{2,1,0:T(8,128)S(1)}, u32[]{:S(2)}, u32[]{:S(2)}) collective-permute-start(f32[2,136,128]{2,1,0:T(8,128)S(1)} %get-tuple-element.16), channel_id=1, source_target_pairs={{0,2},{1,3},{2,0},{3,1},{4,6},{5,7},{6,4},{7,5},{8,10},{9,11},{10,... | collective-permute-start | bytes 417800 | tf_op jit(solution)/shard_map/ppermute | solution.py:345
  42.7 20.1 %collective-permute-start.6 = (f32[4,136,128]{2,1,0:T(8,128)S(1)}, f32[4,136,128]{2,1,0:T(8,128)S(1)}, u32[]{:S(2)}, u32[]{:S(2)}) collective-permute-start(f32[4,136,128]{2,1,0:T(8,128)S(1)} %get-tuple-element.14), channel_id=1, source_target_pairs={{0,1},{1,0},{2,3},{3,2},{4,5},{5,4},{6,7},{7,6},{8,9},{9,8},{10,11... | collective-permute-start | bytes 835592 | tf_op jit(solution)/shard_map/ppermute | solution.py:345

commit v2 on v1

v2 whole, which is shorter than its diff:
```python
import functools

import jax
import jax.numpy as jnp
from jax import lax
from jax.experimental import pallas as pl
from jax.experimental.pallas import tpu as pltpu
from jax.sharding import PartitionSpec as P


ACCOUNTS = 128
LANES = 128
EXTRA = 8
LEVELS = (1, 2)
STARTS = (0, 4, 6)
AXES = ("tm", "users")
F32, BF16, I32 = jnp.float32, jnp.bfloat16, jnp.int32


def split_two(x):
    high = x.astype(BF16)
    return high, (x - high.astype(F32)).astype(BF16)


def account_ids():
    return lax.broadcasted_iota(I32, (ACCOUNTS, LANES), 0).astype(F32).astype(BF16)


def row_positions(tiles):
    shape = (tiles, LANES)
    return lax.broadcasted_iota(I32, shape, 0) * LANES + lax.broadcasted_iota(I32, shape, 1)


def small(value):
    return jnp.asarray(value, BF16)


def closing_kernel(
    flip_ref,
    home_hbm,
    account_hbm,
    flag_hbm,
    x_hbm,
    out_ref,
    home_ref,
    account_ref,
    flag_ref,
    x_ref,
    parts_ref,
    last_ref,
    sems,
):
    pairs = (
        (home_hbm, home_ref),
        (account_hbm, account_ref),
        (flag_hbm, flag_ref),
        (x_hbm, x_ref),
    )
    copies = [pltpu.make_async_copy(a, b, sems.at[i]) for i, (a, b) in enumerate(pairs)]
    for copy in copies:
        copy.start()
    tiles = home_ref.shape[0]
    owners, rows = out_ref.shape[0], out_ref.shape[1]
    events, features = x_ref.shape
    chunk = min(512, events)
    group = 2 if owners % 2 == 0 else 1
    flip = flip_ref[0]
    ids = account_ids()
    lane = lax.broadcasted_iota(I32, (ACCOUNTS, LANES), 1).astype(F32)
    for copy in copies[:3]:
        copy.wait()
    home = home_ref[...]
    account = account_ref[...]
    flag = flag_ref[...]
    account_f = account.astype(F32)

    def find_last(owner, carry):
        kept = jnp.where((home == owner) & (flag == 1), account_f, -1.0).astype(BF16)
        latest = jnp.full((ACCOUNTS, LANES), -1.0, BF16)
        for tile in range(tiles):
            latest = jnp.where(kept[tile : tile + 1] == ids, small(tile), latest)
        latest = latest.astype(F32)
        place = jnp.where(latest >= 0.0, latest * LANES + lane, -1.0)
        last_ref[pl.ds(owner, 1), :] = jnp.max(place.T, axis=0, keepdims=True)
        return carry

    lax.fori_loop(0, owners, find_last, 0, unroll=min(owners, 8))

    def look_up(owner, least):
        row = jnp.broadcast_to(last_ref[pl.ds(owner, 1), :], (tiles, LANES))
        return jnp.where(home == owner, jnp.take_along_axis(row, account, axis=1), least)

    least = jnp.full((tiles, LANES), -1.0, F32)
    least = lax.fori_loop(0, owners, look_up, least, unroll=min(owners, 8))
    live = row_positions(tiles).astype(F32) >= least
    weight = jnp.where(flag == 1, 65.0, 1.0).astype(BF16)

    copies[3].wait()
    high, low = split_two(x_ref[...])
    parts_ref[:, 0:features] = high
    parts_ref[:, features : 2 * features] = low

    def one_group(number, carry):
        kept = [
            jnp.where(live & (home == number * group + i), account_f, -1.0).astype(BF16)
            for i in range(group)
        ]
        total = jnp.zeros((group * ACCOUNTS, 2 * features), F32)
        counts = [jnp.zeros((ACCOUNTS, LANES), BF16) for _ in range(group)]
        for first in range(0, events, chunk):
            blocks = []
            for i in range(group):
                pieces = []
                for tile in range(first // LANES, (first + chunk) // LANES):
                    mask = kept[i][tile : tile + 1] == ids
                    share = jnp.broadcast_to(weight[tile : tile + 1], mask.shape)
                    counts[i] = counts[i] + jnp.where(mask, share, small(0.0))
                    pieces.append(jnp.where(mask, small(1.0), small(0.0)))
                blocks.append(jnp.concatenate(pieces, axis=1))
            total = total + jnp.dot(
                jnp.concatenate(blocks, axis=0),
                parts_ref[first : first + chunk, :],
                preferred_element_type=F32,
            )
        sums = total[:, 0:features] + total[:, features : 2 * features]
        for i in range(group):
            place = jnp.bitwise_xor(number * group + i, flip)
            out_ref[place, 0:features, :] = sums[i * ACCOUNTS : (i + 1) * ACCOUNTS].T
            count = counts[i].astype(F32)
            count = jnp.where(count >= 64.0, count + (8192.0 - 64.0), count)
            tally = jnp.sum(count.T, axis=0, keepdims=True)
            marked = jnp.where(tally >= 8192.0, 1.0, 0.0)
            spot = lax.broadcasted_iota(I32, (rows - features, LANES), 0)
            out_ref[place, features:rows, :] = jnp.where(
                spot == 0, tally - 8192.0 * marked, jnp.where(spot == 1, marked, 0.0)
            )
        return carry

    lax.fori_loop(0, owners // group, one_group, 0, unroll=min(owners // group, 4))


def turn(row):
    return jnp.broadcast_to(row, (LANES, LANES)).T


def parts_kernel(x_ref, parts_ref):
    events, features = x_ref.shape
    rows = parts_ref.shape[0]
    for first in range(0, events, LANES):
        span = slice(first, first + LANES)
        high, low = split_two(x_ref[span, :].T)
        parts_ref[0:features, span] = high
        parts_ref[features : 2 * features, span] = low
    extra = lax.broadcasted_iota(I32, (rows - 2 * features, events), 0)
    parts_ref[2 * features : rows, :] = jnp.where(extra == 0, 1.0, 0.0).astype(BF16)


def stats_kernel(home_ref, account_ref, flag_ref, column_ref, sid_ref, key_ref, start_ref):
    tiles = home_ref.shape[0]
    events = tiles * LANES
    user = home_ref[...] * ACCOUNTS + account_ref[...]
    user_f = user.astype(F32)
    flagged = jnp.where(flag_ref[...] == 1, user_f, -1.0)
    row_id = lax.broadcasted_iota(I32, (LANES, LANES), 0)
    reaches = row_id <= lax.broadcasted_iota(I32, (LANES, LANES), 1)
    spot = row_id.astype(F32)
    for tile in range(tiles):
        column_ref[tile * LANES : (tile + 1) * LANES, :] = turn(flagged[tile : tile + 1])

    wide = 4 if tiles % 4 == 0 else 1
    for first in range(0, tiles, wide):
        mine = [user_f[first + i : first + i + 1] for i in range(wide)]

        def earlier(other, latest):
            column = column_ref[pl.ds(pl.multiple_of(other * LANES, LANES), LANES), :]
            place = spot + (other * LANES).astype(F32)
            return tuple(jnp.where(column == mine[i], place, latest[i]) for i in range(wide))

        latest = tuple(jnp.full((LANES, LANES), -1.0, F32) for _ in range(wide))
        latest = list(lax.fori_loop(0, first, earlier, latest))
        for i in range(wide):
            for other in range(first, first + i + 1):
                column = column_ref[other * LANES : (other + 1) * LANES, :]
                mask = column == mine[i]
                if other == first + i:
                    mask = mask & reaches
                latest[i] = jnp.where(mask, spot + float(other * LANES), latest[i])
            start_ref[first + i : first + i + 1, :] = jnp.max(latest[i], axis=0, keepdims=True)
    start = start_ref[...]
    key_ref[...] = jnp.where(start < 0.0, user, -1)
    sid = jnp.where(start < 0.0, user_f + float(events), start)
    sid_ref[...] = sid
    for tile in range(tiles):
        column_ref[tile * LANES : (tile + 1) * LANES, :] = turn(sid[tile : tile + 1])


def local_kernel(parts_ref, column_ref, sid_ref, out_ref, mask_ref, *, first, chunk):
    features = out_ref.shape[0] - EXTRA
    reaches = lax.broadcasted_iota(I32, (LANES, LANES), 0) <= lax.broadcasted_iota(
        I32, (LANES, LANES), 1
    )
    sid = sid_ref[...]
    for begin in range(first, first + out_ref.shape[1], chunk):
        slot = (begin // chunk) % 2
        depth = begin + chunk
        lines = [sid[t : t + 1] for t in range(begin // LANES, depth // LANES)]
        for c in range(0, depth, LANES):
            column = column_ref[c : c + LANES, :]
            for i, line in enumerate(lines):
                r = begin + i * LANES
                if c > r:
                    block = jnp.zeros((LANES, LANES), BF16)
                else:
                    mask = column == line
                    if c == r:
                        mask = mask & reaches
                    block = jnp.where(mask, 1.0, 0.0).astype(BF16)
                mask_ref[slot, c : c + LANES, i * LANES : (i + 1) * LANES] = block
        total = jnp.dot(
            parts_ref[:, 0:depth], mask_ref[slot, 0:depth, :], preferred_element_type=F32
        )
        span = slice(begin - first, begin - first + chunk)
        out_ref[0:features, span] = total[0:features] + total[features : 2 * features]
        out_ref[features:, span] = total[2 * features : 2 * features + EXTRA]


def final_kernel(flip_ref, key_ref, state_ref, *refs, starts, chunk):
    local_refs, out_ref, table_ref = refs[: len(starts)], refs[-4], refs[-3]
    stage_ref, sems = refs[-2], refs[-1]
    owners = state_ref.shape[0]
    events, features = out_ref.shape
    rows = table_ref.shape[0]
    flip = flip_ref[0]
    group = min(8, owners)
    ids = account_ids()

    def fill(owner, carry):
        place = jnp.bitwise_xor(owner, flip)
        high, low = split_two(state_ref[place, 0:features, :])
        span = pl.ds(pl.multiple_of(owner * ACCOUNTS, ACCOUNTS), ACCOUNTS)
        table_ref[0:features, span] = high
        table_ref[features : 2 * features, span] = low
        count = state_ref[place, features : features + 1, :].astype(I32)
        digit = lax.broadcasted_iota(I32, (rows - 2 * features, LANES), 0)
        extra = jnp.where(
            digit == 0,
            lax.shift_right_logical(count, 16),
            jnp.where(
                digit == 1,
                lax.shift_right_logical(count, 8) & 255,
                jnp.where(digit == 2, count & 255, 0),
            ),
        )
        table_ref[2 * features : rows, span] = extra.astype(F32).astype(BF16)
        return carry

    lax.fori_loop(0, owners, fill, 0, unroll=min(owners, 8))

    key = key_ref[...]
    account_f = (key & (ACCOUNTS - 1)).astype(F32)
    home = lax.shift_right_arithmetic(key, ACCOUNTS.bit_length() - 1)
    copies = []
    for begin in range(0, events, chunk):
        number = begin // chunk
        piece = max(i for i in range(len(starts)) if starts[i] <= begin)
        local_ref = local_refs[piece]
        span = slice(begin - starts[piece], begin - starts[piece] + chunk)

        def part(step, total):
            lines = []
            for i in range(group):
                mine = jnp.where(home == step * group + i, account_f, -1.0).astype(BF16)
                blocks = [
                    jnp.where(mine[tile : tile + 1] == ids, small(1.0), small(0.0))
                    for tile in range(begin // LANES, (begin + chunk) // LANES)
                ]
                lines.append(jnp.concatenate(blocks, axis=1))
            place = pl.ds(pl.multiple_of(step * group * ACCOUNTS, LANES), group * ACCOUNTS)
            found = jnp.dot(
                table_ref[:, place], jnp.concatenate(lines, axis=0), preferred_element_type=F32
            )
            return found if total is None else total + found

        if owners == group:
            total = part(0, None)
        else:
            total = lax.fori_loop(0, owners // group, part, jnp.zeros((rows, chunk), F32))
        more = total[2 * features : 2 * features + 3]
        count = local_ref[features : features + 1, span] + (
            more[0:1] * 65536.0 + more[1:2] * 256.0 + more[2:3]
        )
        sums = local_ref[0:features, span] + (total[0:features] + total[features : 2 * features])
        stage_ref[begin : begin + chunk, :] = (sums * (1.0 / count)).T
        copy = pltpu.make_async_copy(
            stage_ref.at[pl.ds(begin, chunk), :],
            out_ref.at[pl.ds(begin, chunk), :],
            sems.at[number],
        )
        copy.start()
        copies.append(copy)
    for copy in copies:
        copy.wait()


VMEM = pl.BlockSpec(memory_space=pltpu.VMEM)
SMEM = pl.BlockSpec(memory_space=pltpu.SMEM)
HBM = pl.BlockSpec(memory_space=pltpu.HBM)
PARAMS = pltpu.CompilerParams(vmem_limit_bytes=28 * 1024 * 1024)


def closing_states(flip, home, account, flags, features, owners):
    events, width = features.shape
    tiles = events // LANES
    home, account, flags, features = [
        pltpu.with_memory_space_constraint(v, pltpu.HBM) for v in (home, account, flags, features)
    ]
    return pl.pallas_call(
        closing_kernel,
        out_shape=jax.ShapeDtypeStruct((owners, width + EXTRA, LANES), F32),
        in_specs=[SMEM, HBM, HBM, HBM, HBM],
        out_specs=VMEM,
        scratch_shapes=[pltpu.VMEM((tiles, LANES), I32)] * 3
        + [
            pltpu.VMEM((events, width), F32),
            pltpu.VMEM((events, 2 * width), BF16),
            pltpu.VMEM((max(8, owners), LANES), F32),
            pltpu.SemaphoreType.DMA((4,)),
        ],
        compiler_params=PARAMS,
        name="closing",
    )(flip, home, account, flags, features)


def feature_parts(features):
    events, width = features.shape
    return pl.pallas_call(
        parts_kernel,
        out_shape=jax.ShapeDtypeStruct((2 * width + 16, events), BF16),
        in_specs=[VMEM],
        out_specs=VMEM,
        compiler_params=PARAMS,
        name="parts",
    )(features)


def event_stats(home, account, flags):
    tiles = home.shape[0]
    return pl.pallas_call(
        stats_kernel,
        out_shape=(
            jax.ShapeDtypeStruct((tiles * LANES, LANES), F32),
            jax.ShapeDtypeStruct((tiles, LANES), F32),
            jax.ShapeDtypeStruct((tiles, LANES), I32),
        ),
        in_specs=[VMEM, VMEM, VMEM],
        out_specs=(VMEM, VMEM, VMEM),
        scratch_shapes=[pltpu.VMEM((tiles, LANES), F32)],
        compiler_params=PARAMS,
        name="stats",
    )(home, account, flags)


def local_sums(parts, column, sid, first, length, width):
    chunk = min(512, length)
    return pl.pallas_call(
        functools.partial(local_kernel, first=first, chunk=chunk),
        out_shape=jax.ShapeDtypeStruct((width + EXTRA, length), F32),
        in_specs=[VMEM, VMEM, VMEM],
        out_specs=VMEM,
        scratch_shapes=[pltpu.VMEM((2, first + length, chunk), BF16)],
        compiler_params=PARAMS,
        name="local",
    )(parts, column, sid)


def final_means(flip, key, state, pieces, starts, events, width):
    chunk = min(512, events)
    owners = state.shape[0]
    return pl.pallas_call(
        functools.partial(final_kernel, starts=starts, chunk=chunk),
        out_shape=jax.ShapeDtypeStruct((events, width), F32),
        in_specs=[SMEM, VMEM, VMEM] + [VMEM] * len(pieces),
        out_specs=HBM,
        scratch_shapes=[
            pltpu.VMEM((2 * width + 16, owners * ACCOUNTS), BF16),
            pltpu.VMEM((events, width), F32),
            pltpu.SemaphoreType.DMA((events // chunk,)),
        ],
        compiler_params=PARAMS,
        name="final",
    )(flip, key, state, *pieces)


def combine(earlier, later, mark):
    return later + (1.0 - later[:, mark : mark + 1, :]) * earlier


def pick(parts, bits):
    for place, bit in enumerate(bits):
        step = 1 << place
        parts = [jnp.where(bit, parts[i ^ step], parts[i]) for i in range(len(parts))]
    return parts


def levels_of(devices, owners):
    left, levels = min(devices, owners).bit_length() - 1, []
    for want in LEVELS:
        if left > 0:
            levels.append(min(want, left))
            left -= levels[-1]
    return levels


def scan_states(state, me, devices, width, levels):
    mark = width + 1
    steps = devices.bit_length() - 1

    def swap(value, mask):
        return lax.ppermute(value, AXES, [(i, i ^ mask) for i in range(devices)])

    def bit(step):
        return ((me >> step) & 1) == 1

    saved, done = [], 0
    for level in levels:
        part = state.shape[0] >> level
        got = [state[:part]]
        for other in range(1, 1 << level):
            piece = state[other * part : (other + 1) * part]
            got.append(swap(piece, other << done))
        bits = [bit(done + i) for i in range(level)]
        ordered = pick(got, bits)
        saved.append((done, bits, ordered))
        state = ordered[0]
        for later in ordered[1:]:
            state = combine(state, later, mark)
        done += level
    before = jnp.zeros_like(state)
    for step in range(done, steps):
        got = swap(state, 1 << step)
        before = jnp.where(bit(step), combine(got, before, mark), before)
        if step < steps - 1:
            low, high = jnp.where(bit(step), got, state), jnp.where(bit(step), state, got)
            state = combine(low, high, mark)
    for done, bits, ordered in reversed(saved):
        prefixes = [before]
        for earlier in ordered[:-1]:
            prefixes.append(combine(prefixes[-1], earlier, mark))
        mine = pick(prefixes, bits)
        got = [mine[0]]
        for other in range(1, len(mine)):
            got.append(swap(mine[other], other << done))
        before = jnp.concatenate(got, axis=0)
    return before


def flip_of(me, levels, owners):
    flip, done, top = jnp.zeros((), I32), 0, owners.bit_length() - 1
    for level in levels:
        top -= level
        flip = flip | (((me >> done) & ((1 << level) - 1)) << top)
        done += level
    return flip.reshape(1)


def body(features, home, account, flags):
    owners = lax.axis_size("users")
    devices = lax.axis_size("tm") * owners
    events, width = features.shape
    tiles = events // LANES
    me = lax.axis_index("tm") * owners + lax.axis_index("users")
    levels = levels_of(devices, owners)
    flip = flip_of(me, levels, owners)
    home2 = home.reshape(tiles, LANES)
    account2 = account.reshape(tiles, LANES)
    flags2 = flags.reshape(tiles, LANES)
    state = closing_states(flip, home2, account2, flags2, features, owners)
    column, sid, key = event_stats(home2, account2, flags2)
    parts = feature_parts(features)
    starts = [events * i // 8 for i in STARTS]
    pieces = []
    for i, first in enumerate(starts):
        length = (starts + [events])[i + 1] - first
        pieces.append(local_sums(parts, column, sid, first, length, width))
    before = scan_states(state, me, devices, width, levels)
    return final_means(flip, key, before, pieces, starts, events, width)


def solution(mesh):
    return jax.shard_map(
        body,
        mesh=mesh,
        in_specs=(P(AXES, None), P(AXES, None), P(AXES), P(AXES)),
        out_specs=P(AXES, None),
        check_vma=False,
    )
```

time: 68.6 us -> 54.4 us (0.79)
  Pallas kernels: 30.5 us -> 22 us
  waiting for transfers between devices: 22.8 us -> 17.5 us
  local copies, waits for them, and re-layouts: 3.8 us -> 0.06 us
  starting transfers between devices: 10.4 us -> 13.8 us
    pallas_call x2 -> x6, Pallas kernels: 25.2 us -> 17.8 us  [the longest x1 7.08 us: event_stats(): pl.pallas_call(stats_kernel, out_shape=(jax.ShapeDtypeStruct((tiles * LAN...]
    ppermute x7 -> x10, waiting for transfers between devices: 22.8 us -> 17.5 us  [swap(): return lax.ppermute(value, AXES, [(i, i ^ mask) for i in range(devices)])]
    unnamed x16 -> x8, local copies, waits for them, and re-layouts: 3.77 us -> 0.03 us
    ppermute x7 -> x10, starting transfers between devices: 10.4 us -> 13.8 us  [swap(): return lax.ppermute(value, AXES, [(i, i ^ mask) for i in range(devices)])]
    pallas_call x1, Pallas kernels: 5.26 us -> 4.19 us  [closing_states(): pl.pallas_call(closing_kernel, out_shape=jax.ShapeDtypeStruct((owners, wi...]
  transfers between devices with their start and end apart: 7 -> 10, of which waited for: 6 -> 7; matrix products, arithmetic and copies ran while one was open for 0% -> 0% of each run, Pallas kernels for 29% -> 26%
where the time goes in v2:
time: 54.4 us; the launch traced here: 54.1 us
  Pallas kernels  22 us (40%)
  waiting for transfers between devices  17.5 us (32%)
  starting transfers between devices  13.8 us (25%)
    ppermute x10, waiting for transfers between devices, swap(): return lax.ppermute(value, AXES, [(i, i ^ mask) for i in range(devices)])  17.5 us
    ppermute x10, starting transfers between devices, swap(): return lax.ppermute(value, AXES, [(i, i ^ mask) for i in range(devices)])  13.8 us
    pallas_call x1, Pallas kernels, event_stats(): pl.pallas_call(stats_kernel, out_shape=(jax.ShapeDtypeStruct((tiles * LAN...  7.08 us
    pallas_call x3, Pallas kernels, local_sums(): pl.pallas_call(functools.partial(local_kernel, first=first, chunk=chunk),...  6.46 us
    pallas_call x1, Pallas kernels, closing_states(): pl.pallas_call(closing_kernel, out_shape=jax.ShapeDtypeStruct((owners, wi...  4.19 us
    pallas_call x1, Pallas kernels, final_means(): pl.pallas_call(functools.partial(final_kernel, starts=starts, chunk=chunk...  3.62 us
  transfers between devices with their start and end apart: 10, of which 7 were waited for; matrix products, arithmetic and copies ran while one was open for 0% of the time, Pallas kernels for 26%

profile of v2, /device:TPU:0, one launch (start us, length us, event | category | flops | bytes accessed | tf_op | source)
XLA Modules:
  0.0 54.1 jit_solution(17752231047916828778)
XLA Ops:
  0.0 4.2 %closing.1 = f32[8,136,128]{2,1,0:T(8,128)S(1)} custom-call(s32[1]{0:T(128)} %bitcast.flip_ref, s32[32,128]{1,0:T(8,128)} %bitcast.18, s32[32,128]{1,0:T(8,128)} %bitcast.20, s32[32,128]{1,0:T(8,128)} %bitcast.22, f32[4096,128]{1,0:T(8,128)} %x_ref.1), custom_call_target="tpu_custom_call" | custom-call | tf_op jit(solution)/shard_map/closing/pallas_call | solution.py:317
  4.2 0.6 %collective-permute-start = (f32[4,136,128]{2,1,0:T(8,128)S(1)}, f32[4,136,128]{2,1,0:T(8,128)S(1)}, u32[]{:S(2)}, u32[]{:S(2)}) collective-permute-start(f32[4,136,128]{2,1,0:T(8,128)S(1)} %slice.58), channel_id=1, source_target_pairs={{0,1},{1,0},{2,3},{3,2},{4,5},{5,4},{6,7},{7,6},{8,9},{9,8},{10,11... | collective-permute-start | bytes 835592 | tf_op jit(solution)/shard_map/ppermute | solution.py:419
  4.8 1.2 %collective-permute-done = f32[4,136,128]{2,1,0:T(8,128)S(1)} collective-permute-done((f32[4,136,128]{2,1,0:T(8,128)S(1)}, f32[4,136,128]{2,1,0:T(8,128)S(1)}, u32[]{:S(2)}, u32[]{:S(2)}) %collective-permute-start) | collective-permute-done | bytes 278560 | tf_op jit(solution)/shard_map/ppermute | solution.py:419
  6.0 0.1 multiply_add_fusion.1
  6.1 0.0 copy-start.1
  6.1 0.0 copy-start.2
  6.1 0.0 copy-start.3
  6.1 0.0 copy-start
  6.2 3.0 %collective-permute-start.1 = (f32[1,136,128]{2,1,0:T(8,128)S(1)}, f32[1,136,128]{2,1,0:T(8,128)S(1)}, u32[]{:S(2)}, u32[]{:S(2)}) collective-permute-start(f32[1,136,128]{2,1,0:T(8,128)S(1)} %get-tuple-element.25), channel_id=1, source_target_pairs={{0,2},{1,3},{2,0},{3,1},{4,6},{5,7},{6,4},{7,5},{8,10},{9,11},{10,... | collective-permute-start | bytes 208904 | tf_op jit(solution)/shard_map/ppermute | solution.py:419
  9.1 2.6 %collective-permute-start.3 = (f32[1,136,128]{2,1,0:T(8,128)S(1)}, f32[1,136,128]{2,1,0:T(8,128)S(1)}, u32[]{:S(2)}, u32[]{:S(2)}) collective-permute-start(f32[1,136,128]{2,1,0:T(8,128)S(1)} %get-tuple-element.26), channel_id=1, source_target_pairs={{0,4},{1,5},{2,6},{3,7},{4,0},{5,1},{6,2},{7,3},{8,12},{9,13},{10,... | collective-permute-start | bytes 208904 | tf_op jit(solution)/shard_map/ppermute | solution.py:419
  11.7 0.0 collective-permute-start.2
  11.7 0.0 collective-permute-done.1
  11.7 5.2 %collective-permute-done.3 = f32[1,136,128]{2,1,0:T(8,128)S(1)} collective-permute-done((f32[1,136,128]{2,1,0:T(8,128)S(1)}, f32[1,136,128]{2,1,0:T(8,128)S(1)}, u32[]{:S(2)}, u32[]{:S(2)}) %collective-permute-start.3) | collective-permute-done | bytes 69664 | tf_op jit(solution)/shard_map/ppermute | solution.py:419
  16.9 1.0 %collective-permute-done.2 = f32[1,136,128]{2,1,0:T(8,128)S(1)} collective-permute-done((f32[1,136,128]{2,1,0:T(8,128)S(1)}, f32[1,136,128]{2,1,0:T(8,128)S(1)}, u32[]{:S(2)}, u32[]{:S(2)}) %collective-permute-start.2) | collective-permute-done | bytes 69664 | tf_op jit(solution)/shard_map/ppermute | solution.py:419
  18.1 1.6 %collective-permute-start.4 = (f32[1,136,128]{2,1,0:T(8,128)S(1)}, f32[1,136,128]{2,1,0:T(8,128)S(1)}, u32[]{:S(2)}, u32[]{:S(2)}) collective-permute-start(f32[1,136,128]{2,1,0:T(8,128)S(1)} %get-tuple-element.13), channel_id=1, source_target_pairs={{0,8},{1,9},{2,10},{3,11},{4,12},{5,13},{6,14},{7,15},{8,0},{9,1},... | collective-permute-start | bytes 208904 | tf_op jit(solution)/shard_map/ppermute | solution.py:419
  19.6 2.8 %collective-permute-done.4 = f32[1,136,128]{2,1,0:T(8,128)S(1)} collective-permute-done((f32[1,136,128]{2,1,0:T(8,128)S(1)}, f32[1,136,128]{2,1,0:T(8,128)S(1)}, u32[]{:S(2)}, u32[]{:S(2)}) %collective-permute-start.4) | collective-permute-done | bytes 69664 | tf_op jit(solution)/shard_map/ppermute | solution.py:419
  22.5 1.6 %collective-permute-start.5 = (f32[1,136,128]{2,1,0:T(8,128)S(1)}, f32[1,136,128]{2,1,0:T(8,128)S(1)}, u32[]{:S(2)}, u32[]{:S(2)}) collective-permute-start(f32[1,136,128]{2,1,0:T(8,128)S(1)} %get-tuple-element.28), channel_id=1, source_target_pairs={{0,16},{1,17},{2,18},{3,19},{4,20},{5,21},{6,22},{7,23},{8,24},{9,... | collective-permute-start | bytes 208904 | tf_op jit(solution)/shard_map/ppermute | solution.py:419
  24.1 2.8 %collective-permute-done.5 = f32[1,136,128]{2,1,0:T(8,128)S(1)} collective-permute-done((f32[1,136,128]{2,1,0:T(8,128)S(1)}, f32[1,136,128]{2,1,0:T(8,128)S(1)}, u32[]{:S(2)}, u32[]{:S(2)}) %collective-permute-start.5) | collective-permute-done | bytes 69664 | tf_op jit(solution)/shard_map/ppermute | solution.py:419
  27.0 1.2 %collective-permute-start.6 = (f32[1,136,128]{2,1,0:T(8,128)S(1)}, f32[1,136,128]{2,1,0:T(8,128)S(1)}, u32[]{:S(2)}, u32[]{:S(2)}) collective-permute-start(f32[1,136,128]{2,1,0:T(8,128)S(1)} %get-tuple-element.22), channel_id=1, source_target_pairs={{0,2},{1,3},{2,0},{3,1},{4,6},{5,7},{6,4},{7,5},{8,10},{9,11},{10,... | collective-permute-start | bytes 208904 | tf_op jit(solution)/shard_map/ppermute | solution.py:419
  28.2 1.7 %collective-permute-start.7 = (f32[1,136,128]{2,1,0:T(8,128)S(1)}, f32[1,136,128]{2,1,0:T(8,128)S(1)}, u32[]{:S(2)}, u32[]{:S(2)}) collective-permute-start(f32[1,136,128]{2,1,0:T(8,128)S(1)} %get-tuple-element.23), channel_id=1, source_target_pairs={{0,4},{1,5},{2,6},{3,7},{4,0},{5,1},{6,2},{7,3},{8,12},{9,13},{10,... | collective-permute-start | bytes 208904 | tf_op jit(solution)/shard_map/ppermute | solution.py:419
  29.8 1.6 %collective-permute-start.8 = (f32[1,136,128]{2,1,0:T(8,128)S(1)}, f32[1,136,128]{2,1,0:T(8,128)S(1)}, u32[]{:S(2)}, u32[]{:S(2)}) collective-permute-start(f32[1,136,128]{2,1,0:T(8,128)S(1)} %get-tuple-element.24), channel_id=1, source_target_pairs={{0,6},{1,7},{2,4},{3,5},{4,2},{5,3},{6,0},{7,1},{8,14},{9,15},{10,... | collective-permute-start | bytes 208904 | tf_op jit(solution)/shard_map/ppermute | solution.py:419
  31.4 0.0 collective-permute-done.6
  31.4 2.7 %collective-permute-done.7 = f32[1,136,128]{2,1,0:T(8,128)S(1)} collective-permute-done((f32[1,136,128]{2,1,0:T(8,128)S(1)}, f32[1,136,128]{2,1,0:T(8,128)S(1)}, u32[]{:S(2)}, u32[]{:S(2)}) %collective-permute-start.7) | collective-permute-done | bytes 69664 | tf_op jit(solution)/shard_map/ppermute | solution.py:419
  34.1 1.8 %collective-permute-done.8 = f32[1,136,128]{2,1,0:T(8,128)S(1)} collective-permute-done((f32[1,136,128]{2,1,0:T(8,128)S(1)}, f32[1,136,128]{2,1,0:T(8,128)S(1)}, u32[]{:S(2)}, u32[]{:S(2)}) %collective-permute-start.8) | collective-permute-done | bytes 69664 | tf_op jit(solution)/shard_map/ppermute | solution.py:419
  35.9 0.1 fusion.1
  36.0 0.1 collective-permute-start.9
  36.1 0.0 copy-done.1
  36.1 0.0 copy-done.2
  36.1 0.0 copy-done.3
  36.1 7.1 %stats.1 = (f32[4096,128]{1,0:T(8,128)S(1)}, f32[32,128]{1,0:T(8,128)S(1)}, s32[32,128]{1,0:T(8,128)S(1)}) custom-call(s32[32,128]{1,0:T(8,128)S(1)} %bitcast.19, s32[32,128]{1,0:T(8,128)S(1)} %bitcast.21, s32[32,128]{1,0:T(8,128)S(1)} %bitcast.23), custom_call_target="tpu_custom_call" | custom-call | tf_op jit(solution)/shard_map/stats/pallas_call | solution.py:348
  43.2 0.0 copy-done
  43.2 0.6 %parts.1.parts_ref = bf16[272,4096]{1,0:T(8,128)(2,1)S(1)} custom-call(f32[4096,128]{1,0:T(8,128)S(1)} %copy-done), custom_call_target="tpu_custom_call" | custom-call | tf_op jit(solution)/shard_map/parts/pallas_call | solution.py:336
  43.8 2.5 %local.5.refs_2_ = f32[136,1024]{1,0:T(8,128)S(1)} custom-call(bf16[272,4096]{1,0:T(8,128)(2,1)S(1)} %parts.1.parts_ref, f32[4096,128]{1,0:T(8,128)S(1)} %get-tuple-element.9.column_ref, f32[32,128]{1,0:T(8,128)S(1)} %get-tuple-element.10.sid_ref), custom_call_target="tpu_custom_call" | custom-call | tf_op jit(solution)/shard_map/local/pallas_call | solution.py:365
  46.3 1.9 %local.4.refs_1_ = f32[136,1024]{1,0:T(8,128)S(1)} custom-call(bf16[272,4096]{1,0:T(8,128)(2,1)S(1)} %parts.1.parts_ref, f32[4096,128]{1,0:T(8,128)S(1)} %get-tuple-element.9.column_ref, f32[32,128]{1,0:T(8,128)S(1)} %get-tuple-element.10.sid_ref), custom_call_target="tpu_custom_call" | custom-call | tf_op jit(solution)/shard_map/local/pallas_call | solution.py:365
  48.2 2.1 %local.3.refs_0_ = f32[136,2048]{1,0:T(8,128)S(1)} custom-call(bf16[272,4096]{1,0:T(8,128)(2,1)S(1)} %parts.1.parts_ref, f32[4096,128]{1,0:T(8,128)S(1)} %get-tuple-element.9.column_ref, f32[32,128]{1,0:T(8,128)S(1)} %get-tuple-element.10.sid_ref), custom_call_target="tpu_custom_call" | custom-call | tf_op jit(solution)/shard_map/local/pallas_call | solution.py:365
  50.3 0.0 collective-permute-done.9
  50.4 3.6 %final.1 = f32[4096,128]{1,0:T(8,128)} custom-call(s32[1]{0:T(128)} %bitcast.flip_ref, s32[32,128]{1,0:T(8,128)S(1)} %get-tuple-element.8.key_ref, f32[8,136,128]{2,1,0:T(8,128)S(1)} %pad_maximum_fusion.state_ref, f32[136,2048]{1,0:T(8,128)S(1)} %local.3.refs_0_, f32[136,1024]{1,0:T(8,128)S(1)} %local.4.refs_1_, f32[136,1024]{1,0:T(8,128)S(1)} %local.5.refs_2_), custom_call_target="tpu_custom_call" | custom-call | tf_op jit(solution)/shard_map/final/pallas_call | solution.py:379
  (17 shorter events, 0.3 us)
Async XLA Ops:
  4.2 1.7 %collective-permute-start = (f32[4,136,128]{2,1,0:T(8,128)S(1)}, f32[4,136,128]{2,1,0:T(8,128)S(1)}, u32[]{:S(2)}, u32[]{:S(2)}) collective-permute-start(f32[4,136,128]{2,1,0:T(8,128)S(1)} %slice.58), channel_id=1, source_target_pairs={{0,1},{1,0},{2,3},{3,2},{4,5},{5,4},{6,7},{7,6},{8,9},{9,8},{10,11... | collective-permute-start | bytes 835592 | tf_op jit(solution)/shard_map/ppermute | solution.py:419
  6.1 30.0 %copy-start.1 = (s32[4096,1]{0,1:T(1,128)S(1)}, s32[4096,1]{0,1:T(1,128)}, u32[]{:S(2)}) copy-start(s32[4096,1]{0,1:T(1,128)} %param.5) | copy-start | bytes 49156
  6.1 30.0 %copy-start.2 = (s32[4096]{0:T(1024)S(1)}, s32[4096]{0:T(1024)}, u32[]{:S(2)}) copy-start(s32[4096]{0:T(1024)} %param.6) | copy-start | bytes 49156
  6.1 30.0 %copy-start.3 = (s32[4096]{0:T(1024)S(1)}, s32[4096]{0:T(1024)}, u32[]{:S(2)}) copy-start(s32[4096]{0:T(1024)} %param.7) | copy-start | bytes 49156
  6.1 37.1 %copy-start = (f32[4096,128]{1,0:T(8,128)S(1)}, f32[4096,128]{1,0:T(8,128)}, u32[]{:S(2)}) copy-start(f32[4096,128]{1,0:T(8,128)} %x_ref.1) | copy-start | bytes 6291460
  6.2 5.6 %collective-permute-start.1 = (f32[1,136,128]{2,1,0:T(8,128)S(1)}, f32[1,136,128]{2,1,0:T(8,128)S(1)}, u32[]{:S(2)}, u32[]{:S(2)}) collective-permute-start(f32[1,136,128]{2,1,0:T(8,128)S(1)} %get-tuple-element.25), channel_id=1, source_target_pairs={{0,2},{1,3},{2,0},{3,1},{4,6},{5,7},{6,4},{7,5},{8,10},{9,11},{10,... | collective-permute-start | bytes 208904 | tf_op jit(solution)/shard_map/ppermute | solution.py:419
  9.1 7.8 %collective-permute-start.3 = (f32[1,136,128]{2,1,0:T(8,128)S(1)}, f32[1,136,128]{2,1,0:T(8,128)S(1)}, u32[]{:S(2)}, u32[]{:S(2)}) collective-permute-start(f32[1,136,128]{2,1,0:T(8,128)S(1)} %get-tuple-element.26), channel_id=1, source_target_pairs={{0,4},{1,5},{2,6},{3,7},{4,0},{5,1},{6,2},{7,3},{8,12},{9,13},{10,... | collective-permute-start | bytes 208904 | tf_op jit(solution)/shard_map/ppermute | solution.py:419
  11.7 6.2 %collective-permute-start.2 = (f32[1,136,128]{2,1,0:T(8,128)S(1)}, f32[1,136,128]{2,1,0:T(8,128)S(1)}, u32[]{:S(2)}, u32[]{:S(2)}) collective-permute-start(f32[1,136,128]{2,1,0:T(8,128)S(1)} %get-tuple-element.27), channel_id=1, source_target_pairs={{0,6},{1,7},{2,4},{3,5},{4,2},{5,3},{6,0},{7,1},{8,14},{9,15},{10,... | collective-permute-start | bytes 208904 | tf_op jit(solution)/shard_map/ppermute | solution.py:419
  18.1 4.4 %collective-permute-start.4 = (f32[1,136,128]{2,1,0:T(8,128)S(1)}, f32[1,136,128]{2,1,0:T(8,128)S(1)}, u32[]{:S(2)}, u32[]{:S(2)}) collective-permute-start(f32[1,136,128]{2,1,0:T(8,128)S(1)} %get-tuple-element.13), channel_id=1, source_target_pairs={{0,8},{1,9},{2,10},{3,11},{4,12},{5,13},{6,14},{7,15},{8,0},{9,1},... | collective-permute-start | bytes 208904 | tf_op jit(solution)/shard_map/ppermute | solution.py:419
  22.5 4.4 %collective-permute-start.5 = (f32[1,136,128]{2,1,0:T(8,128)S(1)}, f32[1,136,128]{2,1,0:T(8,128)S(1)}, u32[]{:S(2)}, u32[]{:S(2)}) collective-permute-start(f32[1,136,128]{2,1,0:T(8,128)S(1)} %get-tuple-element.28), channel_id=1, source_target_pairs={{0,16},{1,17},{2,18},{3,19},{4,20},{5,21},{6,22},{7,23},{8,24},{9,... | collective-permute-start | bytes 208904 | tf_op jit(solution)/shard_map/ppermute | solution.py:419
  27.0 4.5 %collective-permute-start.6 = (f32[1,136,128]{2,1,0:T(8,128)S(1)}, f32[1,136,128]{2,1,0:T(8,128)S(1)}, u32[]{:S(2)}, u32[]{:S(2)}) collective-permute-start(f32[1,136,128]{2,1,0:T(8,128)S(1)} %get-tuple-element.22), channel_id=1, source_target_pairs={{0,2},{1,3},{2,0},{3,1},{4,6},{5,7},{6,4},{7,5},{8,10},{9,11},{10,... | collective-permute-start | bytes 208904 | tf_op jit(solution)/shard_map/ppermute | solution.py:419
  28.2 6.0 %collective-permute-start.7 = (f32[1,136,128]{2,1,0:T(8,128)S(1)}, f32[1,136,128]{2,1,0:T(8,128)S(1)}, u32[]{:S(2)}, u32[]{:S(2)}) collective-permute-start(f32[1,136,128]{2,1,0:T(8,128)S(1)} %get-tuple-element.23), channel_id=1, source_target_pairs={{0,4},{1,5},{2,6},{3,7},{4,0},{5,1},{6,2},{7,3},{8,12},{9,13},{10,... | collective-permute-start | bytes 208904 | tf_op jit(solution)/shard_map/ppermute | solution.py:419
  29.8 6.1 %collective-permute-start.8 = (f32[1,136,128]{2,1,0:T(8,128)S(1)}, f32[1,136,128]{2,1,0:T(8,128)S(1)}, u32[]{:S(2)}, u32[]{:S(2)}) collective-permute-start(f32[1,136,128]{2,1,0:T(8,128)S(1)} %get-tuple-element.24), channel_id=1, source_target_pairs={{0,6},{1,7},{2,4},{3,5},{4,2},{5,3},{6,0},{7,1},{8,14},{9,15},{10,... | collective-permute-start | bytes 208904 | tf_op jit(solution)/shard_map/ppermute | solution.py:419
  36.0 14.3 %collective-permute-start.9 = (f32[4,136,128]{2,1,0:T(8,128)S(1)}, f32[4,136,128]{2,1,0:T(8,128)S(1)}, u32[]{:S(2)}, u32[]{:S(2)}) collective-permute-start(f32[4,136,128]{2,1,0:T(8,128)S(1)} %get-tuple-element.18), channel_id=1, source_target_pairs={{0,1},{1,0},{2,3},{3,2},{4,5},{5,4},{6,7},{7,6},{8,9},{9,8},{10,11... | collective-permute-start | bytes 835592 | tf_op jit(solution)/shard_map/ppermute | solution.py:419

commit v3 on v2

--- a/solution.py
+++ b/solution.py
@@ -12,7 +12,7 @@
 LANES = 128
 EXTRA = 8
 LEVELS = (1, 2)
-STARTS = (0, 4, 6)
+STARTS = (0, 3, 5, 7)
 AXES = ("tm", "users")
 F32, BF16, I32 = jnp.float32, jnp.bfloat16, jnp.int32
 
@@ -41,7 +41,8 @@
     account_hbm,
     flag_hbm,
     x_hbm,
-    out_ref,
+    kept_ref,
+    sent_ref,
     home_ref,
     account_ref,
     flag_ref,
@@ -59,59 +60,61 @@
     copies = [pltpu.make_async_copy(a, b, sems.at[i]) for i, (a, b) in enumerate(pairs)]
     for copy in copies:
         copy.start()
-    tiles = home_ref.shape[0]
-    owners, rows = out_ref.shape[0], out_ref.shape[1]
+    for copy in copies[:3]:
+        copy.wait()
+    home, account, flag = home_ref[...], account_ref[...], flag_ref[...]
+    flip = flip_ref[0]
+    tiles = home.shape[0]
+    half, rows = kept_ref.shape[0], kept_ref.shape[1]
+    slots = 2 * half
     events, features = x_ref.shape
     chunk = min(512, events)
-    group = 2 if owners % 2 == 0 else 1
-    flip = flip_ref[0]
+    group = 2 if half % 2 == 0 else 1
     ids = account_ids()
     lane = lax.broadcasted_iota(I32, (ACCOUNTS, LANES), 1).astype(F32)
-    for copy in copies[:3]:
-        copy.wait()
-    home = home_ref[...]
-    account = account_ref[...]
-    flag = flag_ref[...]
     account_f = account.astype(F32)
 
-    def find_last(owner, carry):
-        kept = jnp.where((home == owner) & (flag == 1), account_f, -1.0).astype(BF16)
+    def owner_of(slot):
+        return jnp.bitwise_xor(slot, flip)
+
+    def find_last(slot, carry):
+        kept = jnp.where((home == owner_of(slot)) & (flag == 1), account_f, -1.0).astype(BF16)
         latest = jnp.full((ACCOUNTS, LANES), -1.0, BF16)
         for tile in range(tiles):
             latest = jnp.where(kept[tile : tile + 1] == ids, small(tile), latest)
         latest = latest.astype(F32)
         place = jnp.where(latest >= 0.0, latest * LANES + lane, -1.0)
-        last_ref[pl.ds(owner, 1), :] = jnp.max(place.T, axis=0, keepdims=True)
+        last_ref[pl.ds(slot, 1), :] = jnp.max(place.T, axis=0, keepdims=True)
         return carry
 
-    lax.fori_loop(0, owners, find_last, 0, unroll=min(owners, 8))
-
-    def look_up(owner, least):
-        row = jnp.broadcast_to(last_ref[pl.ds(owner, 1), :], (tiles, LANES))
-        return jnp.where(home == owner, jnp.take_along_axis(row, account, axis=1), least)
+    lax.fori_loop(0, slots, find_last, 0, unroll=min(slots, 8))
+
+    def look_up(slot, least):
+        row = jnp.broadcast_to(last_ref[pl.ds(slot, 1), :], (tiles, LANES))
+        found = jnp.take_along_axis(row, account, axis=1)
+        return jnp.where(home == owner_of(slot), found, least)
 
     least = jnp.full((tiles, LANES), -1.0, F32)
-    least = lax.fori_loop(0, owners, look_up, least, unroll=min(owners, 8))
+    least = lax.fori_loop(0, slots, look_up, least, unroll=min(slots, 8))
     live = row_positions(tiles).astype(F32) >= least
     weight = jnp.where(flag == 1, 65.0, 1.0).astype(BF16)
-
     copies[3].wait()
     high, low = split_two(x_ref[...])
     parts_ref[:, 0:features] = high
     parts_ref[:, features : 2 * features] = low
 
-    def one_group(number, carry):
+    def one_group(number, out_ref, base):
         kept = [
-            jnp.where(live & (home == number * group + i), account_f, -1.0).astype(BF16)
+            jnp.where(live & (home == owner_of(base + number * group + i)), account_f, -1.0).astype(BF16)
             for i in range(group)
         ]
         total = jnp.zeros((group * ACCOUNTS, 2 * features), F32)
         counts = [jnp.zeros((ACCOUNTS, LANES), BF16) for _ in range(group)]
-        for first in range(0, events, chunk):
+        for begin in range(0, events, chunk):
             blocks = []
             for i in range(group):
                 pieces = []
-                for tile in range(first // LANES, (first + chunk) // LANES):
+                for tile in range(begin // LANES, (begin + chunk) // LANES):
                     mask = kept[i][tile : tile + 1] == ids
                     share = jnp.broadcast_to(weight[tile : tile + 1], mask.shape)
                     counts[i] = counts[i] + jnp.where(mask, share, small(0.0))
@@ -119,12 +122,12 @@
                 blocks.append(jnp.concatenate(pieces, axis=1))
             total = total + jnp.dot(
                 jnp.concatenate(blocks, axis=0),
-                parts_ref[first : first + chunk, :],
+                parts_ref[begin : begin + chunk, :],
                 preferred_element_type=F32,
             )
         sums = total[:, 0:features] + total[:, features : 2 * features]
         for i in range(group):
-            place = jnp.bitwise_xor(number * group + i, flip)
+            place = number * group + i
             out_ref[place, 0:features, :] = sums[i * ACCOUNTS : (i + 1) * ACCOUNTS].T
             count = counts[i].astype(F32)
             count = jnp.where(count >= 64.0, count + (8192.0 - 64.0), count)
@@ -134,9 +137,13 @@
             out_ref[place, features:rows, :] = jnp.where(
                 spot == 0, tally - 8192.0 * marked, jnp.where(spot == 1, marked, 0.0)
             )
+
+    def both(number, carry):
+        one_group(number, sent_ref, half)
+        one_group(number, kept_ref, 0)
         return carry
 
-    lax.fori_loop(0, owners // group, one_group, 0, unroll=min(owners // group, 4))
+    lax.fori_loop(0, half // group, both, 0, unroll=min(half // group, 2))
 
 
 def turn(row):
@@ -167,25 +174,28 @@
     for tile in range(tiles):
         column_ref[tile * LANES : (tile + 1) * LANES, :] = turn(flagged[tile : tile + 1])
 
-    wide = 4 if tiles % 4 == 0 else 1
+    wide = 2 if tiles % 2 == 0 else 1
     for first in range(0, tiles, wide):
         mine = [user_f[first + i : first + i + 1] for i in range(wide)]
 
-        def earlier(other, latest):
-            column = column_ref[pl.ds(pl.multiple_of(other * LANES, LANES), LANES), :]
-            place = spot + (other * LANES).astype(F32)
-            return tuple(jnp.where(column == mine[i], place, latest[i]) for i in range(wide))
+        def earlier(step, latest):
+            for other in [step * wide + i for i in range(wide)]:
+                column = column_ref[pl.ds(pl.multiple_of(other * LANES, LANES), LANES), :]
+                place = other.astype(F32)
+                latest = tuple(jnp.where(column == mine[i], place, latest[i]) for i in range(wide))
+            return latest
 
         latest = tuple(jnp.full((LANES, LANES), -1.0, F32) for _ in range(wide))
-        latest = list(lax.fori_loop(0, first, earlier, latest))
+        latest = list(lax.fori_loop(0, first // wide, earlier, latest))
         for i in range(wide):
             for other in range(first, first + i + 1):
                 column = column_ref[other * LANES : (other + 1) * LANES, :]
                 mask = column == mine[i]
                 if other == first + i:
                     mask = mask & reaches
-                latest[i] = jnp.where(mask, spot + float(other * LANES), latest[i])
-            start_ref[first + i : first + i + 1, :] = jnp.max(latest[i], axis=0, keepdims=True)
+                latest[i] = jnp.where(mask, float(other), latest[i])
+            place = jnp.where(latest[i] < 0.0, -1.0, latest[i] * LANES + spot)
+            start_ref[first + i : first + i + 1, :] = jnp.max(place, axis=0, keepdims=True)
     start = start_ref[...]
     key_ref[...] = jnp.where(start < 0.0, user, -1)
     sid = jnp.where(start < 0.0, user_f + float(events), start)
@@ -224,23 +234,19 @@
         out_ref[features:, span] = total[2 * features : 2 * features + EXTRA]
 
 
-def final_kernel(flip_ref, key_ref, state_ref, *refs, starts, chunk):
-    local_refs, out_ref, table_ref = refs[: len(starts)], refs[-4], refs[-3]
-    stage_ref, sems = refs[-2], refs[-1]
-    owners = state_ref.shape[0]
-    events, features = out_ref.shape
-    rows = table_ref.shape[0]
-    flip = flip_ref[0]
-    group = min(8, owners)
+def gather_states(flip, first, key, state_ref, table_ref, chunk, finish):
+    slots = state_ref.shape[0]
+    events = key.shape[0] * LANES
+    rows, features = table_ref.shape[0], state_ref.shape[1] - EXTRA
+    group = min(8, slots)
     ids = account_ids()
 
-    def fill(owner, carry):
-        place = jnp.bitwise_xor(owner, flip)
-        high, low = split_two(state_ref[place, 0:features, :])
-        span = pl.ds(pl.multiple_of(owner * ACCOUNTS, ACCOUNTS), ACCOUNTS)
+    def fill(slot, carry):
+        high, low = split_two(state_ref[slot, 0:features, :])
+        span = pl.ds(pl.multiple_of(slot * ACCOUNTS, ACCOUNTS), ACCOUNTS)
         table_ref[0:features, span] = high
         table_ref[features : 2 * features, span] = low
-        count = state_ref[place, features : features + 1, :].astype(I32)
+        count = state_ref[slot, features : features + 1, :].astype(I32)
         digit = lax.broadcasted_iota(I32, (rows - 2 * features, LANES), 0)
         extra = jnp.where(
             digit == 0,
@@ -254,22 +260,17 @@
         table_ref[2 * features : rows, span] = extra.astype(F32).astype(BF16)
         return carry
 
-    lax.fori_loop(0, owners, fill, 0, unroll=min(owners, 8))
-
-    key = key_ref[...]
+    lax.fori_loop(0, slots, fill, 0, unroll=min(slots, 8))
     account_f = (key & (ACCOUNTS - 1)).astype(F32)
     home = lax.shift_right_arithmetic(key, ACCOUNTS.bit_length() - 1)
-    copies = []
+
     for begin in range(0, events, chunk):
-        number = begin // chunk
-        piece = max(i for i in range(len(starts)) if starts[i] <= begin)
-        local_ref = local_refs[piece]
-        span = slice(begin - starts[piece], begin - starts[piece] + chunk)
 
         def part(step, total):
             lines = []
             for i in range(group):
-                mine = jnp.where(home == step * group + i, account_f, -1.0).astype(BF16)
+                owner = jnp.bitwise_xor(first + step * group + i, flip)
+                mine = jnp.where(home == owner, account_f, -1.0).astype(BF16)
                 blocks = [
                     jnp.where(mine[tile : tile + 1] == ids, small(1.0), small(0.0))
                     for tile in range(begin // LANES, (begin + chunk) // LANES)
@@ -281,23 +282,50 @@
             )
             return found if total is None else total + found
 
-        if owners == group:
+        if slots == group:
             total = part(0, None)
         else:
-            total = lax.fori_loop(0, owners // group, part, jnp.zeros((rows, chunk), F32))
+            total = lax.fori_loop(0, slots // group, part, jnp.zeros((rows, chunk), F32))
         more = total[2 * features : 2 * features + 3]
-        count = local_ref[features : features + 1, span] + (
-            more[0:1] * 65536.0 + more[1:2] * 256.0 + more[2:3]
+        count = more[0:1] * 65536.0 + more[1:2] * 256.0 + more[2:3]
+        finish(begin, total[0:features] + total[features : 2 * features], count)
+
+
+def gather_kernel(flip_ref, key_ref, state_ref, *refs, starts, chunk, first):
+    local_refs, out_ref, table_ref = refs[: len(starts)], refs[-2], refs[-1]
+    features = state_ref.shape[1] - EXTRA
+
+    def finish(begin, sums, count):
+        piece = max(i for i in range(len(starts)) if starts[i] <= begin)
+        local_ref = local_refs[piece]
+        span = slice(begin - starts[piece], begin - starts[piece] + chunk)
+        out_ref[0:features, begin : begin + chunk] = local_ref[0:features, span] + sums
+        out_ref[features : features + 1, begin : begin + chunk] = (
+            local_ref[features : features + 1, span] + count
         )
-        sums = local_ref[0:features, span] + (total[0:features] + total[features : 2 * features])
-        stage_ref[begin : begin + chunk, :] = (sums * (1.0 / count)).T
+
+    gather_states(flip_ref[0], first, key_ref[...], state_ref, table_ref, chunk, finish)
+
+
+def final_kernel(
+    flip_ref, key_ref, state_ref, sums_ref, out_ref, table_ref, stage_ref, sems, *, chunk, first
+):
+    features = state_ref.shape[1] - EXTRA
+    copies = []
+
+    def finish(begin, sums, count):
+        span = slice(begin, begin + chunk)
+        sums = sums_ref[0:features, span] + sums
+        count = sums_ref[features : features + 1, span] + count
+        stage_ref[span, :] = (sums * (1.0 / count)).T
+        rows = pl.ds(begin, chunk)
         copy = pltpu.make_async_copy(
-            stage_ref.at[pl.ds(begin, chunk), :],
-            out_ref.at[pl.ds(begin, chunk), :],
-            sems.at[number],
+            stage_ref.at[rows, :], out_ref.at[rows, :], sems.at[begin // chunk]
         )
         copy.start()
         copies.append(copy)
+
+    gather_states(flip_ref[0], first, key_ref[...], state_ref, table_ref, chunk, finish)
     for copy in copies:
         copy.wait()
 
@@ -314,11 +342,12 @@
     home, account, flags, features = [
         pltpu.with_memory_space_constraint(v, pltpu.HBM) for v in (home, account, flags, features)
     ]
+    shape = jax.ShapeDtypeStruct((owners // 2, width + EXTRA, LANES), F32)
     return pl.pallas_call(
         closing_kernel,
-        out_shape=jax.ShapeDtypeStruct((owners, width + EXTRA, LANES), F32),
+        out_shape=(shape, shape),
         in_specs=[SMEM, HBM, HBM, HBM, HBM],
-        out_specs=VMEM,
+        out_specs=(VMEM, VMEM),
         scratch_shapes=[pltpu.VMEM((tiles, LANES), I32)] * 3
         + [
             pltpu.VMEM((events, width), F32),
@@ -373,22 +402,34 @@
     )(parts, column, sid)
 
 
-def final_means(flip, key, state, pieces, starts, events, width):
+def first_gather(flip, key, state, pieces, starts, events, width):
     chunk = min(512, events)
-    owners = state.shape[0]
     return pl.pallas_call(
-        functools.partial(final_kernel, starts=starts, chunk=chunk),
+        functools.partial(gather_kernel, starts=starts, chunk=chunk, first=0),
+        out_shape=jax.ShapeDtypeStruct((width + EXTRA, events), F32),
+        in_specs=[SMEM, VMEM, VMEM] + [VMEM] * len(pieces),
+        out_specs=VMEM,
+        scratch_shapes=[pltpu.VMEM((2 * width + 16, state.shape[0] * ACCOUNTS), BF16)],
+        compiler_params=PARAMS,
+        name="gather",
+    )(flip, key, state, *pieces)
+
+
+def final_means(flip, key, state, sums, events, width, first):
+    chunk = min(512, events)
+    return pl.pallas_call(
+        functools.partial(final_kernel, chunk=chunk, first=first),
         out_shape=jax.ShapeDtypeStruct((events, width), F32),
-        in_specs=[SMEM, VMEM, VMEM] + [VMEM] * len(pieces),
+        in_specs=[SMEM, VMEM, VMEM, VMEM],
         out_specs=HBM,
         scratch_shapes=[
-            pltpu.VMEM((2 * width + 16, owners * ACCOUNTS), BF16),
+            pltpu.VMEM((2 * width + 16, state.shape[0] * ACCOUNTS), BF16),
             pltpu.VMEM((events, width), F32),
             pltpu.SemaphoreType.DMA((events // chunk,)),
         ],
         compiler_params=PARAMS,
         name="final",
-    )(flip, key, state, *pieces)
+    )(flip, key, state, sums)
 
 
 def combine(earlier, later, mark):
@@ -411,8 +452,9 @@
     return levels
 
 
-def scan_states(state, me, devices, width, levels):
+def scan_states(kept, sent, me, devices, width, levels):
     mark = width + 1
+    state = None
     steps = devices.bit_length() - 1
 
     def swap(value, mask):
@@ -423,10 +465,14 @@
 
     saved, done = [], 0
     for level in levels:
-        part = state.shape[0] >> level
-        got = [state[:part]]
+        if done == 0:
+            parts = [kept, sent]
+        else:
+            part = state.shape[0] >> level
+            parts = [state[i * part : (i + 1) * part] for i in range(1 << level)]
+        got = [parts[0]]
         for other in range(1, 1 << level):
-            piece = state[other * part : (other + 1) * part]
+            piece = parts[other]
             got.append(swap(piece, other << done))
         bits = [bit(done + i) for i in range(level)]
         ordered = pick(got, bits)
@@ -436,12 +482,20 @@
             state = combine(state, later, mark)
         done += level
     before = jnp.zeros_like(state)
-    for step in range(done, steps):
-        got = swap(state, 1 << step)
-        before = jnp.where(bit(step), combine(got, before, mark), before)
-        if step < steps - 1:
-            low, high = jnp.where(bit(step), got, state), jnp.where(bit(step), state, got)
-            state = combine(low, high, mark)
+    while done < steps:
+        level = min(2, steps - done)
+        got = [state]
+        for other in range(1, 1 << level):
+            got.append(swap(state, other << done))
+        bits = [bit(done + i) for i in range(level)]
+        ordered = pick(got, bits)
+        earlier = [jnp.zeros_like(state), ordered[0]]
+        for later in ordered[1:-1]:
+            earlier.append(combine(earlier[-1], later, mark))
+        before = combine(pick(earlier, bits)[0], before, mark)
+        done += level
+        if done < steps:
+            state = combine(earlier[-1], ordered[-1], mark)
     for done, bits, ordered in reversed(saved):
         prefixes = [before]
         for earlier in ordered[:-1]:
@@ -450,8 +504,9 @@
         got = [mine[0]]
         for other in range(1, len(mine)):
             got.append(swap(mine[other], other << done))
+        if done == 0:
+            return got
         before = jnp.concatenate(got, axis=0)
-    return before
 
 
 def flip_of(me, levels, owners):
@@ -474,7 +529,8 @@
     home2 = home.reshape(tiles, LANES)
     account2 = account.reshape(tiles, LANES)
     flags2 = flags.reshape(tiles, LANES)
-    state = closing_states(flip, home2, account2, flags2, features, owners)
+    half = owners // 2
+    kept, sent = closing_states(flip, home2, account2, flags2, features, owners)
     column, sid, key = event_stats(home2, account2, flags2)
     parts = feature_parts(features)
     starts = [events * i // 8 for i in STARTS]
@@ -482,8 +538,9 @@
     for i, first in enumerate(starts):
         length = (starts + [events])[i + 1] - first
         pieces.append(local_sums(parts, column, sid, first, length, width))
-    before = scan_states(state, me, devices, width, levels)
-    return final_means(flip, key, before, pieces, starts, events, width)
+    mine, theirs = scan_states(kept, sent, me, devices, width, levels)
+    sums = first_gather(flip, key, mine, pieces, starts, events, width)
+    return final_means(flip, key, theirs, sums, events, width, half)
 
 
 def solution(mesh):

time: 54.4 us -> 51.2 us (0.941)
  Pallas kernels: 22 us -> 20.2 us
  waiting for transfers between devices: 17.5 us -> 15.7 us
    pallas_call x1, Pallas kernels: 7.08 us -> 5.18 us  [event_stats(): pl.pallas_call(stats_kernel, out_shape=(jax.ShapeDtypeStruct((tiles * LAN...]
    ppermute x10 -> x11, waiting for transfers between devices: 17.5 us -> 15.7 us  [swap(): return lax.ppermute(value, AXES, [(i, i ^ mask) for i in range(devices)])]
    ppermute x10 -> x11, starting transfers between devices: 13.8 us -> 14.2 us  [swap(): return lax.ppermute(value, AXES, [(i, i ^ mask) for i in range(devices)])]
    pallas_call x2 -> x3, Pallas kernels: 7.81 us -> 8.01 us  [the longest x1 4.19 us: closing_states(): pl.pallas_call(closing_kernel, out_shape=(shape, shape), in_specs=[SMEM,...]
    pallas_call x3 -> x4, Pallas kernels: 6.46 us -> 6.45 us  [local_sums(): pl.pallas_call(functools.partial(local_kernel, first=first, chunk=chunk),...]
  transfers between devices with their start and end apart: 10 -> 11, of which waited for: 7 -> 9; matrix products, arithmetic and copies ran while one was open for 0% -> 0% of each run, Pallas kernels for 26% -> 27%
where the time goes in v3:
time: 51.2 us; the launch traced here: 51 us
  Pallas kernels  20.2 us (39%)
  waiting for transfers between devices  15.7 us (31%)
  starting transfers between devices  14.2 us (28%)
    ppermute x11, waiting for transfers between devices, swap(): return lax.ppermute(value, AXES, [(i, i ^ mask) for i in range(devices)])  15.7 us
    ppermute x11, starting transfers between devices, swap(): return lax.ppermute(value, AXES, [(i, i ^ mask) for i in range(devices)])  14.2 us
    pallas_call x4, Pallas kernels, local_sums(): pl.pallas_call(functools.partial(local_kernel, first=first, chunk=chunk),...  6.45 us
    pallas_call x1, Pallas kernels, event_stats(): pl.pallas_call(stats_kernel, out_shape=(jax.ShapeDtypeStruct((tiles * LAN...  5.18 us
    pallas_call x1, Pallas kernels, closing_states(): pl.pallas_call(closing_kernel, out_shape=(shape, shape), in_specs=[SMEM,...  4.19 us
    pallas_call x1, Pallas kernels, final_means(): pl.pallas_call(functools.partial(final_kernel, chunk=chunk, first=first),...  2.45 us
    pallas_call x1, Pallas kernels, first_gather(): pl.pallas_call(functools.partial(gather_kernel, starts=starts, chunk=chun...  1.37 us
  transfers between devices with their start and end apart: 11, of which 9 were waited for; matrix products, arithmetic and copies ran while one was open for 0% of the time, Pallas kernels for 27%

profile of v3, /device:TPU:0, one launch (start us, length us, event | category | flops | bytes accessed | tf_op | source)
XLA Modules:
  0.0 51.0 jit_solution(5386126160479586678)
XLA Ops:
  0.0 4.2 %closing.1 = (f32[4,136,128]{2,1,0:T(8,128)S(1)}, f32[4,136,128]{2,1,0:T(8,128)S(1)}) custom-call(s32[1]{0:T(128)} %bitcast.flip_ref, s32[32,128]{1,0:T(8,128)} %bitcast.18, s32[32,128]{1,0:T(8,128)} %bitcast.20, s32[32,128]{1,0:T(8,128)} %bitcast.22, f32[4096,128]{1,0:T(8,128)} %x_ref.1), custom_call_target="tpu_custom_call" | custom-call | tf_op jit(solution)/shard_map/closing/pallas_call | solution.py:346
  4.2 0.6 %collective-permute-start = (f32[4,136,128]{2,1,0:T(8,128)S(1)}, f32[4,136,128]{2,1,0:T(8,128)S(1)}, u32[]{:S(2)}, u32[]{:S(2)}) collective-permute-start(f32[4,136,128]{2,1,0:T(8,128)S(1)} %get-tuple-element.12), channel_id=1, source_target_pairs={{0,1},{1,0},{2,3},{3,2},{4,5},{5,4},{6,7},{7,6},{8,9},{9,8},{10,11... | collective-permute-start | bytes 835592 | tf_op jit(solution)/shard_map/ppermute | solution.py:461
  4.8 1.2 %collective-permute-done = f32[4,136,128]{2,1,0:T(8,128)S(1)} collective-permute-done((f32[4,136,128]{2,1,0:T(8,128)S(1)}, f32[4,136,128]{2,1,0:T(8,128)S(1)}, u32[]{:S(2)}, u32[]{:S(2)}) %collective-permute-start) | collective-permute-done | bytes 278560 | tf_op jit(solution)/shard_map/ppermute | solution.py:461
  6.0 0.1 multiply_add_fusion.1
  6.1 0.0 copy-start.1
  6.1 0.0 copy-start.2
  6.1 0.0 copy-start.3
  6.1 0.0 copy-start
  6.1 3.0 %collective-permute-start.1 = (f32[1,136,128]{2,1,0:T(8,128)S(1)}, f32[1,136,128]{2,1,0:T(8,128)S(1)}, u32[]{:S(2)}, u32[]{:S(2)}) collective-permute-start(f32[1,136,128]{2,1,0:T(8,128)S(1)} %get-tuple-element.31), channel_id=1, source_target_pairs={{0,2},{1,3},{2,0},{3,1},{4,6},{5,7},{6,4},{7,5},{8,10},{9,11},{10,... | collective-permute-start | bytes 208904 | tf_op jit(solution)/shard_map/ppermute | solution.py:461
  9.1 2.6 %collective-permute-start.3 = (f32[1,136,128]{2,1,0:T(8,128)S(1)}, f32[1,136,128]{2,1,0:T(8,128)S(1)}, u32[]{:S(2)}, u32[]{:S(2)}) collective-permute-start(f32[1,136,128]{2,1,0:T(8,128)S(1)} %get-tuple-element.32), channel_id=1, source_target_pairs={{0,4},{1,5},{2,6},{3,7},{4,0},{5,1},{6,2},{7,3},{8,12},{9,13},{10,... | collective-permute-start | bytes 208904 | tf_op jit(solution)/shard_map/ppermute | solution.py:461
  11.7 0.0 collective-permute-start.2
  11.7 0.0 collective-permute-done.1
  11.7 5.2 %collective-permute-done.3 = f32[1,136,128]{2,1,0:T(8,128)S(1)} collective-permute-done((f32[1,136,128]{2,1,0:T(8,128)S(1)}, f32[1,136,128]{2,1,0:T(8,128)S(1)}, u32[]{:S(2)}, u32[]{:S(2)}) %collective-permute-start.3) | collective-permute-done | bytes 69664 | tf_op jit(solution)/shard_map/ppermute | solution.py:461
  16.9 1.0 %collective-permute-done.2 = f32[1,136,128]{2,1,0:T(8,128)S(1)} collective-permute-done((f32[1,136,128]{2,1,0:T(8,128)S(1)}, f32[1,136,128]{2,1,0:T(8,128)S(1)}, u32[]{:S(2)}, u32[]{:S(2)}) %collective-permute-start.2) | collective-permute-done | bytes 69664 | tf_op jit(solution)/shard_map/ppermute | solution.py:461
  18.0 1.6 %collective-permute-start.6 = (f32[1,136,128]{2,1,0:T(8,128)S(1)}, f32[1,136,128]{2,1,0:T(8,128)S(1)}, u32[]{:S(2)}, u32[]{:S(2)}) collective-permute-start(f32[1,136,128]{2,1,0:T(8,128)S(1)} %get-tuple-element.17), channel_id=1, source_target_pairs={{0,16},{1,17},{2,18},{3,19},{4,20},{5,21},{6,22},{7,23},{8,24},{9,... | collective-permute-start | bytes 208904 | tf_op jit(solution)/shard_map/ppermute | solution.py:461
  19.6 1.4 %collective-permute-start.5 = (f32[1,136,128]{2,1,0:T(8,128)S(1)}, f32[1,136,128]{2,1,0:T(8,128)S(1)}, u32[]{:S(2)}, u32[]{:S(2)}) collective-permute-start(f32[1,136,128]{2,1,0:T(8,128)S(1)} %get-tuple-element.17), channel_id=1, source_target_pairs={{0,24},{1,25},{2,26},{3,27},{4,28},{5,29},{6,30},{7,31},{8,16},{9,... | collective-permute-start | bytes 208904 | tf_op jit(solution)/shard_map/ppermute | solution.py:461
  21.0 0.5 %collective-permute-start.4 = (f32[1,136,128]{2,1,0:T(8,128)S(1)}, f32[1,136,128]{2,1,0:T(8,128)S(1)}, u32[]{:S(2)}, u32[]{:S(2)}) collective-permute-start(f32[1,136,128]{2,1,0:T(8,128)S(1)} %get-tuple-element.17), channel_id=1, source_target_pairs={{0,8},{1,9},{2,10},{3,11},{4,12},{5,13},{6,14},{7,15},{8,0},{9,1},... | collective-permute-start | bytes 208904 | tf_op jit(solution)/shard_map/ppermute | solution.py:461
  21.6 1.1 %collective-permute-done.6 = f32[1,136,128]{2,1,0:T(8,128)S(1)} collective-permute-done((f32[1,136,128]{2,1,0:T(8,128)S(1)}, f32[1,136,128]{2,1,0:T(8,128)S(1)}, u32[]{:S(2)}, u32[]{:S(2)}) %collective-permute-start.6) | collective-permute-done | bytes 69664 | tf_op jit(solution)/shard_map/ppermute | solution.py:461
  22.6 2.2 %collective-permute-done.5 = f32[1,136,128]{2,1,0:T(8,128)S(1)} collective-permute-done((f32[1,136,128]{2,1,0:T(8,128)S(1)}, f32[1,136,128]{2,1,0:T(8,128)S(1)}, u32[]{:S(2)}, u32[]{:S(2)}) %collective-permute-start.5) | collective-permute-done | bytes 69664 | tf_op jit(solution)/shard_map/ppermute | solution.py:461
  24.8 0.5 %collective-permute-done.4 = f32[1,136,128]{2,1,0:T(8,128)S(1)} collective-permute-done((f32[1,136,128]{2,1,0:T(8,128)S(1)}, f32[1,136,128]{2,1,0:T(8,128)S(1)}, u32[]{:S(2)}, u32[]{:S(2)}) %collective-permute-start.4) | collective-permute-done | bytes 69664 | tf_op jit(solution)/shard_map/ppermute | solution.py:461
  25.4 0.1 broadcast_select_fusion.10
  25.5 1.2 %collective-permute-start.7 = (f32[1,136,128]{2,1,0:T(8,128)S(1)}, f32[1,136,128]{2,1,0:T(8,128)S(1)}, u32[]{:S(2)}, u32[]{:S(2)}) collective-permute-start(f32[1,136,128]{2,1,0:T(8,128)S(1)} %get-tuple-element.26), channel_id=1, source_target_pairs={{0,2},{1,3},{2,0},{3,1},{4,6},{5,7},{6,4},{7,5},{8,10},{9,11},{10,... | collective-permute-start | bytes 208904 | tf_op jit(solution)/shard_map/ppermute | solution.py:461
  26.7 1.7 %collective-permute-start.8 = (f32[1,136,128]{2,1,0:T(8,128)S(1)}, f32[1,136,128]{2,1,0:T(8,128)S(1)}, u32[]{:S(2)}, u32[]{:S(2)}) collective-permute-start(f32[1,136,128]{2,1,0:T(8,128)S(1)} %get-tuple-element.27), channel_id=1, source_target_pairs={{0,4},{1,5},{2,6},{3,7},{4,0},{5,1},{6,2},{7,3},{8,12},{9,13},{10,... | collective-permute-start | bytes 208904 | tf_op jit(solution)/shard_map/ppermute | solution.py:461
  28.4 1.6 %collective-permute-start.9 = (f32[1,136,128]{2,1,0:T(8,128)S(1)}, f32[1,136,128]{2,1,0:T(8,128)S(1)}, u32[]{:S(2)}, u32[]{:S(2)}) collective-permute-start(f32[1,136,128]{2,1,0:T(8,128)S(1)} %get-tuple-element.28), channel_id=1, source_target_pairs={{0,6},{1,7},{2,4},{3,5},{4,2},{5,3},{6,0},{7,1},{8,14},{9,15},{10,... | collective-permute-start | bytes 208904 | tf_op jit(solution)/shard_map/ppermute | solution.py:461
  30.0 0.7 %collective-permute-done.7 = f32[1,136,128]{2,1,0:T(8,128)S(1)} collective-permute-done((f32[1,136,128]{2,1,0:T(8,128)S(1)}, f32[1,136,128]{2,1,0:T(8,128)S(1)}, u32[]{:S(2)}, u32[]{:S(2)}) %collective-permute-start.7) | collective-permute-done | bytes 69664 | tf_op jit(solution)/shard_map/ppermute | solution.py:461
  30.6 2.0 %collective-permute-done.8 = f32[1,136,128]{2,1,0:T(8,128)S(1)} collective-permute-done((f32[1,136,128]{2,1,0:T(8,128)S(1)}, f32[1,136,128]{2,1,0:T(8,128)S(1)}, u32[]{:S(2)}, u32[]{:S(2)}) %collective-permute-start.8) | collective-permute-done | bytes 69664 | tf_op jit(solution)/shard_map/ppermute | solution.py:461
  32.7 1.8 %collective-permute-done.9 = f32[1,136,128]{2,1,0:T(8,128)S(1)} collective-permute-done((f32[1,136,128]{2,1,0:T(8,128)S(1)}, f32[1,136,128]{2,1,0:T(8,128)S(1)}, u32[]{:S(2)}, u32[]{:S(2)}) %collective-permute-start.9) | collective-permute-done | bytes 69664 | tf_op jit(solution)/shard_map/ppermute | solution.py:461
  34.5 0.1 fusion
  34.6 0.1 collective-permute-start.10
  34.6 0.0 copy-done.1
  34.7 0.0 copy-done.2
  34.7 0.0 copy-done.3
  34.7 5.2 %stats.1 = (f32[4096,128]{1,0:T(8,128)S(1)}, f32[32,128]{1,0:T(8,128)S(1)}, s32[32,128]{1,0:T(8,128)S(1)}) custom-call(s32[32,128]{1,0:T(8,128)S(1)} %bitcast.19, s32[32,128]{1,0:T(8,128)S(1)} %bitcast.21, s32[32,128]{1,0:T(8,128)S(1)} %bitcast.23), custom_call_target="tpu_custom_call" | custom-call | tf_op jit(solution)/shard_map/stats/pallas_call | solution.py:377
  39.9 0.0 copy-done
  39.9 0.6 %parts.1.parts_ref = bf16[272,4096]{1,0:T(8,128)(2,1)S(1)} custom-call(f32[4096,128]{1,0:T(8,128)S(1)} %copy-done), custom_call_target="tpu_custom_call" | custom-call | tf_op jit(solution)/shard_map/parts/pallas_call | solution.py:365
  40.5 1.4 %local.7.refs_3_ = f32[136,512]{1,0:T(8,128)S(1)} custom-call(bf16[272,4096]{1,0:T(8,128)(2,1)S(1)} %parts.1.parts_ref, f32[4096,128]{1,0:T(8,128)S(1)} %get-tuple-element.13.column_ref, f32[32,128]{1,0:T(8,128)S(1)} %get-tuple-element.14.sid_ref), custom_call_target="tpu_custom_call" | custom-call | tf_op jit(solution)/shard_map/local/pallas_call | solution.py:394
  41.9 2.2 %local.6.refs_2_ = f32[136,1024]{1,0:T(8,128)S(1)} custom-call(bf16[272,4096]{1,0:T(8,128)(2,1)S(1)} %parts.1.parts_ref, f32[4096,128]{1,0:T(8,128)S(1)} %get-tuple-element.13.column_ref, f32[32,128]{1,0:T(8,128)S(1)} %get-tuple-element.14.sid_ref), custom_call_target="tpu_custom_call" | custom-call | tf_op jit(solution)/shard_map/local/pallas_call | solution.py:394
  44.1 1.6 %local.5.refs_1_ = f32[136,1024]{1,0:T(8,128)S(1)} custom-call(bf16[272,4096]{1,0:T(8,128)(2,1)S(1)} %parts.1.parts_ref, f32[4096,128]{1,0:T(8,128)S(1)} %get-tuple-element.13.column_ref, f32[32,128]{1,0:T(8,128)S(1)} %get-tuple-element.14.sid_ref), custom_call_target="tpu_custom_call" | custom-call | tf_op jit(solution)/shard_map/local/pallas_call | solution.py:394
  45.7 1.3 %local.4.refs_0_ = f32[136,1536]{1,0:T(8,128)S(1)} custom-call(bf16[272,4096]{1,0:T(8,128)(2,1)S(1)} %parts.1.parts_ref, f32[4096,128]{1,0:T(8,128)S(1)} %get-tuple-element.13.column_ref, f32[32,128]{1,0:T(8,128)S(1)} %get-tuple-element.14.sid_ref), custom_call_target="tpu_custom_call" | custom-call | tf_op jit(solution)/shard_map/local/pallas_call | solution.py:394
  47.0 1.4 %gather.1.sums_ref = f32[136,4096]{1,0:T(8,128)S(1)} custom-call(s32[1]{0:T(128)} %bitcast.flip_ref, s32[32,128]{1,0:T(8,128)S(1)} %get-tuple-element.10.key_ref, f32[4,136,128]{2,1,0:T(8,128)S(1)} %get-tuple-element.21.state_ref, f32[136,1536]{1,0:T(8,128)S(1)} %local.4.refs_0_, f32[136,1024]{1,0:T(8,128)S(1)} %local.5.refs_1_, ...), custom_call_target="tpu_custom_call" | custom-call | tf_op jit(solution)/shard_map/gather/pallas_call | solution.py:407
  48.3 0.0 collective-permute-done.10.state_ref
  48.3 2.5 %final.1 = f32[4096,128]{1,0:T(8,128)} custom-call(s32[1]{0:T(128)} %bitcast.flip_ref, s32[32,128]{1,0:T(8,128)S(1)} %get-tuple-element.10.key_ref, f32[4,136,128]{2,1,0:T(8,128)S(1)} %collective-permute-done.10.state_ref, f32[136,4096]{1,0:T(8,128)S(1)} %gather.1.sums_ref), custom_call_target="tpu_custom_call" | custom-call | tf_op jit(solution)/shard_map/final/pallas_call | solution.py:420
  (13 shorter events, 0.2 us)
Async XLA Ops:
  4.2 1.7 %collective-permute-start = (f32[4,136,128]{2,1,0:T(8,128)S(1)}, f32[4,136,128]{2,1,0:T(8,128)S(1)}, u32[]{:S(2)}, u32[]{:S(2)}) collective-permute-start(f32[4,136,128]{2,1,0:T(8,128)S(1)} %get-tuple-element.12), channel_id=1, source_target_pairs={{0,1},{1,0},{2,3},{3,2},{4,5},{5,4},{6,7},{7,6},{8,9},{9,8},{10,11... | collective-permute-start | bytes 835592 | tf_op jit(solution)/shard_map/ppermute | solution.py:461
  6.1 28.6 %copy-start.1 = (s32[4096,1]{0,1:T(1,128)S(1)}, s32[4096,1]{0,1:T(1,128)}, u32[]{:S(2)}) copy-start(s32[4096,1]{0,1:T(1,128)} %param.5) | copy-start | bytes 49156
  6.1 28.6 %copy-start.2 = (s32[4096]{0:T(1024)S(1)}, s32[4096]{0:T(1024)}, u32[]{:S(2)}) copy-start(s32[4096]{0:T(1024)} %param.6) | copy-start | bytes 49156
  6.1 28.6 %copy-start.3 = (s32[4096]{0:T(1024)S(1)}, s32[4096]{0:T(1024)}, u32[]{:S(2)}) copy-start(s32[4096]{0:T(1024)} %param.7) | copy-start | bytes 49156
  6.1 33.8 %copy-start = (f32[4096,128]{1,0:T(8,128)S(1)}, f32[4096,128]{1,0:T(8,128)}, u32[]{:S(2)}) copy-start(f32[4096,128]{1,0:T(8,128)} %x_ref.1) | copy-start | bytes 6291460
  6.1 5.6 %collective-permute-start.1 = (f32[1,136,128]{2,1,0:T(8,128)S(1)}, f32[1,136,128]{2,1,0:T(8,128)S(1)}, u32[]{:S(2)}, u32[]{:S(2)}) collective-permute-start(f32[1,136,128]{2,1,0:T(8,128)S(1)} %get-tuple-element.31), channel_id=1, source_target_pairs={{0,2},{1,3},{2,0},{3,1},{4,6},{5,7},{6,4},{7,5},{8,10},{9,11},{10,... | collective-permute-start | bytes 208904 | tf_op jit(solution)/shard_map/ppermute | solution.py:461
  9.1 7.8 %collective-permute-start.3 = (f32[1,136,128]{2,1,0:T(8,128)S(1)}, f32[1,136,128]{2,1,0:T(8,128)S(1)}, u32[]{:S(2)}, u32[]{:S(2)}) collective-permute-start(f32[1,136,128]{2,1,0:T(8,128)S(1)} %get-tuple-element.32), channel_id=1, source_target_pairs={{0,4},{1,5},{2,6},{3,7},{4,0},{5,1},{6,2},{7,3},{8,12},{9,13},{10,... | collective-permute-start | bytes 208904 | tf_op jit(solution)/shard_map/ppermute | solution.py:461
  11.7 6.2 %collective-permute-start.2 = (f32[1,136,128]{2,1,0:T(8,128)S(1)}, f32[1,136,128]{2,1,0:T(8,128)S(1)}, u32[]{:S(2)}, u32[]{:S(2)}) collective-permute-start(f32[1,136,128]{2,1,0:T(8,128)S(1)} %get-tuple-element.33), channel_id=1, source_target_pairs={{0,6},{1,7},{2,4},{3,5},{4,2},{5,3},{6,0},{7,1},{8,14},{9,15},{10,... | collective-permute-start | bytes 208904 | tf_op jit(solution)/shard_map/ppermute | solution.py:461
  18.0 4.6 %collective-permute-start.6 = (f32[1,136,128]{2,1,0:T(8,128)S(1)}, f32[1,136,128]{2,1,0:T(8,128)S(1)}, u32[]{:S(2)}, u32[]{:S(2)}) collective-permute-start(f32[1,136,128]{2,1,0:T(8,128)S(1)} %get-tuple-element.17), channel_id=1, source_target_pairs={{0,16},{1,17},{2,18},{3,19},{4,20},{5,21},{6,22},{7,23},{8,24},{9,... | collective-permute-start | bytes 208904 | tf_op jit(solution)/shard_map/ppermute | solution.py:461
  19.6 5.2 %collective-permute-start.5 = (f32[1,136,128]{2,1,0:T(8,128)S(1)}, f32[1,136,128]{2,1,0:T(8,128)S(1)}, u32[]{:S(2)}, u32[]{:S(2)}) collective-permute-start(f32[1,136,128]{2,1,0:T(8,128)S(1)} %get-tuple-element.17), channel_id=1, source_target_pairs={{0,24},{1,25},{2,26},{3,27},{4,28},{5,29},{6,30},{7,31},{8,16},{9,... | collective-permute-start | bytes 208904 | tf_op jit(solution)/shard_map/ppermute | solution.py:461
  21.0 4.3 %collective-permute-start.4 = (f32[1,136,128]{2,1,0:T(8,128)S(1)}, f32[1,136,128]{2,1,0:T(8,128)S(1)}, u32[]{:S(2)}, u32[]{:S(2)}) collective-permute-start(f32[1,136,128]{2,1,0:T(8,128)S(1)} %get-tuple-element.17), channel_id=1, source_target_pairs={{0,8},{1,9},{2,10},{3,11},{4,12},{5,13},{6,14},{7,15},{8,0},{9,1},... | collective-permute-start | bytes 208904 | tf_op jit(solution)/shard_map/ppermute | solution.py:461
  25.5 5.1 %collective-permute-start.7 = (f32[1,136,128]{2,1,0:T(8,128)S(1)}, f32[1,136,128]{2,1,0:T(8,128)S(1)}, u32[]{:S(2)}, u32[]{:S(2)}) collective-permute-start(f32[1,136,128]{2,1,0:T(8,128)S(1)} %get-tuple-element.26), channel_id=1, source_target_pairs={{0,2},{1,3},{2,0},{3,1},{4,6},{5,7},{6,4},{7,5},{8,10},{9,11},{10,... | collective-permute-start | bytes 208904 | tf_op jit(solution)/shard_map/ppermute | solution.py:461
  26.7 6.0 %collective-permute-start.8 = (f32[1,136,128]{2,1,0:T(8,128)S(1)}, f32[1,136,128]{2,1,0:T(8,128)S(1)}, u32[]{:S(2)}, u32[]{:S(2)}) collective-permute-start(f32[1,136,128]{2,1,0:T(8,128)S(1)} %get-tuple-element.27), channel_id=1, source_target_pairs={{0,4},{1,5},{2,6},{3,7},{4,0},{5,1},{6,2},{7,3},{8,12},{9,13},{10,... | collective-permute-start | bytes 208904 | tf_op jit(solution)/shard_map/ppermute | solution.py:461
  28.4 6.1 %collective-permute-start.9 = (f32[1,136,128]{2,1,0:T(8,128)S(1)}, f32[1,136,128]{2,1,0:T(8,128)S(1)}, u32[]{:S(2)}, u32[]{:S(2)}) collective-permute-start(f32[1,136,128]{2,1,0:T(8,128)S(1)} %get-tuple-element.28), channel_id=1, source_target_pairs={{0,6},{1,7},{2,4},{3,5},{4,2},{5,3},{6,0},{7,1},{8,14},{9,15},{10,... | collective-permute-start | bytes 208904 | tf_op jit(solution)/shard_map/ppermute | solution.py:461
  34.6 13.8 %collective-permute-start.10 = (f32[4,136,128]{2,1,0:T(8,128)S(1)}, f32[4,136,128]{2,1,0:T(8,128)S(1)}, u32[]{:S(2)}, u32[]{:S(2)}) collective-permute-start(f32[4,136,128]{2,1,0:T(8,128)S(1)} %get-tuple-element.22), channel_id=1, source_target_pairs={{0,1},{1,0},{2,3},{3,2},{4,5},{5,4},{6,7},{7,6},{8,9},{9,8},{10,11... | collective-permute-start | bytes 835592 | tf_op jit(solution)/shard_map/ppermute | solution.py:461

commit v4 on v3

--- a/solution.py
+++ b/solution.py
@@ -162,40 +162,60 @@
     parts_ref[2 * features : rows, :] = jnp.where(extra == 0, 1.0, 0.0).astype(BF16)
 
 
-def stats_kernel(home_ref, account_ref, flag_ref, column_ref, sid_ref, key_ref, start_ref):
+def stats_kernel(
+    home_ref, account_ref, flag_ref, column_ref, sid_ref, key_ref, start_ref, *, owners
+):
     tiles = home_ref.shape[0]
     events = tiles * LANES
-    user = home_ref[...] * ACCOUNTS + account_ref[...]
+    per = 4 if tiles % 8 == 0 else tiles
+    home, account, flag = home_ref[...], account_ref[...], flag_ref[...]
+    account_f = account.astype(F32)
+    user = home * ACCOUNTS + account
     user_f = user.astype(F32)
-    flagged = jnp.where(flag_ref[...] == 1, user_f, -1.0)
+    flagged = jnp.where(flag == 1, user_f, -1.0)
     row_id = lax.broadcasted_iota(I32, (LANES, LANES), 0)
     reaches = row_id <= lax.broadcasted_iota(I32, (LANES, LANES), 1)
     spot = row_id.astype(F32)
-    for tile in range(tiles):
-        column_ref[tile * LANES : (tile + 1) * LANES, :] = turn(flagged[tile : tile + 1])
-
-    wide = 2 if tiles % 2 == 0 else 1
-    for first in range(0, tiles, wide):
-        mine = [user_f[first + i : first + i + 1] for i in range(wide)]
-
-        def earlier(step, latest):
-            for other in [step * wide + i for i in range(wide)]:
-                column = column_ref[pl.ds(pl.multiple_of(other * LANES, LANES), LANES), :]
-                place = other.astype(F32)
-                latest = tuple(jnp.where(column == mine[i], place, latest[i]) for i in range(wide))
-            return latest
-
-        latest = tuple(jnp.full((LANES, LANES), -1.0, F32) for _ in range(wide))
-        latest = list(lax.fori_loop(0, first // wide, earlier, latest))
-        for i in range(wide):
-            for other in range(first, first + i + 1):
-                column = column_ref[other * LANES : (other + 1) * LANES, :]
-                mask = column == mine[i]
-                if other == first + i:
+    lane = lax.broadcasted_iota(I32, (ACCOUNTS, LANES), 1).astype(F32)
+    ids = account_ids()
+    upper = lax.broadcasted_iota(I32, (8, LANES), 0) >= 4
+
+    def before_block(owner, least):
+        mine = home == owner
+        kept = jnp.where(mine & (flag == 1), account_f, -1.0).astype(BF16)
+        latest = jnp.full((ACCOUNTS, LANES), -1.0, BF16)
+        rows = [jnp.full((1, LANES), -1.0, F32)]
+        for tile in range(tiles - per):
+            latest = jnp.where(kept[tile : tile + 1] == ids, small(tile), latest)
+            if (tile + 1) % per == 0:
+                place = latest.astype(F32)
+                place = jnp.where(place >= 0.0, place * LANES + lane, -1.0)
+                rows.append(jnp.max(place.T, axis=0, keepdims=True))
+        if per == tiles:
+            wide = jnp.broadcast_to(rows[0], (tiles, LANES))
+        else:
+            wide = jnp.concatenate(
+                [jnp.where(upper, rows[i + 1], rows[i]) for i in range(0, len(rows), 2)], axis=0
+            )
+        return jnp.where(mine, jnp.take_along_axis(wide, account, axis=1), least)
+
+    base = jnp.full((tiles, LANES), -1.0, F32)
+    base = lax.fori_loop(0, owners, before_block, base, unroll=min(owners, 8))
+
+    for first in range(0, tiles, per):
+        columns = [turn(flagged[tile : tile + 1]) for tile in range(first, first + per)]
+        for tile in range(first, first + per):
+            line = user_f[tile : tile + 1]
+            latest = jnp.full((LANES, LANES), -1.0, F32)
+            for other in range(first, tile + 1):
+                mask = columns[other - first] == line
+                if other == tile:
                     mask = mask & reaches
-                latest[i] = jnp.where(mask, float(other), latest[i])
-            place = jnp.where(latest[i] < 0.0, -1.0, latest[i] * LANES + spot)
-            start_ref[first + i : first + i + 1, :] = jnp.max(place, axis=0, keepdims=True)
+                latest = jnp.where(mask, float(other), latest)
+            place = jnp.where(latest < 0.0, -1.0, latest * LANES + spot)
+            start_ref[tile : tile + 1, :] = jnp.maximum(
+                base[tile : tile + 1], jnp.max(place, axis=0, keepdims=True)
+            )
     start = start_ref[...]
     key_ref[...] = jnp.where(start < 0.0, user, -1)
     sid = jnp.where(start < 0.0, user_f + float(events), start)
@@ -372,10 +392,10 @@
     )(features)
 
 
-def event_stats(home, account, flags):
+def event_stats(home, account, flags, owners):
     tiles = home.shape[0]
     return pl.pallas_call(
-        stats_kernel,
+        functools.partial(stats_kernel, owners=owners),
         out_shape=(
             jax.ShapeDtypeStruct((tiles * LANES, LANES), F32),
             jax.ShapeDtypeStruct((tiles, LANES), F32),
@@ -531,7 +551,7 @@
     flags2 = flags.reshape(tiles, LANES)
     half = owners // 2
     kept, sent = closing_states(flip, home2, account2, flags2, features, owners)
-    column, sid, key = event_stats(home2, account2, flags2)
+    column, sid, key = event_stats(home2, account2, flags2, owners)
     parts = feature_parts(features)
     starts = [events * i // 8 for i in STARTS]
     pieces = []

time: 51.2 us -> 49 us (0.957)
  Pallas kernels: 20.2 us -> 18.1 us
    pallas_call x1, Pallas kernels: 5.18 us -> 2.81 us  [event_stats(): pl.pallas_call(functools.partial(stats_kernel, owners=owners), out_shape=...]
  transfers between devices with their start and end apart: 11 -> 11, of which waited for: 9 -> 9; matrix products, arithmetic and copies ran while one was open for 0% -> 0% of each run, Pallas kernels for 27% -> 23%
where the time goes in v4:
time: 49 us; the launch traced here: 48.8 us
  Pallas kernels  18.1 us (37%)
  waiting for transfers between devices  15.7 us (32%)
  starting transfers between devices  14.2 us (29%)
    ppermute x11, waiting for transfers between devices, swap(): return lax.ppermute(value, AXES, [(i, i ^ mask) for i in range(devices)])  15.7 us
    ppermute x11, starting transfers between devices, swap(): return lax.ppermute(value, AXES, [(i, i ^ mask) for i in range(devices)])  14.2 us
    pallas_call x4, Pallas kernels, local_sums(): pl.pallas_call(functools.partial(local_kernel, first=first, chunk=chunk),...  6.64 us
    pallas_call x1, Pallas kernels, closing_states(): pl.pallas_call(closing_kernel, out_shape=(shape, shape), in_specs=[SMEM,...  4.19 us
    pallas_call x1, Pallas kernels, event_stats(): pl.pallas_call(functools.partial(stats_kernel, owners=owners), out_shape=...  2.81 us
    pallas_call x1, Pallas kernels, final_means(): pl.pallas_call(functools.partial(final_kernel, chunk=chunk, first=first),...  2.46 us
    pallas_call x1, Pallas kernels, first_gather(): pl.pallas_call(functools.partial(gather_kernel, starts=starts, chunk=chun...  1.37 us
  transfers between devices with their start and end apart: 11, of which 9 were waited for; matrix products, arithmetic and copies ran while one was open for 0% of the time, Pallas kernels for 23%

profile of v4, /device:TPU:0, one launch (start us, length us, event | category | flops | bytes accessed | tf_op | source)
XLA Modules:
  0.0 48.8 jit_solution(8932221803568988557)
XLA Ops:
  0.0 4.2 %closing.1 = (f32[4,136,128]{2,1,0:T(8,128)S(1)}, f32[4,136,128]{2,1,0:T(8,128)S(1)}) custom-call(s32[1]{0:T(128)} %bitcast.flip_ref, s32[32,128]{1,0:T(8,128)} %bitcast.18, s32[32,128]{1,0:T(8,128)} %bitcast.20, s32[32,128]{1,0:T(8,128)} %bitcast.22, f32[4096,128]{1,0:T(8,128)} %x_ref.1), custom_call_target="tpu_custom_call" | custom-call | tf_op jit(solution)/shard_map/closing/pallas_call | solution.py:366
  4.2 0.6 %collective-permute-start = (f32[4,136,128]{2,1,0:T(8,128)S(1)}, f32[4,136,128]{2,1,0:T(8,128)S(1)}, u32[]{:S(2)}, u32[]{:S(2)}) collective-permute-start(f32[4,136,128]{2,1,0:T(8,128)S(1)} %get-tuple-element.12), channel_id=1, source_target_pairs={{0,1},{1,0},{2,3},{3,2},{4,5},{5,4},{6,7},{7,6},{8,9},{9,8},{10,11... | collective-permute-start | bytes 835592 | tf_op jit(solution)/shard_map/ppermute | solution.py:481
  4.8 1.2 %collective-permute-done = f32[4,136,128]{2,1,0:T(8,128)S(1)} collective-permute-done((f32[4,136,128]{2,1,0:T(8,128)S(1)}, f32[4,136,128]{2,1,0:T(8,128)S(1)}, u32[]{:S(2)}, u32[]{:S(2)}) %collective-permute-start) | collective-permute-done | bytes 278560 | tf_op jit(solution)/shard_map/ppermute | solution.py:481
  6.0 0.1 multiply_add_fusion.1
  6.1 0.0 copy-start.1
  6.1 0.0 copy-start.2
  6.1 0.0 copy-start.3
  6.1 0.0 copy-start
  6.1 3.0 %collective-permute-start.1 = (f32[1,136,128]{2,1,0:T(8,128)S(1)}, f32[1,136,128]{2,1,0:T(8,128)S(1)}, u32[]{:S(2)}, u32[]{:S(2)}) collective-permute-start(f32[1,136,128]{2,1,0:T(8,128)S(1)} %get-tuple-element.31), channel_id=1, source_target_pairs={{0,2},{1,3},{2,0},{3,1},{4,6},{5,7},{6,4},{7,5},{8,10},{9,11},{10,... | collective-permute-start | bytes 208904 | tf_op jit(solution)/shard_map/ppermute | solution.py:481
  9.1 2.6 %collective-permute-start.3 = (f32[1,136,128]{2,1,0:T(8,128)S(1)}, f32[1,136,128]{2,1,0:T(8,128)S(1)}, u32[]{:S(2)}, u32[]{:S(2)}) collective-permute-start(f32[1,136,128]{2,1,0:T(8,128)S(1)} %get-tuple-element.32), channel_id=1, source_target_pairs={{0,4},{1,5},{2,6},{3,7},{4,0},{5,1},{6,2},{7,3},{8,12},{9,13},{10,... | collective-permute-start | bytes 208904 | tf_op jit(solution)/shard_map/ppermute | solution.py:481
  11.7 0.0 collective-permute-start.2
  11.7 0.0 collective-permute-done.1
  11.7 5.2 %collective-permute-done.3 = f32[1,136,128]{2,1,0:T(8,128)S(1)} collective-permute-done((f32[1,136,128]{2,1,0:T(8,128)S(1)}, f32[1,136,128]{2,1,0:T(8,128)S(1)}, u32[]{:S(2)}, u32[]{:S(2)}) %collective-permute-start.3) | collective-permute-done | bytes 69664 | tf_op jit(solution)/shard_map/ppermute | solution.py:481
  16.9 1.0 %collective-permute-done.2 = f32[1,136,128]{2,1,0:T(8,128)S(1)} collective-permute-done((f32[1,136,128]{2,1,0:T(8,128)S(1)}, f32[1,136,128]{2,1,0:T(8,128)S(1)}, u32[]{:S(2)}, u32[]{:S(2)}) %collective-permute-start.2) | collective-permute-done | bytes 69664 | tf_op jit(solution)/shard_map/ppermute | solution.py:481
  18.0 1.6 %collective-permute-start.6 = (f32[1,136,128]{2,1,0:T(8,128)S(1)}, f32[1,136,128]{2,1,0:T(8,128)S(1)}, u32[]{:S(2)}, u32[]{:S(2)}) collective-permute-start(f32[1,136,128]{2,1,0:T(8,128)S(1)} %get-tuple-element.17), channel_id=1, source_target_pairs={{0,16},{1,17},{2,18},{3,19},{4,20},{5,21},{6,22},{7,23},{8,24},{9,... | collective-permute-start | bytes 208904 | tf_op jit(solution)/shard_map/ppermute | solution.py:481
  19.6 1.4 %collective-permute-start.5 = (f32[1,136,128]{2,1,0:T(8,128)S(1)}, f32[1,136,128]{2,1,0:T(8,128)S(1)}, u32[]{:S(2)}, u32[]{:S(2)}) collective-permute-start(f32[1,136,128]{2,1,0:T(8,128)S(1)} %get-tuple-element.17), channel_id=1, source_target_pairs={{0,24},{1,25},{2,26},{3,27},{4,28},{5,29},{6,30},{7,31},{8,16},{9,... | collective-permute-start | bytes 208904 | tf_op jit(solution)/shard_map/ppermute | solution.py:481
  21.0 0.5 %collective-permute-start.4 = (f32[1,136,128]{2,1,0:T(8,128)S(1)}, f32[1,136,128]{2,1,0:T(8,128)S(1)}, u32[]{:S(2)}, u32[]{:S(2)}) collective-permute-start(f32[1,136,128]{2,1,0:T(8,128)S(1)} %get-tuple-element.17), channel_id=1, source_target_pairs={{0,8},{1,9},{2,10},{3,11},{4,12},{5,13},{6,14},{7,15},{8,0},{9,1},... | collective-permute-start | bytes 208904 | tf_op jit(solution)/shard_map/ppermute | solution.py:481
  21.6 1.1 %collective-permute-done.6 = f32[1,136,128]{2,1,0:T(8,128)S(1)} collective-permute-done((f32[1,136,128]{2,1,0:T(8,128)S(1)}, f32[1,136,128]{2,1,0:T(8,128)S(1)}, u32[]{:S(2)}, u32[]{:S(2)}) %collective-permute-start.6) | collective-permute-done | bytes 69664 | tf_op jit(solution)/shard_map/ppermute | solution.py:481
  22.6 2.2 %collective-permute-done.5 = f32[1,136,128]{2,1,0:T(8,128)S(1)} collective-permute-done((f32[1,136,128]{2,1,0:T(8,128)S(1)}, f32[1,136,128]{2,1,0:T(8,128)S(1)}, u32[]{:S(2)}, u32[]{:S(2)}) %collective-permute-start.5) | collective-permute-done | bytes 69664 | tf_op jit(solution)/shard_map/ppermute | solution.py:481
  24.8 0.5 %collective-permute-done.4 = f32[1,136,128]{2,1,0:T(8,128)S(1)} collective-permute-done((f32[1,136,128]{2,1,0:T(8,128)S(1)}, f32[1,136,128]{2,1,0:T(8,128)S(1)}, u32[]{:S(2)}, u32[]{:S(2)}) %collective-permute-start.4) | collective-permute-done | bytes 69664 | tf_op jit(solution)/shard_map/ppermute | solution.py:481
  25.4 0.1 broadcast_select_fusion.10
  25.5 1.2 %collective-permute-start.7 = (f32[1,136,128]{2,1,0:T(8,128)S(1)}, f32[1,136,128]{2,1,0:T(8,128)S(1)}, u32[]{:S(2)}, u32[]{:S(2)}) collective-permute-start(f32[1,136,128]{2,1,0:T(8,128)S(1)} %get-tuple-element.26), channel_id=1, source_target_pairs={{0,2},{1,3},{2,0},{3,1},{4,6},{5,7},{6,4},{7,5},{8,10},{9,11},{10,... | collective-permute-start | bytes 208904 | tf_op jit(solution)/shard_map/ppermute | solution.py:481
  26.7 1.7 %collective-permute-start.8 = (f32[1,136,128]{2,1,0:T(8,128)S(1)}, f32[1,136,128]{2,1,0:T(8,128)S(1)}, u32[]{:S(2)}, u32[]{:S(2)}) collective-permute-start(f32[1,136,128]{2,1,0:T(8,128)S(1)} %get-tuple-element.27), channel_id=1, source_target_pairs={{0,4},{1,5},{2,6},{3,7},{4,0},{5,1},{6,2},{7,3},{8,12},{9,13},{10,... | collective-permute-start | bytes 208904 | tf_op jit(solution)/shard_map/ppermute | solution.py:481
  28.4 1.6 %collective-permute-start.9 = (f32[1,136,128]{2,1,0:T(8,128)S(1)}, f32[1,136,128]{2,1,0:T(8,128)S(1)}, u32[]{:S(2)}, u32[]{:S(2)}) collective-permute-start(f32[1,136,128]{2,1,0:T(8,128)S(1)} %get-tuple-element.28), channel_id=1, source_target_pairs={{0,6},{1,7},{2,4},{3,5},{4,2},{5,3},{6,0},{7,1},{8,14},{9,15},{10,... | collective-permute-start | bytes 208904 | tf_op jit(solution)/shard_map/ppermute | solution.py:481
  30.0 0.7 %collective-permute-done.7 = f32[1,136,128]{2,1,0:T(8,128)S(1)} collective-permute-done((f32[1,136,128]{2,1,0:T(8,128)S(1)}, f32[1,136,128]{2,1,0:T(8,128)S(1)}, u32[]{:S(2)}, u32[]{:S(2)}) %collective-permute-start.7) | collective-permute-done | bytes 69664 | tf_op jit(solution)/shard_map/ppermute | solution.py:481
  30.6 2.0 %collective-permute-done.8 = f32[1,136,128]{2,1,0:T(8,128)S(1)} collective-permute-done((f32[1,136,128]{2,1,0:T(8,128)S(1)}, f32[1,136,128]{2,1,0:T(8,128)S(1)}, u32[]{:S(2)}, u32[]{:S(2)}) %collective-permute-start.8) | collective-permute-done | bytes 69664 | tf_op jit(solution)/shard_map/ppermute | solution.py:481
  32.7 1.8 %collective-permute-done.9 = f32[1,136,128]{2,1,0:T(8,128)S(1)} collective-permute-done((f32[1,136,128]{2,1,0:T(8,128)S(1)}, f32[1,136,128]{2,1,0:T(8,128)S(1)}, u32[]{:S(2)}, u32[]{:S(2)}) %collective-permute-start.9) | collective-permute-done | bytes 69664 | tf_op jit(solution)/shard_map/ppermute | solution.py:481
  34.5 0.1 fusion
  34.6 0.1 collective-permute-start.10
  34.6 0.0 copy-done.1
  34.7 0.0 copy-done.2
  34.7 0.0 copy-done.3
  34.7 2.8 %stats.1 = (f32[4096,128]{1,0:T(8,128)S(1)}, f32[32,128]{1,0:T(8,128)S(1)}, s32[32,128]{1,0:T(8,128)S(1)}) custom-call(s32[32,128]{1,0:T(8,128)S(1)} %bitcast.19, s32[32,128]{1,0:T(8,128)S(1)} %bitcast.21, s32[32,128]{1,0:T(8,128)S(1)} %bitcast.23), custom_call_target="tpu_custom_call" | custom-call | tf_op jit(solution)/shard_map/stats/pallas_call | solution.py:397
  37.5 0.0 copy-done
  37.5 0.6 %parts.1.parts_ref = bf16[272,4096]{1,0:T(8,128)(2,1)S(1)} custom-call(f32[4096,128]{1,0:T(8,128)S(1)} %copy-done), custom_call_target="tpu_custom_call" | custom-call | tf_op jit(solution)/shard_map/parts/pallas_call | solution.py:385
  38.1 1.4 %local.7.refs_3_ = f32[136,512]{1,0:T(8,128)S(1)} custom-call(bf16[272,4096]{1,0:T(8,128)(2,1)S(1)} %parts.1.parts_ref, f32[4096,128]{1,0:T(8,128)S(1)} %get-tuple-element.13.column_ref, f32[32,128]{1,0:T(8,128)S(1)} %get-tuple-element.14.sid_ref), custom_call_target="tpu_custom_call" | custom-call | tf_op jit(solution)/shard_map/local/pallas_call | solution.py:414
  39.5 2.2 %local.6.refs_2_ = f32[136,1024]{1,0:T(8,128)S(1)} custom-call(bf16[272,4096]{1,0:T(8,128)(2,1)S(1)} %parts.1.parts_ref, f32[4096,128]{1,0:T(8,128)S(1)} %get-tuple-element.13.column_ref, f32[32,128]{1,0:T(8,128)S(1)} %get-tuple-element.14.sid_ref), custom_call_target="tpu_custom_call" | custom-call | tf_op jit(solution)/shard_map/local/pallas_call | solution.py:414
  41.7 1.8 %local.5.refs_1_ = f32[136,1024]{1,0:T(8,128)S(1)} custom-call(bf16[272,4096]{1,0:T(8,128)(2,1)S(1)} %parts.1.parts_ref, f32[4096,128]{1,0:T(8,128)S(1)} %get-tuple-element.13.column_ref, f32[32,128]{1,0:T(8,128)S(1)} %get-tuple-element.14.sid_ref), custom_call_target="tpu_custom_call" | custom-call | tf_op jit(solution)/shard_map/local/pallas_call | solution.py:414
  43.5 1.3 %local.4.refs_0_ = f32[136,1536]{1,0:T(8,128)S(1)} custom-call(bf16[272,4096]{1,0:T(8,128)(2,1)S(1)} %parts.1.parts_ref, f32[4096,128]{1,0:T(8,128)S(1)} %get-tuple-element.13.column_ref, f32[32,128]{1,0:T(8,128)S(1)} %get-tuple-element.14.sid_ref), custom_call_target="tpu_custom_call" | custom-call | tf_op jit(solution)/shard_map/local/pallas_call | solution.py:414
  44.8 1.4 %gather.1.sums_ref = f32[136,4096]{1,0:T(8,128)S(1)} custom-call(s32[1]{0:T(128)} %bitcast.flip_ref, s32[32,128]{1,0:T(8,128)S(1)} %get-tuple-element.10.key_ref, f32[4,136,128]{2,1,0:T(8,128)S(1)} %get-tuple-element.21.state_ref, f32[136,1536]{1,0:T(8,128)S(1)} %local.4.refs_0_, f32[136,1024]{1,0:T(8,128)S(1)} %local.5.refs_1_, ...), custom_call_target="tpu_custom_call" | custom-call | tf_op jit(solution)/shard_map/gather/pallas_call | solution.py:427
  46.2 0.0 collective-permute-done.10.state_ref
  46.2 2.5 %final.1 = f32[4096,128]{1,0:T(8,128)} custom-call(s32[1]{0:T(128)} %bitcast.flip_ref, s32[32,128]{1,0:T(8,128)S(1)} %get-tuple-element.10.key_ref, f32[4,136,128]{2,1,0:T(8,128)S(1)} %collective-permute-done.10.state_ref, f32[136,4096]{1,0:T(8,128)S(1)} %gather.1.sums_ref), custom_call_target="tpu_custom_call" | custom-call | tf_op jit(solution)/shard_map/final/pallas_call | solution.py:440
  (13 shorter events, 0.2 us)
Async XLA Ops:
  4.2 1.7 %collective-permute-start = (f32[4,136,128]{2,1,0:T(8,128)S(1)}, f32[4,136,128]{2,1,0:T(8,128)S(1)}, u32[]{:S(2)}, u32[]{:S(2)}) collective-permute-start(f32[4,136,128]{2,1,0:T(8,128)S(1)} %get-tuple-element.12), channel_id=1, source_target_pairs={{0,1},{1,0},{2,3},{3,2},{4,5},{5,4},{6,7},{7,6},{8,9},{9,8},{10,11... | collective-permute-start | bytes 835592 | tf_op jit(solution)/shard_map/ppermute | solution.py:481
  6.1 28.6 %copy-start.1 = (s32[4096,1]{0,1:T(1,128)S(1)}, s32[4096,1]{0,1:T(1,128)}, u32[]{:S(2)}) copy-start(s32[4096,1]{0,1:T(1,128)} %param.5) | copy-start | bytes 49156
  6.1 28.6 %copy-start.2 = (s32[4096]{0:T(1024)S(1)}, s32[4096]{0:T(1024)}, u32[]{:S(2)}) copy-start(s32[4096]{0:T(1024)} %param.6) | copy-start | bytes 49156
  6.1 28.6 %copy-start.3 = (s32[4096]{0:T(1024)S(1)}, s32[4096]{0:T(1024)}, u32[]{:S(2)}) copy-start(s32[4096]{0:T(1024)} %param.7) | copy-start | bytes 49156
  6.1 31.4 %copy-start = (f32[4096,128]{1,0:T(8,128)S(1)}, f32[4096,128]{1,0:T(8,128)}, u32[]{:S(2)}) copy-start(f32[4096,128]{1,0:T(8,128)} %x_ref.1) | copy-start | bytes 6291460
  6.1 5.6 %collective-permute-start.1 = (f32[1,136,128]{2,1,0:T(8,128)S(1)}, f32[1,136,128]{2,1,0:T(8,128)S(1)}, u32[]{:S(2)}, u32[]{:S(2)}) collective-permute-start(f32[1,136,128]{2,1,0:T(8,128)S(1)} %get-tuple-element.31), channel_id=1, source_target_pairs={{0,2},{1,3},{2,0},{3,1},{4,6},{5,7},{6,4},{7,5},{8,10},{9,11},{10,... | collective-permute-start | bytes 208904 | tf_op jit(solution)/shard_map/ppermute | solution.py:481
  9.1 7.8 %collective-permute-start.3 = (f32[1,136,128]{2,1,0:T(8,128)S(1)}, f32[1,136,128]{2,1,0:T(8,128)S(1)}, u32[]{:S(2)}, u32[]{:S(2)}) collective-permute-start(f32[1,136,128]{2,1,0:T(8,128)S(1)} %get-tuple-element.32), channel_id=1, source_target_pairs={{0,4},{1,5},{2,6},{3,7},{4,0},{5,1},{6,2},{7,3},{8,12},{9,13},{10,... | collective-permute-start | bytes 208904 | tf_op jit(solution)/shard_map/ppermute | solution.py:481
  11.7 6.2 %collective-permute-start.2 = (f32[1,136,128]{2,1,0:T(8,128)S(1)}, f32[1,136,128]{2,1,0:T(8,128)S(1)}, u32[]{:S(2)}, u32[]{:S(2)}) collective-permute-start(f32[1,136,128]{2,1,0:T(8,128)S(1)} %get-tuple-element.33), channel_id=1, source_target_pairs={{0,6},{1,7},{2,4},{3,5},{4,2},{5,3},{6,0},{7,1},{8,14},{9,15},{10,... | collective-permute-start | bytes 208904 | tf_op jit(solution)/shard_map/ppermute | solution.py:481
  18.0 4.6 %collective-permute-start.6 = (f32[1,136,128]{2,1,0:T(8,128)S(1)}, f32[1,136,128]{2,1,0:T(8,128)S(1)}, u32[]{:S(2)}, u32[]{:S(2)}) collective-permute-start(f32[1,136,128]{2,1,0:T(8,128)S(1)} %get-tuple-element.17), channel_id=1, source_target_pairs={{0,16},{1,17},{2,18},{3,19},{4,20},{5,21},{6,22},{7,23},{8,24},{9,... | collective-permute-start | bytes 208904 | tf_op jit(solution)/shard_map/ppermute | solution.py:481
  19.6 5.2 %collective-permute-start.5 = (f32[1,136,128]{2,1,0:T(8,128)S(1)}, f32[1,136,128]{2,1,0:T(8,128)S(1)}, u32[]{:S(2)}, u32[]{:S(2)}) collective-permute-start(f32[1,136,128]{2,1,0:T(8,128)S(1)} %get-tuple-element.17), channel_id=1, source_target_pairs={{0,24},{1,25},{2,26},{3,27},{4,28},{5,29},{6,30},{7,31},{8,16},{9,... | collective-permute-start | bytes 208904 | tf_op jit(solution)/shard_map/ppermute | solution.py:481
  21.0 4.3 %collective-permute-start.4 = (f32[1,136,128]{2,1,0:T(8,128)S(1)}, f32[1,136,128]{2,1,0:T(8,128)S(1)}, u32[]{:S(2)}, u32[]{:S(2)}) collective-permute-start(f32[1,136,128]{2,1,0:T(8,128)S(1)} %get-tuple-element.17), channel_id=1, source_target_pairs={{0,8},{1,9},{2,10},{3,11},{4,12},{5,13},{6,14},{7,15},{8,0},{9,1},... | collective-permute-start | bytes 208904 | tf_op jit(solution)/shard_map/ppermute | solution.py:481
  25.5 5.1 %collective-permute-start.7 = (f32[1,136,128]{2,1,0:T(8,128)S(1)}, f32[1,136,128]{2,1,0:T(8,128)S(1)}, u32[]{:S(2)}, u32[]{:S(2)}) collective-permute-start(f32[1,136,128]{2,1,0:T(8,128)S(1)} %get-tuple-element.26), channel_id=1, source_target_pairs={{0,2},{1,3},{2,0},{3,1},{4,6},{5,7},{6,4},{7,5},{8,10},{9,11},{10,... | collective-permute-start | bytes 208904 | tf_op jit(solution)/shard_map/ppermute | solution.py:481
  26.7 6.0 %collective-permute-start.8 = (f32[1,136,128]{2,1,0:T(8,128)S(1)}, f32[1,136,128]{2,1,0:T(8,128)S(1)}, u32[]{:S(2)}, u32[]{:S(2)}) collective-permute-start(f32[1,136,128]{2,1,0:T(8,128)S(1)} %get-tuple-element.27), channel_id=1, source_target_pairs={{0,4},{1,5},{2,6},{3,7},{4,0},{5,1},{6,2},{7,3},{8,12},{9,13},{10,... | collective-permute-start | bytes 208904 | tf_op jit(solution)/shard_map/ppermute | solution.py:481
  28.4 6.1 %collective-permute-start.9 = (f32[1,136,128]{2,1,0:T(8,128)S(1)}, f32[1,136,128]{2,1,0:T(8,128)S(1)}, u32[]{:S(2)}, u32[]{:S(2)}) collective-permute-start(f32[1,136,128]{2,1,0:T(8,128)S(1)} %get-tuple-element.28), channel_id=1, source_target_pairs={{0,6},{1,7},{2,4},{3,5},{4,2},{5,3},{6,0},{7,1},{8,14},{9,15},{10,... | collective-permute-start | bytes 208904 | tf_op jit(solution)/shard_map/ppermute | solution.py:481
  34.6 11.6 %collective-permute-start.10 = (f32[4,136,128]{2,1,0:T(8,128)S(1)}, f32[4,136,128]{2,1,0:T(8,128)S(1)}, u32[]{:S(2)}, u32[]{:S(2)}) collective-permute-start(f32[4,136,128]{2,1,0:T(8,128)S(1)} %get-tuple-element.22), channel_id=1, source_target_pairs={{0,1},{1,0},{2,3},{3,2},{4,5},{5,4},{6,7},{7,6},{8,9},{9,8},{10,11... | collective-permute-start | bytes 835592 | tf_op jit(solution)/shard_map/ppermute | solution.py:481

commit v5 on v4

--- a/solution.py
+++ b/solution.py
@@ -254,7 +254,7 @@
         out_ref[features:, span] = total[2 * features : 2 * features + EXTRA]
 
 
-def gather_states(flip, first, key, state_ref, table_ref, chunk, finish):
+def gather_states(flip, first, key, state_ref, table_ref, chunk, tail, finish):
     slots = state_ref.shape[0]
     events = key.shape[0] * LANES
     rows, features = table_ref.shape[0], state_ref.shape[1] - EXTRA
@@ -284,7 +284,11 @@
     account_f = (key & (ACCOUNTS - 1)).astype(F32)
     home = lax.shift_right_arithmetic(key, ACCOUNTS.bit_length() - 1)
 
-    for begin in range(0, events, chunk):
+    spans = [(begin, chunk) for begin in range(0, events, chunk)]
+    if tail < chunk:
+        begin = spans.pop()[0]
+        spans += [(first, tail) for first in range(begin, events, tail)]
+    for begin, chunk in spans:
 
         def part(step, total):
             lines = []
@@ -308,14 +312,14 @@
             total = lax.fori_loop(0, slots // group, part, jnp.zeros((rows, chunk), F32))
         more = total[2 * features : 2 * features + 3]
         count = more[0:1] * 65536.0 + more[1:2] * 256.0 + more[2:3]
-        finish(begin, total[0:features] + total[features : 2 * features], count)
+        finish(begin, chunk, total[0:features] + total[features : 2 * features], count)
 
 
 def gather_kernel(flip_ref, key_ref, state_ref, *refs, starts, chunk, first):
     local_refs, out_ref, table_ref = refs[: len(starts)], refs[-2], refs[-1]
     features = state_ref.shape[1] - EXTRA
 
-    def finish(begin, sums, count):
+    def finish(begin, chunk, sums, count):
         piece = max(i for i in range(len(starts)) if starts[i] <= begin)
         local_ref = local_refs[piece]
         span = slice(begin - starts[piece], begin - starts[piece] + chunk)
@@ -324,28 +328,28 @@
             local_ref[features : features + 1, span] + count
         )
 
-    gather_states(flip_ref[0], first, key_ref[...], state_ref, table_ref, chunk, finish)
+    gather_states(flip_ref[0], first, key_ref[...], state_ref, table_ref, chunk, chunk, finish)
 
 
 def final_kernel(
-    flip_ref, key_ref, state_ref, sums_ref, out_ref, table_ref, stage_ref, sems, *, chunk, first
+    flip_ref, key_ref, state_ref, sums_ref, out_ref, table_ref, stage_ref, sems, *, chunk, tail, first
 ):
     features = state_ref.shape[1] - EXTRA
     copies = []
 
-    def finish(begin, sums, count):
+    def finish(begin, chunk, sums, count):
         span = slice(begin, begin + chunk)
         sums = sums_ref[0:features, span] + sums
         count = sums_ref[features : features + 1, span] + count
         stage_ref[span, :] = (sums * (1.0 / count)).T
         rows = pl.ds(begin, chunk)
         copy = pltpu.make_async_copy(
-            stage_ref.at[rows, :], out_ref.at[rows, :], sems.at[begin // chunk]
+            stage_ref.at[rows, :], out_ref.at[rows, :], sems.at[len(copies)]
         )
         copy.start()
         copies.append(copy)
 
-    gather_states(flip_ref[0], first, key_ref[...], state_ref, table_ref, chunk, finish)
+    gather_states(flip_ref[0], first, key_ref[...], state_ref, table_ref, chunk, tail, finish)
     for copy in copies:
         copy.wait()
 
@@ -438,14 +442,14 @@
 def final_means(flip, key, state, sums, events, width, first):
     chunk = min(512, events)
     return pl.pallas_call(
-        functools.partial(final_kernel, chunk=chunk, first=first),
+        functools.partial(final_kernel, chunk=chunk, tail=min(256, chunk), first=first),
         out_shape=jax.ShapeDtypeStruct((events, width), F32),
         in_specs=[SMEM, VMEM, VMEM, VMEM],
         out_specs=HBM,
         scratch_shapes=[
             pltpu.VMEM((2 * width + 16, state.shape[0] * ACCOUNTS), BF16),
             pltpu.VMEM((events, width), F32),
-            pltpu.SemaphoreType.DMA((events // chunk,)),
+            pltpu.SemaphoreType.DMA((events // chunk + 1,)),
         ],
         compiler_params=PARAMS,
         name="final",
@@ -496,10 +500,11 @@
             got.append(swap(piece, other << done))
         bits = [bit(done + i) for i in range(level)]
         ordered = pick(got, bits)
-        saved.append((done, bits, ordered))
-        state = ordered[0]
+        inside = [jnp.zeros_like(ordered[0]), ordered[0]]
         for later in ordered[1:]:
-            state = combine(state, later, mark)
+            inside.append(combine(inside[-1], later, mark))
+        state = inside.pop()
+        saved.append((done, pick(inside, bits)))
         done += level
     before = jnp.zeros_like(state)
     while done < steps:
@@ -516,14 +521,11 @@
         done += level
         if done < steps:
             state = combine(earlier[-1], ordered[-1], mark)
-    for done, bits, ordered in reversed(saved):
-        prefixes = [before]
-        for earlier in ordered[:-1]:
-            prefixes.append(combine(prefixes[-1], earlier, mark))
-        mine = pick(prefixes, bits)
-        got = [mine[0]]
-        for other in range(1, len(mine)):
-            got.append(swap(mine[other], other << done))
+    for done, inside in reversed(saved):
+        got = [combine(before, inside[0], mark)]
+        for other in range(1, len(inside)):
+            ahead = combine(before, inside[other], mark)
+            got.append(swap(ahead, other << done))
         if done == 0:
             return got
         before = jnp.concatenate(got, axis=0)

time: 49 us -> 49 us (level)
  no operation moved by 1% of the time
where the time goes in v5:
time: 49 us; the launch traced here: 48.8 us
  Pallas kernels  18 us (37%)
  waiting for transfers between devices  15.7 us (32%)
  starting transfers between devices  14.2 us (29%)
    ppermute x11, waiting for transfers between devices, swap(): return lax.ppermute(value, AXES, [(i, i ^ mask) for i in range(devices)])  15.7 us
    ppermute x11, starting transfers between devices, swap(): return lax.ppermute(value, AXES, [(i, i ^ mask) for i in range(devices)])  14.2 us
    pallas_call x4, Pallas kernels, local_sums(): pl.pallas_call(functools.partial(local_kernel, first=first, chunk=chunk),...  6.64 us
    pallas_call x1, Pallas kernels, closing_states(): pl.pallas_call(closing_kernel, out_shape=(shape, shape), in_specs=[SMEM,...  4.19 us
    pallas_call x1, Pallas kernels, event_stats(): pl.pallas_call(functools.partial(stats_kernel, owners=owners), out_shape=...  2.81 us
    pallas_call x1, Pallas kernels, final_means(): pl.pallas_call(functools.partial(final_kernel, chunk=chunk, tail=min(256,...  2.42 us
    pallas_call x1, Pallas kernels, first_gather(): pl.pallas_call(functools.partial(gather_kernel, starts=starts, chunk=chun...  1.37 us
  transfers between devices with their start and end apart: 11, of which 9 were waited for; matrix products, arithmetic and copies ran while one was open for 0% of the time, Pallas kernels for 23%

profile of v5, /device:TPU:0, one launch (start us, length us, event | category | flops | bytes accessed | tf_op | source)
XLA Modules:
  0.0 48.8 jit_solution(15566537928443579984)
XLA Ops:
  0.0 4.2 %closing.1 = (f32[4,136,128]{2,1,0:T(8,128)S(1)}, f32[4,136,128]{2,1,0:T(8,128)S(1)}) custom-call(s32[1]{0:T(128)} %bitcast.flip_ref, s32[32,128]{1,0:T(8,128)} %bitcast.25, s32[32,128]{1,0:T(8,128)} %bitcast.27, s32[32,128]{1,0:T(8,128)} %bitcast.29, f32[4096,128]{1,0:T(8,128)} %x_ref.1), custom_call_target="tpu_custom_call" | custom-call | tf_op jit(solution)/shard_map/closing/pallas_call | solution.py:370
  4.2 0.6 %collective-permute-start = (f32[4,136,128]{2,1,0:T(8,128)S(1)}, f32[4,136,128]{2,1,0:T(8,128)S(1)}, u32[]{:S(2)}, u32[]{:S(2)}) collective-permute-start(f32[4,136,128]{2,1,0:T(8,128)S(1)} %get-tuple-element.11), channel_id=1, source_target_pairs={{0,1},{1,0},{2,3},{3,2},{4,5},{5,4},{6,7},{7,6},{8,9},{9,8},{10,11... | collective-permute-start | bytes 835592 | tf_op jit(solution)/shard_map/ppermute | solution.py:485
  4.8 1.2 %collective-permute-done = f32[4,136,128]{2,1,0:T(8,128)S(1)} collective-permute-done((f32[4,136,128]{2,1,0:T(8,128)S(1)}, f32[4,136,128]{2,1,0:T(8,128)S(1)}, u32[]{:S(2)}, u32[]{:S(2)}) %collective-permute-start) | collective-permute-done | bytes 278560 | tf_op jit(solution)/shard_map/ppermute | solution.py:485
  5.9 0.1 broadcast_select_fusion
  6.0 0.1 multiply_add_fusion.2
  6.1 3.0 %collective-permute-start.1 = (f32[1,136,128]{2,1,0:T(8,128)S(1)}, f32[1,136,128]{2,1,0:T(8,128)S(1)}, u32[]{:S(2)}, u32[]{:S(2)}) collective-permute-start(f32[1,136,128]{2,1,0:T(8,128)S(1)} %get-tuple-element.29), channel_id=1, source_target_pairs={{0,2},{1,3},{2,0},{3,1},{4,6},{5,7},{6,4},{7,5},{8,10},{9,11},{10,... | collective-permute-start | bytes 208904 | tf_op jit(solution)/shard_map/ppermute | solution.py:485
  9.1 2.6 %collective-permute-start.3 = (f32[1,136,128]{2,1,0:T(8,128)S(1)}, f32[1,136,128]{2,1,0:T(8,128)S(1)}, u32[]{:S(2)}, u32[]{:S(2)}) collective-permute-start(f32[1,136,128]{2,1,0:T(8,128)S(1)} %get-tuple-element.30), channel_id=1, source_target_pairs={{0,4},{1,5},{2,6},{3,7},{4,0},{5,1},{6,2},{7,3},{8,12},{9,13},{10,... | collective-permute-start | bytes 208904 | tf_op jit(solution)/shard_map/ppermute | solution.py:485
  11.7 0.0 collective-permute-start.2
  11.7 0.0 collective-permute-done.1
  11.7 5.2 %collective-permute-done.3 = f32[1,136,128]{2,1,0:T(8,128)S(1)} collective-permute-done((f32[1,136,128]{2,1,0:T(8,128)S(1)}, f32[1,136,128]{2,1,0:T(8,128)S(1)}, u32[]{:S(2)}, u32[]{:S(2)}) %collective-permute-start.3) | collective-permute-done | bytes 69664 | tf_op jit(solution)/shard_map/ppermute | solution.py:485
  16.9 1.0 %collective-permute-done.2 = f32[1,136,128]{2,1,0:T(8,128)S(1)} collective-permute-done((f32[1,136,128]{2,1,0:T(8,128)S(1)}, f32[1,136,128]{2,1,0:T(8,128)S(1)}, u32[]{:S(2)}, u32[]{:S(2)}) %collective-permute-start.2) | collective-permute-done | bytes 69664 | tf_op jit(solution)/shard_map/ppermute | solution.py:485
  17.9 0.0 copy-start.1
  18.0 0.0 copy-start.2
  18.0 0.0 copy-start.3
  18.0 0.0 copy-start
  18.1 1.6 %collective-permute-start.6 = (f32[1,136,128]{2,1,0:T(8,128)S(1)}, f32[1,136,128]{2,1,0:T(8,128)S(1)}, u32[]{:S(2)}, u32[]{:S(2)}) collective-permute-start(f32[1,136,128]{2,1,0:T(8,128)S(1)} %get-tuple-element.35), channel_id=1, source_target_pairs={{0,16},{1,17},{2,18},{3,19},{4,20},{5,21},{6,22},{7,23},{8,24},{9,... | collective-permute-start | bytes 208904 | tf_op jit(solution)/shard_map/ppermute | solution.py:485
  19.7 1.4 %collective-permute-start.5 = (f32[1,136,128]{2,1,0:T(8,128)S(1)}, f32[1,136,128]{2,1,0:T(8,128)S(1)}, u32[]{:S(2)}, u32[]{:S(2)}) collective-permute-start(f32[1,136,128]{2,1,0:T(8,128)S(1)} %get-tuple-element.35), channel_id=1, source_target_pairs={{0,24},{1,25},{2,26},{3,27},{4,28},{5,29},{6,30},{7,31},{8,16},{9,... | collective-permute-start | bytes 208904 | tf_op jit(solution)/shard_map/ppermute | solution.py:485
  21.1 0.5 %collective-permute-start.4 = (f32[1,136,128]{2,1,0:T(8,128)S(1)}, f32[1,136,128]{2,1,0:T(8,128)S(1)}, u32[]{:S(2)}, u32[]{:S(2)}) collective-permute-start(f32[1,136,128]{2,1,0:T(8,128)S(1)} %get-tuple-element.35), channel_id=1, source_target_pairs={{0,8},{1,9},{2,10},{3,11},{4,12},{5,13},{6,14},{7,15},{8,0},{9,1},... | collective-permute-start | bytes 208904 | tf_op jit(solution)/shard_map/ppermute | solution.py:485
  21.7 1.0 %collective-permute-done.6 = f32[1,136,128]{2,1,0:T(8,128)S(1)} collective-permute-done((f32[1,136,128]{2,1,0:T(8,128)S(1)}, f32[1,136,128]{2,1,0:T(8,128)S(1)}, u32[]{:S(2)}, u32[]{:S(2)}) %collective-permute-start.6) | collective-permute-done | bytes 69664 | tf_op jit(solution)/shard_map/ppermute | solution.py:485
  22.7 2.2 %collective-permute-done.5 = f32[1,136,128]{2,1,0:T(8,128)S(1)} collective-permute-done((f32[1,136,128]{2,1,0:T(8,128)S(1)}, f32[1,136,128]{2,1,0:T(8,128)S(1)}, u32[]{:S(2)}, u32[]{:S(2)}) %collective-permute-start.5) | collective-permute-done | bytes 69664 | tf_op jit(solution)/shard_map/ppermute | solution.py:485
  24.9 0.5 %collective-permute-done.4 = f32[1,136,128]{2,1,0:T(8,128)S(1)} collective-permute-done((f32[1,136,128]{2,1,0:T(8,128)S(1)}, f32[1,136,128]{2,1,0:T(8,128)S(1)}, u32[]{:S(2)}, u32[]{:S(2)}) %collective-permute-start.4) | collective-permute-done | bytes 69664 | tf_op jit(solution)/shard_map/ppermute | solution.py:485
  25.6 1.2 %collective-permute-start.7 = (f32[1,136,128]{2,1,0:T(8,128)S(1)}, f32[1,136,128]{2,1,0:T(8,128)S(1)}, u32[]{:S(2)}, u32[]{:S(2)}) collective-permute-start(f32[1,136,128]{2,1,0:T(8,128)S(1)} %get-tuple-element.36), channel_id=1, source_target_pairs={{0,2},{1,3},{2,0},{3,1},{4,6},{5,7},{6,4},{7,5},{8,10},{9,11},{10,... | collective-permute-start | bytes 208904 | tf_op jit(solution)/shard_map/ppermute | solution.py:485
  26.8 1.7 %collective-permute-start.8 = (f32[1,136,128]{2,1,0:T(8,128)S(1)}, f32[1,136,128]{2,1,0:T(8,128)S(1)}, u32[]{:S(2)}, u32[]{:S(2)}) collective-permute-start(f32[1,136,128]{2,1,0:T(8,128)S(1)} %get-tuple-element.37), channel_id=1, source_target_pairs={{0,4},{1,5},{2,6},{3,7},{4,0},{5,1},{6,2},{7,3},{8,12},{9,13},{10,... | collective-permute-start | bytes 208904 | tf_op jit(solution)/shard_map/ppermute | solution.py:485
  28.5 1.6 %collective-permute-start.9 = (f32[1,136,128]{2,1,0:T(8,128)S(1)}, f32[1,136,128]{2,1,0:T(8,128)S(1)}, u32[]{:S(2)}, u32[]{:S(2)}) collective-permute-start(f32[1,136,128]{2,1,0:T(8,128)S(1)} %get-tuple-element.38), channel_id=1, source_target_pairs={{0,6},{1,7},{2,4},{3,5},{4,2},{5,3},{6,0},{7,1},{8,14},{9,15},{10,... | collective-permute-start | bytes 208904 | tf_op jit(solution)/shard_map/ppermute | solution.py:485
  30.0 0.7 %collective-permute-done.7 = f32[1,136,128]{2,1,0:T(8,128)S(1)} collective-permute-done((f32[1,136,128]{2,1,0:T(8,128)S(1)}, f32[1,136,128]{2,1,0:T(8,128)S(1)}, u32[]{:S(2)}, u32[]{:S(2)}) %collective-permute-start.7) | collective-permute-done | bytes 69664 | tf_op jit(solution)/shard_map/ppermute | solution.py:485
  30.7 2.0 %collective-permute-done.8 = f32[1,136,128]{2,1,0:T(8,128)S(1)} collective-permute-done((f32[1,136,128]{2,1,0:T(8,128)S(1)}, f32[1,136,128]{2,1,0:T(8,128)S(1)}, u32[]{:S(2)}, u32[]{:S(2)}) %collective-permute-start.8) | collective-permute-done | bytes 69664 | tf_op jit(solution)/shard_map/ppermute | solution.py:485
  32.7 1.8 %collective-permute-done.9 = f32[1,136,128]{2,1,0:T(8,128)S(1)} collective-permute-done((f32[1,136,128]{2,1,0:T(8,128)S(1)}, f32[1,136,128]{2,1,0:T(8,128)S(1)}, u32[]{:S(2)}, u32[]{:S(2)}) %collective-permute-start.9) | collective-permute-done | bytes 69664 | tf_op jit(solution)/shard_map/ppermute | solution.py:485
  34.6 0.1 multiply_add_fusion
  34.6 0.1 collective-permute-start.10
  34.7 0.0 copy-done.1
  34.7 0.0 copy-done.2
  34.7 0.0 copy-done.3
  34.7 2.8 %stats.1 = (f32[4096,128]{1,0:T(8,128)S(1)}, f32[32,128]{1,0:T(8,128)S(1)}, s32[32,128]{1,0:T(8,128)S(1)}) custom-call(s32[32,128]{1,0:T(8,128)S(1)} %bitcast.26, s32[32,128]{1,0:T(8,128)S(1)} %bitcast.28, s32[32,128]{1,0:T(8,128)S(1)} %bitcast.30), custom_call_target="tpu_custom_call" | custom-call | tf_op jit(solution)/shard_map/stats/pallas_call | solution.py:401
  37.6 0.0 copy-done
  37.6 0.6 %parts.1.parts_ref = bf16[272,4096]{1,0:T(8,128)(2,1)S(1)} custom-call(f32[4096,128]{1,0:T(8,128)S(1)} %copy-done), custom_call_target="tpu_custom_call" | custom-call | tf_op jit(solution)/shard_map/parts/pallas_call | solution.py:389
  38.2 1.4 %local.7.refs_3_ = f32[136,512]{1,0:T(8,128)S(1)} custom-call(bf16[272,4096]{1,0:T(8,128)(2,1)S(1)} %parts.1.parts_ref, f32[4096,128]{1,0:T(8,128)S(1)} %get-tuple-element.13.column_ref, f32[32,128]{1,0:T(8,128)S(1)} %get-tuple-element.14.sid_ref), custom_call_target="tpu_custom_call" | custom-call | tf_op jit(solution)/shard_map/local/pallas_call | solution.py:418
  39.6 2.2 %local.6.refs_2_ = f32[136,1024]{1,0:T(8,128)S(1)} custom-call(bf16[272,4096]{1,0:T(8,128)(2,1)S(1)} %parts.1.parts_ref, f32[4096,128]{1,0:T(8,128)S(1)} %get-tuple-element.13.column_ref, f32[32,128]{1,0:T(8,128)S(1)} %get-tuple-element.14.sid_ref), custom_call_target="tpu_custom_call" | custom-call | tf_op jit(solution)/shard_map/local/pallas_call | solution.py:418
  41.8 1.8 %local.5.refs_1_ = f32[136,1024]{1,0:T(8,128)S(1)} custom-call(bf16[272,4096]{1,0:T(8,128)(2,1)S(1)} %parts.1.parts_ref, f32[4096,128]{1,0:T(8,128)S(1)} %get-tuple-element.13.column_ref, f32[32,128]{1,0:T(8,128)S(1)} %get-tuple-element.14.sid_ref), custom_call_target="tpu_custom_call" | custom-call | tf_op jit(solution)/shard_map/local/pallas_call | solution.py:418
  43.6 1.3 %local.4.refs_0_ = f32[136,1536]{1,0:T(8,128)S(1)} custom-call(bf16[272,4096]{1,0:T(8,128)(2,1)S(1)} %parts.1.parts_ref, f32[4096,128]{1,0:T(8,128)S(1)} %get-tuple-element.13.column_ref, f32[32,128]{1,0:T(8,128)S(1)} %get-tuple-element.14.sid_ref), custom_call_target="tpu_custom_call" | custom-call | tf_op jit(solution)/shard_map/local/pallas_call | solution.py:418
  44.8 1.4 %gather.1.sums_ref = f32[136,4096]{1,0:T(8,128)S(1)} custom-call(s32[1]{0:T(128)} %bitcast.flip_ref, s32[32,128]{1,0:T(8,128)S(1)} %get-tuple-element.10.key_ref, f32[4,136,128]{2,1,0:T(8,128)S(1)} %get-tuple-element.25.state_ref, f32[136,1536]{1,0:T(8,128)S(1)} %local.4.refs_0_, f32[136,1024]{1,0:T(8,128)S(1)} %local.5.refs_1_, ...), custom_call_target="tpu_custom_call" | custom-call | tf_op jit(solution)/shard_map/gather/pallas_call | solution.py:431
  46.2 0.0 collective-permute-done.10.state_ref
  46.2 2.4 %final.1 = f32[4096,128]{1,0:T(8,128)} custom-call(s32[1]{0:T(128)} %bitcast.flip_ref, s32[32,128]{1,0:T(8,128)S(1)} %get-tuple-element.10.key_ref, f32[4,136,128]{2,1,0:T(8,128)S(1)} %collective-permute-done.10.state_ref, f32[136,4096]{1,0:T(8,128)S(1)} %gather.1.sums_ref), custom_call_target="tpu_custom_call" | custom-call | tf_op jit(solution)/shard_map/final/pallas_call | solution.py:444
  (17 shorter events, 0.3 us)
Async XLA Ops:
  4.2 1.7 %collective-permute-start = (f32[4,136,128]{2,1,0:T(8,128)S(1)}, f32[4,136,128]{2,1,0:T(8,128)S(1)}, u32[]{:S(2)}, u32[]{:S(2)}) collective-permute-start(f32[4,136,128]{2,1,0:T(8,128)S(1)} %get-tuple-element.11), channel_id=1, source_target_pairs={{0,1},{1,0},{2,3},{3,2},{4,5},{5,4},{6,7},{7,6},{8,9},{9,8},{10,11... | collective-permute-start | bytes 835592 | tf_op jit(solution)/shard_map/ppermute | solution.py:485
  6.1 5.6 %collective-permute-start.1 = (f32[1,136,128]{2,1,0:T(8,128)S(1)}, f32[1,136,128]{2,1,0:T(8,128)S(1)}, u32[]{:S(2)}, u32[]{:S(2)}) collective-permute-start(f32[1,136,128]{2,1,0:T(8,128)S(1)} %get-tuple-element.29), channel_id=1, source_target_pairs={{0,2},{1,3},{2,0},{3,1},{4,6},{5,7},{6,4},{7,5},{8,10},{9,11},{10,... | collective-permute-start | bytes 208904 | tf_op jit(solution)/shard_map/ppermute | solution.py:485
  9.1 7.8 %collective-permute-start.3 = (f32[1,136,128]{2,1,0:T(8,128)S(1)}, f32[1,136,128]{2,1,0:T(8,128)S(1)}, u32[]{:S(2)}, u32[]{:S(2)}) collective-permute-start(f32[1,136,128]{2,1,0:T(8,128)S(1)} %get-tuple-element.30), channel_id=1, source_target_pairs={{0,4},{1,5},{2,6},{3,7},{4,0},{5,1},{6,2},{7,3},{8,12},{9,13},{10,... | collective-permute-start | bytes 208904 | tf_op jit(solution)/shard_map/ppermute | solution.py:485
  11.7 6.2 %collective-permute-start.2 = (f32[1,136,128]{2,1,0:T(8,128)S(1)}, f32[1,136,128]{2,1,0:T(8,128)S(1)}, u32[]{:S(2)}, u32[]{:S(2)}) collective-permute-start(f32[1,136,128]{2,1,0:T(8,128)S(1)} %get-tuple-element.31), channel_id=1, source_target_pairs={{0,6},{1,7},{2,4},{3,5},{4,2},{5,3},{6,0},{7,1},{8,14},{9,15},{10,... | collective-permute-start | bytes 208904 | tf_op jit(solution)/shard_map/ppermute | solution.py:485
  17.9 16.8 %copy-start.1 = (s32[4096,1]{0,1:T(1,128)S(1)}, s32[4096,1]{0,1:T(1,128)}, u32[]{:S(2)}) copy-start(s32[4096,1]{0,1:T(1,128)} %param.5) | copy-start | bytes 49156
  18.0 16.8 %copy-start.2 = (s32[4096]{0:T(1024)S(1)}, s32[4096]{0:T(1024)}, u32[]{:S(2)}) copy-start(s32[4096]{0:T(1024)} %param.6) | copy-start | bytes 49156
  18.0 16.8 %copy-start.3 = (s32[4096]{0:T(1024)S(1)}, s32[4096]{0:T(1024)}, u32[]{:S(2)}) copy-start(s32[4096]{0:T(1024)} %param.7) | copy-start | bytes 49156
  18.0 19.6 %copy-start = (f32[4096,128]{1,0:T(8,128)S(1)}, f32[4096,128]{1,0:T(8,128)}, u32[]{:S(2)}) copy-start(f32[4096,128]{1,0:T(8,128)} %x_ref.1) | copy-start | bytes 6291460
  18.1 4.6 %collective-permute-start.6 = (f32[1,136,128]{2,1,0:T(8,128)S(1)}, f32[1,136,128]{2,1,0:T(8,128)S(1)}, u32[]{:S(2)}, u32[]{:S(2)}) collective-permute-start(f32[1,136,128]{2,1,0:T(8,128)S(1)} %get-tuple-element.35), channel_id=1, source_target_pairs={{0,16},{1,17},{2,18},{3,19},{4,20},{5,21},{6,22},{7,23},{8,24},{9,... | collective-permute-start | bytes 208904 | tf_op jit(solution)/shard_map/ppermute | solution.py:485
  19.7 5.2 %collective-permute-start.5 = (f32[1,136,128]{2,1,0:T(8,128)S(1)}, f32[1,136,128]{2,1,0:T(8,128)S(1)}, u32[]{:S(2)}, u32[]{:S(2)}) collective-permute-start(f32[1,136,128]{2,1,0:T(8,128)S(1)} %get-tuple-element.35), channel_id=1, source_target_pairs={{0,24},{1,25},{2,26},{3,27},{4,28},{5,29},{6,30},{7,31},{8,16},{9,... | collective-permute-start | bytes 208904 | tf_op jit(solution)/shard_map/ppermute | solution.py:485
  21.1 4.3 %collective-permute-start.4 = (f32[1,136,128]{2,1,0:T(8,128)S(1)}, f32[1,136,128]{2,1,0:T(8,128)S(1)}, u32[]{:S(2)}, u32[]{:S(2)}) collective-permute-start(f32[1,136,128]{2,1,0:T(8,128)S(1)} %get-tuple-element.35), channel_id=1, source_target_pairs={{0,8},{1,9},{2,10},{3,11},{4,12},{5,13},{6,14},{7,15},{8,0},{9,1},... | collective-permute-start | bytes 208904 | tf_op jit(solution)/shard_map/ppermute | solution.py:485
  25.6 5.1 %collective-permute-start.7 = (f32[1,136,128]{2,1,0:T(8,128)S(1)}, f32[1,136,128]{2,1,0:T(8,128)S(1)}, u32[]{:S(2)}, u32[]{:S(2)}) collective-permute-start(f32[1,136,128]{2,1,0:T(8,128)S(1)} %get-tuple-element.36), channel_id=1, source_target_pairs={{0,2},{1,3},{2,0},{3,1},{4,6},{5,7},{6,4},{7,5},{8,10},{9,11},{10,... | collective-permute-start | bytes 208904 | tf_op jit(solution)/shard_map/ppermute | solution.py:485
  26.8 6.0 %collective-permute-start.8 = (f32[1,136,128]{2,1,0:T(8,128)S(1)}, f32[1,136,128]{2,1,0:T(8,128)S(1)}, u32[]{:S(2)}, u32[]{:S(2)}) collective-permute-start(f32[1,136,128]{2,1,0:T(8,128)S(1)} %get-tuple-element.37), channel_id=1, source_target_pairs={{0,4},{1,5},{2,6},{3,7},{4,0},{5,1},{6,2},{7,3},{8,12},{9,13},{10,... | collective-permute-start | bytes 208904 | tf_op jit(solution)/shard_map/ppermute | solution.py:485
  28.5 6.1 %collective-permute-start.9 = (f32[1,136,128]{2,1,0:T(8,128)S(1)}, f32[1,136,128]{2,1,0:T(8,128)S(1)}, u32[]{:S(2)}, u32[]{:S(2)}) collective-permute-start(f32[1,136,128]{2,1,0:T(8,128)S(1)} %get-tuple-element.38), channel_id=1, source_target_pairs={{0,6},{1,7},{2,4},{3,5},{4,2},{5,3},{6,0},{7,1},{8,14},{9,15},{10,... | collective-permute-start | bytes 208904 | tf_op jit(solution)/shard_map/ppermute | solution.py:485
  34.6 11.6 %collective-permute-start.10 = (f32[4,136,128]{2,1,0:T(8,128)S(1)}, f32[4,136,128]{2,1,0:T(8,128)S(1)}, u32[]{:S(2)}, u32[]{:S(2)}) collective-permute-start(f32[4,136,128]{2,1,0:T(8,128)S(1)} %get-tuple-element.26), channel_id=1, source_target_pairs={{0,1},{1,0},{2,3},{3,2},{4,5},{5,4},{6,7},{7,6},{8,9},{9,8},{10,11... | collective-permute-start | bytes 835592 | tf_op jit(solution)/shard_map/ppermute | solution.py:485
